TPU v7x, 32 devices: a whole 2x2x4 slice. The times are simulated.
32 devices in a mesh: ty: 2 (over core), tx: 4 (over z), pos: 4 (over y, x).
Axes of the slice: x: 2, y: 2, z: 4, core: 2. Of those that a mesh axis runs over, the one named last changes fastest.
Arguments:
- object_field: float32 [2, 2, 512, 1024], P(None, None, ('ty', 'pos'), 'tx'), may hold values from -6 to 6
- momentum: float32 [2, 2, 512, 1024], P(None, None, ('ty', 'pos'), 'tx'), may hold values from -12 to 12
- measured: float32 [2, 4, 4, 256, 256], P('ty', 'tx', 'pos'), may hold values from 0 to 2
- illumination: float32 [2, 256, 256], replicated, may hold values from -6 to 6
- slab_phase: float32 [256, 256], replicated, may hold values from -3.140625 to 3.140625
- offsets: int32 [2, 4, 4, 2], P('ty', 'tx'), may hold values from 0 to 128, as said below
- entry_counts: int32 [2, 4], P('ty', 'tx'), may hold values from 1 to 2, as said below
Outputs:
- new_object: float32 [2, 2, 512, 1024], P(None, None, ('ty', 'pos'), 'tx')
- new_momentum: float32 [2, 2, 512, 1024], P(None, None, ('ty', 'pos'), 'tx')
- amplitudes: float32 [2, 4, 4, 256, 256], P('ty', 'tx', 'pos')
Inputs may be any that keep to these rules, and one draw needn't show every extreme that they name: offsets[a, b, k] is the corner of a window of 256 x 256 cells, counted from the corner of tile (a, b) widened by 64 cells on every side. Tile (a, b) uses the first entry_counts[a, b] slots of its list; some tile uses exactly 2 slots in every draw.
All inputs are finite; a program needn't handle non-finite values.
Results may differ from a plain program's by a relative error of at most 0.0003.
Values sent between devices are 32-bit elements; how exact they have to be, the bound alone decides.
No kernel may reach another device: no remote copies, remote signals or barrier semaphores. Data moves between devices by JAX's collectives and lax.ppermute only.
A program may use at most 64 MiB of HBM per device.

v0:
```python
import math

import jax
import jax.numpy as jnp
from jax import lax
from jax.sharding import PartitionSpec as P

HIGHEST = lax.Precision.HIGHEST
magnitude_floor = 0.5
momentum_rate = 0.9
step_length = 0.05


def padded(value, sides, width):
    for axis, dim in sides:
        devices, length = (lax.axis_size(axis), value.shape[dim])
        up = [(i, (i + 1) % devices) for i in range(devices - 1)]
        down = [(j, i) for i, j in up]
        last = lax.slice_in_dim(value, length - width, length, axis=dim)
        leading = lax.slice_in_dim(value, 0, width, axis=dim)
        before = lax.ppermute(last, axis, up)
        after = lax.ppermute(leading, axis, down)
        value = jnp.concatenate([before, value, after], axis=dim)
    return value


def tables(length):
    indices = jnp.arange(length, dtype=jnp.int32)
    product = indices[:, None] * indices[None, :] % length
    angles = product.astype(jnp.float32) * (2.0 * math.pi / length)
    factor = 1.0 / math.sqrt(length)
    return (jnp.cos(angles) * factor, jnp.sin(angles) * factor)


def matmul(left, right):
    return jnp.dot(left, right, precision=HIGHEST)


def transform(real_part, imag_part, cosine, sine_table, inverse):
    factor = 1.0 if inverse else -1.0
    right_real = matmul(real_part, cosine) - factor * matmul(imag_part, sine_table)
    right_imag = matmul(imag_part, cosine) + factor * matmul(real_part, sine_table)
    left_real = matmul(cosine, right_real) - factor * matmul(sine_table, right_imag)
    left_imag = matmul(cosine, right_imag) + factor * matmul(sine_table, right_real)
    return (left_real, left_imag)


def complex_product(first_real, first_imag, second_real, second_imag):
    return (
        first_real * second_real - first_imag * second_imag,
        first_real * second_imag + first_imag * second_real,
    )


def forward_window(window, illumination, slab_real, slab_imag, cosine, sine_table):
    entering = complex_product(illumination[0], illumination[1], window[0], window[1])
    spectrum = transform(entering[0], entering[1], cosine, sine_table, False)
    spectrum = complex_product(spectrum[0], spectrum[1], slab_real, slab_imag)
    between = transform(spectrum[0], spectrum[1], cosine, sine_table, True)
    leaving = complex_product(between[0], between[1], window[2], window[3])
    farfield = transform(leaving[0], leaving[1], cosine, sine_table, False)
    return (between, farfield)


def window_gradient(
    window, measured_window, illumination, slab_real, slab_imag, cosine, sine_table
):
    between, farfield = forward_window(
        window, illumination, slab_real, slab_imag, cosine, sine_table
    )
    magnitude = jnp.sqrt(farfield[0] * farfield[0] + farfield[1] * farfield[1])
    keeping = 1.0 - measured_window / jnp.maximum(magnitude, magnitude_floor)
    backward = transform(farfield[0] * keeping, farfield[1] * keeping, cosine, sine_table, True)
    grad_second = complex_product(between[0], -between[1], backward[0], backward[1])
    toward = complex_product(window[2], -window[3], backward[0], backward[1])
    spectrum = transform(toward[0], toward[1], cosine, sine_table, False)
    spectrum = complex_product(spectrum[0], spectrum[1], slab_real, -slab_imag)
    incoming = transform(spectrum[0], spectrum[1], cosine, sine_table, True)
    grad_first = complex_product(illumination[0], -illumination[1], incoming[0], incoming[1])
    return jnp.stack([grad_first[0], grad_first[1], grad_second[0], grad_second[1]])


def fetch(shard, margin):
    shard = padded(shard, (("tx", 2),), margin)
    full_tile = lax.all_gather(shard, "pos", axis=1, tiled=True)
    return padded(full_tile, (("ty", 1),), margin)


def fold_edges(received, inner, margin, tile_side, axis_dim):
    widths_low = [(0, 0), (0, 0), (0, 0)]
    widths_high = [(0, 0), (0, 0), (0, 0)]
    widths_low[axis_dim] = (0, tile_side - margin)
    widths_high[axis_dim] = (tile_side - margin, 0)
    lower_piece = lax.slice_in_dim(received, 0, margin, axis=axis_dim)
    upper_piece = lax.slice_in_dim(received, 3 * margin, 4 * margin, axis=axis_dim)
    return inner + jnp.pad(lower_piece, widths_low) + jnp.pad(upper_piece, widths_high)


def shards(object_field, momentum, measured, illumination, slab_phase, offsets, entry_counts):
    width = illumination.shape[-1]
    margin = width // 4
    shard_rows = object_field.shape[2]
    tile_side = object_field.shape[3]
    capacity = measured.shape[2]
    extent = tile_side + 2 * margin
    cosine, sine_table = tables(width)
    slab_real = jnp.cos(slab_phase)
    slab_imag = jnp.sin(slab_phase)
    layers = object_field.reshape(4, shard_rows, tile_side)
    velocity_old = momentum.reshape(4, shard_rows, tile_side)
    places = offsets[0, 0]
    valid_count = entry_counts[0, 0]
    own_measured = measured[0, 0]
    own_index = lax.axis_index("pos")
    zero = jnp.zeros((), jnp.int32)
    last_slot = jnp.clip(valid_count - own_index * capacity, 0, capacity)

    def entry_of(slot_index):
        return own_index * capacity + slot_index

    extended = fetch(layers, margin)

    def accumulate(position, gradient):
        place = places[entry_of(position)]
        corner = (zero, place[0], place[1])
        window = lax.dynamic_slice(extended, corner, (4, width, width))
        term = window_gradient(
            window, own_measured[position], illumination, slab_real, slab_imag, cosine, sine_table
        )
        current = lax.dynamic_slice(gradient, corner, (4, width, width))
        return lax.dynamic_update_slice(gradient, current + term, corner)

    gradient = lax.fori_loop(
        zero, last_slot, accumulate, jnp.zeros((4, extent, extent), jnp.float32)
    )
    column_strips = jnp.concatenate(
        [gradient[:, :, :margin], gradient[:, :, extent - margin :]], axis=2
    )
    column_gains = padded(column_strips, (("tx", 2),), margin)
    inner_columns = fold_edges(
        column_gains, gradient[:, :, margin : margin + tile_side], margin, tile_side, 2
    )
    row_strips = jnp.concatenate(
        [inner_columns[:, :margin], inner_columns[:, extent - margin :]], axis=1
    )
    row_gains = padded(row_strips, (("ty", 1),), margin)
    folded = fold_edges(
        row_gains, inner_columns[:, margin : margin + tile_side], margin, tile_side, 1
    )
    gradient_shard = lax.psum_scatter(folded, "pos", scatter_dimension=1, tiled=True)
    velocity = momentum_rate * velocity_old + gradient_shard
    updated = layers - step_length * velocity
    refreshed = fetch(updated, margin)

    def predict(position, buffer):
        place = places[entry_of(position)]
        window = lax.dynamic_slice(refreshed, (zero, place[0], place[1]), (4, width, width))
        farfield = forward_window(window, illumination, slab_real, slab_imag, cosine, sine_table)[1]
        magnitude = jnp.sqrt(farfield[0] * farfield[0] + farfield[1] * farfield[1])
        return magnitude[None]

    buffer = lax.fori_loop(
        zero, last_slot, predict, jnp.zeros((own_measured.shape[0], width, width), jnp.float32)
    )
    return (
        updated.reshape(2, 2, shard_rows, tile_side),
        velocity.reshape(2, 2, shard_rows, tile_side),
        buffer[None, None],
    )


def solution(mesh):
    placed = (
        P(None, None, ("ty", "pos"), "tx"),
        P(None, None, ("ty", "pos"), "tx"),
        P("ty", "tx", "pos", None, None),
        P(),
        P(),
        P("ty", "tx", None, None),
        P("ty", "tx"),
    )
    return jax.shard_map(
        shards,
        mesh=mesh,
        in_specs=placed,
        out_specs=(
            P(None, None, ("ty", "pos"), "tx"),
            P(None, None, ("ty", "pos"), "tx"),
            P("ty", "tx", "pos", None, None),
        ),
        check_vma=False,
    )
```

profile of v0, /device:TPU:1, one launch (start us, length us, event | category | flops | bytes accessed | tf_op | source)
XLA Modules:
  0.0 368.2 jit_solution(7131746287392692887)
XLA Ops:
  8.5 4.0 %collective-permute-start = (f32[4,64,64]{2,0,1:T(4,128)S(1)}, f32[4,64,64]{2,0,1:T(4,128)S(1)}, u32[]{:S(2)}, u32[]{:S(2)}) collective-permute-start(f32[4,64,64]{2,0,1:T(4,128)S(1)} %get-tuple-element.727), channel_id=1, source_target_pairs={{0,4},{4,8},{8,12},{1,5},{5,9},{9,13},{2,6},{6,10},{10,14},{3,7},{... | collective-permute-start | bytes 196616 | tf_op jit(solution)/shard_map/ppermute | solution.py:21
  14.7 3.6 collective-permute-done.1
  19.6 32.3 %all-gather.3.cloned.1.call-done = f32[4,256,384]{2,0,1:T(4,128)} async-done(((f32[4,64,384]{2,0,1:T(4,128)}), f32[4,256,384]{2,0,1:T(4,128)}) %all-gather.3.cloned.1.call-update) | async-done | bytes 1572880 | tf_op jit(solution)/shard_map/all_gather | solution.py:85
  55.3 4.7 %collective-permute-start.3 = (f32[4,64,384]{2,1,0:T(8,128)}, f32[4,64,384]{2,1,0:T(8,128)}, u32[]{:S(2)}, u32[]{:S(2)}) collective-permute-start(f32[4,64,384]{2,1,0:T(8,128)} %copy.48), channel_id=1, source_target_pairs={{16,0},{17,1},{18,2},{19,3},{20,4},{21,5},{22,6},{23,7},{24,8},{25... | collective-permute-start | bytes 1179656 | tf_op jit(solution)/shard_map/ppermute | solution.py:22
  66.3 1.9 pad_maximum_fusion
  69.8 102.1 %while.25 = (s32[]{:T(128)}, f32[4,384,384]{1,2,0:T(8,128)}, s32[]{:T(128)}, s32[]{:T(128)}, s32[4,2]{0,1:T(2,128)S(1)}, /*index=5*/f32[2,256,256]{1,2,0:T(8,128...) while((s32[]{:T(128)}, f32[4,384,384]{1,2,0:T(8,128)}, ...), condition=%wide.region_1.2_spmd.clone.clone, body=%wide.region_0.1_spmd.clone.clone.sunk | while | flops 9717678080 | bytes 49807748 | solution.py:133
  74.9 5.5 %fusion.744 = (f32[1,256,256]{2,0,1:T(1,128)S(1)}, f32[1,256,256]{2,0,1:T(1,128)S(1)}, f32[1,256,256]{2,0,1:T(1,128)S(1)}, f32[1,256,256]{2,0,1:T(1,128)S(1)}) fusion(f32[4,384,384]{2,0,1:T(4,128)} %get-tuple-element.971, s32[]{:T(128)S(6)} %add.829, s32[]{:T(128)S(6)} %select_n.437, s32[]{:T(128)S(6)} %select_n.438, s32[]{:T(128)S(6)} %add.834, ...), kind=kLoop, calls=%fused_computation.563.clone.1 | loop fusion | bytes 2097172 | tf_op jit(solution)/shard_map/while/body/slice | solution.py:75
  89.7 1.6 fusion.752
  101.7 1.7 fusion.757
  112.6 1.9 fusion.764
  124.9 1.7 fusion.770
  137.0 1.7 fusion.778
  149.1 1.9 fusion.783
  154.0 1.8 maximum_add_fusion.2
  155.8 11.6 %dynamic_update_slice.7 = f32[4,384,384]{1,2,0:T(8,128)} dynamic-update-slice(f32[4,384,384]{1,2,0:T(8,128)} %get-tuple-element.947, f32[4,256,256]{1,2,0:T(8,128)S(1)} %maximum_add_fusion.2, s32[]{:T(128)} %constant.57.clone.1..sunk, s32[]{:T(128)S(6)} %select_n.437, s32[]{:T(128)S(6)} %select_n.438) | dynamic-update-slice | bytes 2097156 | tf_op jit(solution)/shard_map/while/body/dynamic_update_slice | solution.py:131
  173.1 2.6 collective-permute-start.4
  177.1 6.7 %collective-permute-done.4 = f32[4,384,64]{1,2,0:T(8,128)S(1)} collective-permute-done((f32[4,384,64]{1,2,0:T(8,128)S(1)}, f32[4,384,64]{1,2,0:T(8,128)S(1)}, u32[]{:S(2)}, u32[]{:S(2)}) %collective-permute-start.4) | collective-permute-done | bytes 393248 | tf_op jit(solution)/shard_map/ppermute | solution.py:21
  183.7 4.1 %collective-permute-done.5 = f32[4,384,64]{1,2,0:T(8,128)S(1)} collective-permute-done((f32[4,384,64]{1,2,0:T(8,128)S(1)}, f32[4,384,64]{1,2,0:T(8,128)S(1)}, u32[]{:S(2)}, u32[]{:S(2)}) %collective-permute-start.5) | collective-permute-done | bytes 393248 | tf_op jit(solution)/shard_map/ppermute | solution.py:22
  190.9 3.1 collective-permute-start.7
  198.7 48.9 %all-reduce.7.cloned.1.call-done = f32[4,256,256]{2,0,1:T(4,128)} async-done(((f32[4,256,256]{2,0,1:T(4,128)}), f32[4,256,256]{2,0,1:T(4,128)}) %all-reduce.7.cloned.1.call-update) | async-done | bytes 1048592
  249.1 3.1 collective-permute-start.8
  254.2 3.8 %collective-permute-done.9 = f32[4,64,64]{2,0,1:T(4,128)S(1)} collective-permute-done((f32[4,64,64]{2,0,1:T(4,128)S(1)}, f32[4,64,64]{2,0,1:T(4,128)S(1)}, u32[]{:S(2)}, u32[]{:S(2)}) %collective-permute-start.9) | collective-permute-done | bytes 65568 | tf_op jit(solution)/shard_map/ppermute | solution.py:22
  259.1 31.5 %all-gather.5.cloned.1.call-done = f32[4,256,384]{2,0,1:T(4,128)} async-done(((f32[4,64,384]{2,0,1:T(4,128)}), f32[4,256,384]{2,0,1:T(4,128)}) %all-gather.5.cloned.1.call-update) | async-done | bytes 1572880 | tf_op jit(solution)/shard_map/all_gather | solution.py:85
  294.0 4.5 %collective-permute-start.11 = (f32[4,64,384]{2,1,0:T(8,128)}, f32[4,64,384]{2,1,0:T(8,128)}, u32[]{:S(2)}, u32[]{:S(2)}) collective-permute-start(f32[4,64,384]{2,1,0:T(8,128)} %copy.59), channel_id=1, source_target_pairs={{16,0},{17,1},{18,2},{19,3},{20,4},{21,5},{22,6},{23,7},{24,8},{25... | collective-permute-start | bytes 1179656 | tf_op jit(solution)/shard_map/ppermute | solution.py:22
  302.6 1.9 pad_maximum_fusion.1
  305.2 54.4 %while.26 = (s32[]{:T(128)}, f32[1,256,256]{1,2,0:T(8,128)}, s32[]{:T(128)}, f32[2,256,256]{1,2,0:T(8,128)S(1)}, s32[]{:T(128)}, /*index=5*/s32[4,2]{0,1:T(2,128...) while((s32[]{:T(128)}, f32[1,256,256]{1,2,0:T(8,128)}, ...), condition=%wide.region_4.5_spmd.clone.clone, body=%wide.region_3.4_spmd.clone.clone.sunk | while | flops 4858118144 | bytes 23855460 | solution.py:162
  310.0 5.5 %fusion.811 = (f32[1,256,256]{2,0,1:T(1,128)S(1)}, f32[1,256,256]{2,0,1:T(1,128)S(1)}, f32[1,256,256]{2,0,1:T(1,128)S(1)}, f32[1,256,256]{2,0,1:T(1,128)S(1)}) fusion(f32[4,384,384]{2,0,1:T(4,128)} %get-tuple-element.1022, s32[]{:T(128)S(6)} %add.867, s32[]{:T(128)S(6)} %select_n.464, s32[]{:T(128)S(6)} %select_n.465, s32[]{:T(128)S(6)} %add.872, ...), kind=kLoop, calls=%fused_computation.565.clone.1 | loop fusion | bytes 2097172 | tf_op jit(solution)/shard_map/while/body/slice | solution.py:60
  324.8 1.6 fusion.818
  336.9 1.7 fusion.823
  347.8 1.9 fusion.830
  351.1 2.2 fusion.832
  359.6 1.8 copy.64
  (147 shorter events, 131.7 us)
Async XLA Ops:
  7.2 12.3 %copy-start.3 = (f32[256,256]{1,0:T(8,128)S(1)}, f32[256,256]{1,0:T(8,128)}, u32[]{:S(2)}) copy-start(f32[256,256]{1,0:T(8,128)} %param.15) | copy-start | bytes 786436
  7.2 44.7 %all-gather.3.cloned.1.call-start = ((), (), s32[]{:S(2)}) async-start(), calls=%async_computation | async-start | bytes 1966080 | tf_op jit(solution)/shard_map/all_gather | solution.py:85
  8.5 6.2 %collective-permute-start = (f32[4,64,64]{2,0,1:T(4,128)S(1)}, f32[4,64,64]{2,0,1:T(4,128)S(1)}, u32[]{:S(2)}, u32[]{:S(2)}) collective-permute-start(f32[4,64,64]{2,0,1:T(4,128)S(1)} %get-tuple-element.727), channel_id=1, source_target_pairs={{0,4},{4,8},{8,12},{1,5},{5,9},{9,13},{2,6},{6,10},{10,14},{3,7},{... | collective-permute-start | bytes 196616 | tf_op jit(solution)/shard_map/ppermute | solution.py:21
  12.5 5.7 %collective-permute-start.1 = (f32[4,64,64]{2,0,1:T(4,128)S(1)}, f32[4,64,64]{2,0,1:T(4,128)S(1)}, u32[]{:S(2)}, u32[]{:S(2)}) collective-permute-start(f32[4,64,64]{2,0,1:T(4,128)S(1)} %get-tuple-element.728), channel_id=1, source_target_pairs={{4,0},{8,4},{12,8},{5,1},{9,5},{13,9},{6,2},{10,6},{14,10},{7,3},{... | collective-permute-start | bytes 196616 | tf_op jit(solution)/shard_map/ppermute | solution.py:22
  19.4 228.3 %all-reduce.7.cloned.1.call-start = ((), (), s32[]{:S(2)}) async-start(), calls=%async_computation.2 | async-start | bytes 2097152
  53.1 9.8 %copy-start.4 = (f32[1,1,1,256,256]{4,3,2,1,0:T(8,128)S(1)}, f32[1,1,1,256,256]{4,3,2,1,0:T(8,128)}, u32[]{:S(2)}) copy-start(f32[1,1,1,256,256]{4,3,2,1,0:T(8,128)} %param.13) | copy-start | bytes 786436
  53.1 10.6 %collective-permute-start.2 = (f32[4,64,384]{2,1,0:T(8,128)S(1)}, f32[4,64,384]{2,1,0:T(8,128)}, u32[]{:S(2)}, u32[]{:S(2)}) collective-permute-start(f32[4,64,384]{2,1,0:T(8,128)S(1)} %copy.47), channel_id=1, source_target_pairs={{0,16},{1,17},{2,18},{3,19},{4,20},{5,21},{6,22},{7,23},{8,24},{9,... | collective-permute-start | bytes 1179656 | tf_op jit(solution)/shard_map/ppermute | solution.py:21
  55.3 11.0 %copy-start = (f32[4,256,384]{2,0,1:T(4,128)S(1)}, f32[4,256,384]{2,0,1:T(4,128)}, u32[]{:S(2)}) copy-start(f32[4,256,384]{2,0,1:T(4,128)} %all-gather.3.cloned.1.call-done) | copy-start | bytes 4718596
  55.3 9.7 %collective-permute-start.3 = (f32[4,64,384]{2,1,0:T(8,128)}, f32[4,64,384]{2,1,0:T(8,128)}, u32[]{:S(2)}, u32[]{:S(2)}) collective-permute-start(f32[4,64,384]{2,1,0:T(8,128)} %copy.48), channel_id=1, source_target_pairs={{16,0},{17,1},{18,2},{19,3},{20,4},{21,5},{22,6},{23,7},{24,8},{25... | collective-permute-start | bytes 1179656 | tf_op jit(solution)/shard_map/ppermute | solution.py:22
  68.2 1.6 copy-start.6
  68.2 1.6 copy-start.7
  173.1 10.6 %collective-permute-start.4 = (f32[4,384,64]{1,2,0:T(8,128)S(1)}, f32[4,384,64]{1,2,0:T(8,128)S(1)}, u32[]{:S(2)}, u32[]{:S(2)}) collective-permute-start(f32[4,384,64]{1,2,0:T(8,128)S(1)} %get-tuple-element.715), channel_id=1, source_target_pairs={{0,4},{4,8},{8,12},{1,5},{5,9},{9,13},{2,6},{6,10},{10,14},{3,7},{... | collective-permute-start | bytes 1179656 | tf_op jit(solution)/shard_map/ppermute | solution.py:21
  175.8 12.1 %collective-permute-start.5 = (f32[4,384,64]{1,2,0:T(8,128)S(1)}, f32[4,384,64]{1,2,0:T(8,128)S(1)}, u32[]{:S(2)}, u32[]{:S(2)}) collective-permute-start(f32[4,384,64]{1,2,0:T(8,128)S(1)} %get-tuple-element.716), channel_id=1, source_target_pairs={{4,0},{8,4},{12,8},{5,1},{9,5},{13,9},{6,2},{10,6},{14,10},{7,3},{... | collective-permute-start | bytes 1179656 | tf_op jit(solution)/shard_map/ppermute | solution.py:22
  189.6 4.4 %collective-permute-start.6 = (f32[4,64,256]{1,2,0:T(8,128)S(1)}, f32[4,64,256]{1,2,0:T(8,128)S(1)}, u32[]{:S(2)}, u32[]{:S(2)}) collective-permute-start(f32[4,64,256]{1,2,0:T(8,128)S(1)} %get-tuple-element.719), channel_id=1, source_target_pairs={{0,16},{1,17},{2,18},{3,19},{4,20},{5,21},{6,22},{7,23},{8,24},{9,... | collective-permute-start | bytes 786440 | tf_op jit(solution)/shard_map/ppermute | solution.py:21
  190.9 4.6 %collective-permute-start.7 = (f32[4,64,256]{1,2,0:T(8,128)S(1)}, f32[4,64,256]{1,2,0:T(8,128)S(1)}, u32[]{:S(2)}, u32[]{:S(2)}) collective-permute-start(f32[4,64,256]{1,2,0:T(8,128)S(1)} %get-tuple-element.720), channel_id=1, source_target_pairs={{16,0},{17,1},{18,2},{19,3},{20,4},{21,5},{22,6},{23,7},{24,8},{25... | collective-permute-start | bytes 786440 | tf_op jit(solution)/shard_map/ppermute | solution.py:22
  196.0 1.4 copy-start.8
  196.0 2.7 copy-start.5
  196.0 51.6 %copy-start.2 = (f32[2,2,64,256]{3,2,1,0:T(8,128)S(1)}, f32[2,2,64,256]{3,2,1,0:T(8,128)}, u32[]{:S(2)}) copy-start(f32[2,2,64,256]{3,2,1,0:T(8,128)} %param.11) | copy-start | bytes 786436
  197.4 93.2 %all-gather.5.cloned.1.call-start = ((), (), s32[]{:S(2)}) async-start(), calls=%async_computation.1 | async-start | bytes 1966080 | tf_op jit(solution)/shard_map/all_gather | solution.py:85
  249.1 5.0 %collective-permute-start.8 = (f32[4,64,64]{2,0,1:T(4,128)S(1)}, f32[4,64,64]{2,0,1:T(4,128)S(1)}, u32[]{:S(2)}, u32[]{:S(2)}) collective-permute-start(f32[4,64,64]{2,0,1:T(4,128)S(1)} %get-tuple-element.723), channel_id=1, source_target_pairs={{0,4},{4,8},{8,12},{1,5},{5,9},{9,13},{2,6},{6,10},{10,14},{3,7},{... | collective-permute-start | bytes 196616 | tf_op jit(solution)/shard_map/ppermute | solution.py:21
  252.3 5.7 %collective-permute-start.9 = (f32[4,64,64]{2,0,1:T(4,128)S(1)}, f32[4,64,64]{2,0,1:T(4,128)S(1)}, u32[]{:S(2)}, u32[]{:S(2)}) collective-permute-start(f32[4,64,64]{2,0,1:T(4,128)S(1)} %get-tuple-element.724), channel_id=1, source_target_pairs={{4,0},{8,4},{12,8},{5,1},{9,5},{13,9},{6,2},{10,6},{14,10},{7,3},{... | collective-permute-start | bytes 196616 | tf_op jit(solution)/shard_map/ppermute | solution.py:22
  291.8 10.8 %copy-start.1 = (f32[4,256,384]{2,0,1:T(4,128)S(1)}, f32[4,256,384]{2,0,1:T(4,128)}, u32[]{:S(2)}) copy-start(f32[4,256,384]{2,0,1:T(4,128)} %all-gather.5.cloned.1.call-done) | copy-start | bytes 4718596
  291.8 8.3 %collective-permute-start.10 = (f32[4,64,384]{2,1,0:T(8,128)S(1)}, f32[4,64,384]{2,1,0:T(8,128)}, u32[]{:S(2)}, u32[]{:S(2)}) collective-permute-start(f32[4,64,384]{2,1,0:T(8,128)S(1)} %copy.58), channel_id=1, source_target_pairs={{0,16},{1,17},{2,18},{3,19},{4,20},{5,21},{6,22},{7,23},{8,24},{9,... | collective-permute-start | bytes 1179656 | tf_op jit(solution)/shard_map/ppermute | solution.py:21
  294.0 7.3 %collective-permute-start.11 = (f32[4,64,384]{2,1,0:T(8,128)}, f32[4,64,384]{2,1,0:T(8,128)}, u32[]{:S(2)}, u32[]{:S(2)}) collective-permute-start(f32[4,64,384]{2,1,0:T(8,128)} %copy.59), channel_id=1, source_target_pairs={{16,0},{17,1},{18,2},{19,3},{20,4},{21,5},{22,6},{23,7},{24,8},{25... | collective-permute-start | bytes 1179656 | tf_op jit(solution)/shard_map/ppermute | solution.py:22
Sparse Core Ops, SparseCore 0:
  19.5 32.3 all-gather.2
  197.5 50.0 all-reduce.6
  259.2 31.3 all-gather.4
where the time goes:
time: 373 us; the launch traced here: 368 us
  waiting for transfers between devices  134 us (36%)
  matrix products  110 us (29%)
  local copies, waits for them, and re-layouts  47.5 us (13%)
  starting transfers between devices  30.2 us (8%)
  loops' own time  20.1 us (5%)
  between operations  15.7 us (4%)
  other arithmetic  11.4 us (3%)
    dot_general x72, matrix products, matmul(): return jnp.dot(left, right, precision=HIGHEST)  110 us
    all_gather x2, waiting for transfers between devices, fetch(): full_tile = lax.all_gather(shard, 'pos', axis=1, tiled=True)  63.8 us
    unnamed x4, waiting for transfers between devices  49 us
    ppermute x6, starting transfers between devices, padded(): after = lax.ppermute(leading, axis, down)  16.2 us
    ppermute x6, starting transfers between devices, padded(): before = lax.ppermute(last, axis, up)  13.9 us
    ppermute x6, waiting for transfers between devices, padded(): after = lax.ppermute(leading, axis, down)  12.9 us
    dynamic_update_slice x1, local copies, waits for them, and re-layouts, accumulate(): return lax.dynamic_update_slice(gradient, current + term, corner)  11.6 us
    another operation x1, loops' own time, shards(): lax.fori_loop(zero, last_slot, predict, jnp.zeros((own_measured.shape[0],...  10.6 us
  transfers between devices with their start and end apart: 15, of which 10 were waited for; matrix products, arithmetic and copies ran while one was open for 3% of the time, Pallas kernels for 0%

commit v1 on v0

v1 whole, which is shorter than its diff:
```python
import math

import jax
import jax.numpy as jnp
import numpy as np
from jax import lax
from jax.experimental import pallas as pl
from jax.experimental.pallas import tpu as pltpu
from jax.sharding import PartitionSpec as P

magnitude_floor = 0.5
momentum_rate = 0.9
step_length = 0.05
F32 = jnp.float32
BF16 = jnp.bfloat16


def vmem():
    return pl.BlockSpec(memory_space=pltpu.VMEM)


def smem():
    return pl.BlockSpec(memory_space=pltpu.SMEM)


def call(body, outs, args, scalars=0, scratch=(), name=None):
    specs = [smem()] * scalars + [vmem()] * (len(args) - scalars)
    return pl.pallas_call(
        body,
        out_shape=tuple(jax.ShapeDtypeStruct(s, F32) for s in outs),
        in_specs=specs,
        out_specs=tuple(vmem() for _ in outs),
        scratch_shapes=list(scratch),
        name=name,
        compiler_params=pltpu.CompilerParams(vmem_limit_bytes=56 * 1024 * 1024),
    )(*args)


def split_table(values):
    high = values.astype(jnp.bfloat16)
    low = (values - high.astype(np.float64)).astype(jnp.bfloat16)
    return high, low


def dft_tables(length):
    index = np.arange(length)
    angles = (index[:, None] * index[None, :] % length) * (2.0 * math.pi / length)
    cosine, sine = np.cos(angles) / math.sqrt(length), np.sin(angles) / math.sqrt(length)
    parts = [part for t in (cosine, cosine + sine, cosine - sine) for part in split_table(t)]
    return np.stack(parts)


def iota(shape, dim):
    return lax.broadcasted_iota(jnp.int32, shape, dim)


def split(value):
    high = value.astype(BF16)
    return high, (value - high.astype(F32)).astype(BF16)


def dot(left, right):
    return jnp.dot(left, right, preferred_element_type=F32)


def mul3(left, right):
    return dot(left[0], right[0]) + dot(left[0], right[1]) + dot(left[1], right[0])


def transform(real, imag, tab, inverse):
    cos = (tab[0], tab[1])
    plus, minus = ((tab[4], tab[5]), (tab[2], tab[3])) if inverse else ((tab[2], tab[3]), (tab[4], tab[5]))
    both = mul3(split(real + imag), cos)
    right_imag = both - mul3(split(real), plus)
    right_real = both - mul3(split(imag), minus)
    both = mul3(cos, split(right_real + right_imag))
    left_imag = both - mul3(plus, split(right_real))
    left_real = both - mul3(minus, split(right_imag))
    return left_real, left_imag


def cmul(ar, ai, br, bi):
    return ar * br - ai * bi, ar * bi + ai * br


class Layout:
    def __init__(self, object_field, illumination, offsets):
        self.n = lax.axis_size("pos")
        self.ntx = lax.axis_size("tx")
        self.nty = lax.axis_size("ty")
        self.h = object_field.shape[2]
        self.t = object_field.shape[3]
        self.m = illumination.shape[-1] // 4
        self.slots = offsets.shape[2]
        self.half = self.n // 2
        assert self.nty == 2 and self.slots == self.n and self.n & (self.n - 1) == 0
        assert self.t == illumination.shape[-1] == self.n * self.h == 4 * self.m

    def window_of(self, device, row, home):
        return device if home else device - row * self.half

    def holds(self, device, row, home):
        return 0 <= self.window_of(device, row, home) < self.half

    def inward(self, s, home):
        n = self.n
        return [(a * n + p, a * n + (p ^ s)) for a in range(2) for p in range(n) if self.holds(p ^ s, a, home)]

    def outward(self, s):
        return [(d, o) for o, d in self.inward(s, False)]


def complete(pairs, n):
    sources, targets = {x for x, _ in pairs}, {y for _, y in pairs}
    other = lambda x: (x + n) % (2 * n)
    extra = [(x, other(x)) for x in range(2 * n) if x not in sources and other(x) not in targets]
    return pairs + extra if len(pairs) + len(extra) == 2 * n else pairs


def where_am_i():
    return lax.axis_index("ty"), lax.axis_index("tx"), lax.axis_index("pos")


def masks(place_ref, k, a, p, lay):
    h, t, m = lay.h, lay.t, lay.m
    k = jnp.clip(k, 0, lay.slots - 1)
    top = place_ref[0, 0, k, 0] - m
    left = place_ref[0, 0, k, 1] - m
    rows = iota((h, t), 0) + p * h
    cols = iota((h, t), 1)
    above = rows >= top + t
    below = rows < top
    outside = above | below
    partner = (above & (a == 1)) | (below & (a == 0))
    halo = (cols >= left + t) | (cols < left)
    return outside, partner, halo


def pack_blocks(place_ref, own, own_halo, prt, prt_halo, out_refs, lay, home):
    a, _, p = where_am_i()
    for s in range(lay.n):
        k = lay.window_of(p ^ s, a, home)
        outside, partner, halo = masks(place_ref, k, a, p, lay)
        for c in range(4):
            mine = jnp.where(halo, spread(own_halo[c], lay), own[c])
            theirs = jnp.where(halo, spread(prt_halo[c], lay), prt[c])
            out_refs[s][c] = jnp.where(partner, theirs, jnp.where(outside, 0.0, mine))


def spread(halo, lay):
    return halo if lay.t == 2 * lay.m else jnp.concatenate([halo, halo], axis=1)


def roll_half(x, lay):
    return pltpu.roll(x, lay.m, 1)


def kernel_strips(lay):
    t, m = lay.t, lay.m

    def body(own_ref, prt_ref, out_ref):
        a = lax.axis_index("ty")
        low = iota((lay.h, 2 * m), 1) < m
        for c in range(4):
            for row in (0, 1):

                @pl.when(a == row)
                def _(c=c, row=row):
                    cut = slice(t - 2 * m, t) if row == 0 else slice(0, 2 * m)
                    first, second = (own_ref, prt_ref) if row == 0 else (prt_ref, own_ref)
                    x0, x1 = first[c, :, cut], roll_half(second[c, :, cut], lay)
                    out_ref[c] = jnp.where(low, x1, x0) if row == 0 else jnp.where(low, x0, x1)

    return body


def kernel_pack(lay):
    m = lay.m

    def body(place_ref, own_ref, prt_ref, mine_ref, theirs_ref, *outs):
        a, b, _ = where_am_i()
        blocks, own_halo_ref, prt_halo_ref = outs[: lay.n], outs[lay.n], outs[lay.n + 1]
        low = iota((lay.h, 2 * m), 1) < m
        keep = jnp.where(low, (b < lay.ntx - 1).astype(F32), (b > 0).astype(F32))
        for c in range(4):
            from_left = jnp.where(a == 0, mine_ref[c], theirs_ref[c])
            from_right = jnp.where(a == 0, theirs_ref[c], mine_ref[c])
            halo0 = jnp.where(low, from_right, from_left)
            halo1 = jnp.where(low, roll_half(from_right, lay), roll_half(from_left, lay))
            own_halo_ref[c] = jnp.where(keep > 0, jnp.where(a == 0, halo0, halo1), 0.0)
            prt_halo_ref[c] = jnp.where(keep > 0, jnp.where(a == 0, halo1, halo0), 0.0)
        pack_blocks(place_ref, own_ref, own_halo_ref, prt_ref, prt_halo_ref, blocks, lay, False)

    return body


def kernel_probe(lay):
    def body(place_ref, light_ref, out_ref):
        a, _, p = where_am_i()
        for i, home in enumerate((False, True)):
            k = jnp.clip(lay.window_of(p, a, home), 0, lay.slots - 1)
            down = (place_ref[0, 0, k, 0] + (lay.t - lay.m)) % lay.t
            along = (place_ref[0, 0, k, 1] + (lay.t - lay.m)) % lay.t
            for c in range(2):
                out_ref[i, c] = pltpu.roll(pltpu.roll(light_ref[c], down, 0), along, 1)

    return body


def assemble(blocks, window_ref, lay):
    p = lax.axis_index("pos")
    for s in range(lay.n):
        start = pl.multiple_of((p ^ s) * lay.h, lay.h)
        for c in range(4):
            window_ref[c, pl.ds(start, lay.h), :] = blocks[s][c]


def forward(window_ref, light_ref, which, slab_ref, tab):
    o1r, o1i, o2r, o2i = (window_ref[c] for c in range(4))
    er, ei = cmul(light_ref[which, 0], light_ref[which, 1], o1r, o1i)
    sr, si = transform(er, ei, tab, False)
    sr, si = cmul(sr, si, slab_ref[0], slab_ref[1])
    br, bi = transform(sr, si, tab, True)
    lr, li = cmul(br, bi, o2r, o2i)
    return br, bi, transform(lr, li, tab, False)


def kernel_gradient(lay):
    def body(count_ref, *refs):
        n = lay.n
        blocks, (light_ref, slab_ref, tab, meas_ref, moved_ref) = refs[:n], refs[n : n + 5]
        outs, window_ref = refs[n + 5 : 2 * n + 5], refs[2 * n + 5]
        a, _, p = where_am_i()
        k = lay.window_of(p, a, False)

        @pl.when((k >= 0) & (k < count_ref[0, 0]))
        def _():
            assemble(blocks, window_ref, lay)
            br, bi, (fr, fi) = forward(window_ref, light_ref, 0, slab_ref, tab)
            seen = jnp.where(a == 0, meas_ref[0, 0, 0], moved_ref[0, 0, 0])
            keeping = 1.0 - seen / jnp.maximum(jnp.sqrt(fr * fr + fi * fi), magnitude_floor)
            kr, ki = transform(fr * keeping, fi * keeping, tab, True)
            g2r, g2i = cmul(br, -bi, kr, ki)
            tr, ti = cmul(window_ref[2], -window_ref[3], kr, ki)
            window_ref[2] = g2r
            window_ref[3] = g2i
            sr, si = transform(tr, ti, tab, False)
            sr, si = cmul(sr, si, slab_ref[0], -slab_ref[1])
            ir, ii = transform(sr, si, tab, True)
            g1r, g1i = cmul(light_ref[0, 0], -light_ref[0, 1], ir, ii)
            window_ref[0] = g1r
            window_ref[1] = g1i
            for s in range(n):
                start = pl.multiple_of((p ^ s) * lay.h, lay.h)
                for c in range(4):
                    outs[s][c] = window_ref[c, pl.ds(start, lay.h), :]

    return body


def kernel_collect(lay):
    t, m = lay.t, lay.m

    def body(place_ref, count_ref, *refs):
        n = lay.n
        blocks, mom_ref = refs[:n], refs[n]
        own_ref, halo_ref = refs[n + 1 :]
        a, _, p = where_am_i()
        low = iota((lay.h, 2 * m), 1) < m
        own_ref[0] = momentum_rate * mom_ref[...]
        own_ref[1] = jnp.zeros(own_ref.shape[1:], F32)
        halo_ref[...] = jnp.zeros(halo_ref.shape, F32)
        for s in range(n):
            k = lay.window_of(p ^ s, a, False)

            @pl.when((k >= 0) & (k < count_ref[0, 0]))
            def _(s=s, k=k):
                outside, partner, halo = masks(place_ref, k, a, p, lay)
                for c in range(4):
                    g = blocks[s][c]
                    for i, rows in enumerate((~outside, partner)):
                        own_ref[i, c] += jnp.where(rows & ~halo, g, 0.0)
                        x = jnp.where(rows & halo, g, 0.0)
                        halo_ref[i, c] += jnp.where(low, x[:, : 2 * m], x[:, t - 2 * m :])

    return body


def kernel_strips_back(lay):
    t, m = lay.t, lay.m

    def body(own_ref, halo_ref, their_own_ref, their_halo_ref, sum_ref, halo_sum_ref, out_ref):
        a = lax.axis_index("ty")
        low = iota((lay.h, 2 * m), 1) < m
        for c in range(4):
            for i in range(2):
                sum_ref[i, c] = own_ref[i, c] + their_own_ref[1 - i, c]
                halo_sum_ref[i, c] = halo_ref[i, c] + their_halo_ref[1 - i, c]
        for row in (0, 1):

            @pl.when(a == row)
            def _(row=row):
                for tile in range(2):
                    i = tile ^ row
                    for c in range(4):
                        halo = halo_sum_ref[i, c]
                        if row == 0:
                            out_ref[tile, c] = jnp.where(low, halo, sum_ref[i, c, :, t - 2 * m :])
                        else:
                            out_ref[tile, c] = jnp.where(low, sum_ref[i, c, :, : 2 * m], halo)

    return body


def kernel_update(lay):
    t, m = lay.t, lay.m

    def body(place_ref, obj_ref, prt_ref, obj_halo_ref, prt_halo_ref, sum_ref, halo_sum_ref, mine_ref, theirs_ref, *outs):
        n = lay.n
        new_ref, vel_ref, blocks, prt_new, own_halo, prt_halo = outs[0], outs[1], outs[2 : n + 2], *outs[n + 2 :]
        a, b, _ = where_am_i()
        low = iota((lay.h, 2 * m), 1) < m
        not_first, not_last = b > 0, b < lay.ntx - 1
        keep = (low & not_last) | (~low & not_first)
        for i in range(2):
            tile = a if i == 0 else 1 - a
            for c in range(4):
                mine, theirs = mine_ref[tile, c], theirs_ref[tile, c]
                from_left = jnp.where(not_first, jnp.where(a == 0, mine, theirs), 0.0)
                from_right = jnp.where(not_last, jnp.where(a == 0, theirs, mine), 0.0)
                v = sum_ref[i, c] + jnp.concatenate(
                    [jnp.where(low, from_left, 0.0), jnp.where(low, 0.0, from_right)], axis=1
                )
                hv = halo_sum_ref[i, c] + jnp.where(low, from_right, from_left)
                obj, halo = (obj_ref, obj_halo_ref) if i == 0 else (prt_ref, prt_halo_ref)
                new, new_halo = (new_ref, own_halo) if i == 0 else (prt_new, prt_halo)
                if i == 0:
                    vel_ref[c] = v
                new[c] = obj[c] - step_length * v
                new_halo[c] = jnp.where(keep, halo[c] - step_length * hv, 0.0)
        pack_blocks(place_ref, new_ref, own_halo, prt_new, prt_halo, blocks, lay, True)

    return body


def kernel_predict(lay):
    def body(count_ref, *refs):
        n = lay.n
        blocks, (light_ref, slab_ref, tab), out_ref, window_ref = refs[:n], refs[n : n + 3], refs[n + 3], refs[n + 4]
        p = lax.axis_index("pos")

        @pl.when(p < count_ref[0, 0])
        def _():
            assemble(blocks, window_ref, lay)
            _, _, (fr, fi) = forward(window_ref, light_ref, 1, slab_ref, tab)
            out_ref[0, 0, 0] = jnp.sqrt(fr * fr + fi * fi)

        @pl.when(p >= count_ref[0, 0])
        def _():
            out_ref[...] = jnp.zeros(out_ref.shape, F32)

    return body


def shards(object_field, momentum, measured, illumination, slab_phase, offsets, entry_counts):
    lay = Layout(object_field, illumination, offsets)
    n, h, t, m = lay.n, lay.h, lay.t, lay.m
    own = object_field.reshape(4, h, t)
    velocity_old = momentum.reshape(4, h, t)
    block, halo_shape = (4, h, t), (4, h, 2 * m)
    cores = lambda x: lax.ppermute(x, "ty", [(0, 1), (1, 0)])
    ring = [((a * lay.ntx + b), a * lay.ntx + (b + 1 - 2 * a) % lay.ntx) for a in range(2) for b in range(lay.ntx)]
    columns = lambda x: lax.ppermute(x, ("ty", "tx"), ring)
    send = lambda x, pairs: lax.ppermute(x, ("ty", "pos"), complete(pairs, n))

    moved = lax.ppermute(measured, "pos", [(p, p ^ lay.half) for p in range(n)])
    tab = jnp.asarray(dft_tables(t))
    slab = jnp.stack([jnp.cos(slab_phase), jnp.sin(slab_phase)])
    (light,) = call(kernel_probe(lay), [(2, 2, t, t)], [offsets, illumination], 1, name="probe_move")

    partner = cores(own)
    (strips,) = call(kernel_strips(lay), [halo_shape], [own, partner], name="strips")
    strips = columns(strips)
    strips_other = cores(strips)
    *blocks, own_halo, partner_halo = call(
        kernel_pack(lay),
        [block] * n + [halo_shape] * 2,
        [offsets, own, partner, strips, strips_other],
        1,
        name="pack",
    )
    received = [blocks[0]] + [send(blocks[s], lay.inward(s, False)) for s in range(1, n)]
    window = pltpu.VMEM((4, t, t), F32)
    terms = call(
        kernel_gradient(lay),
        [block] * n,
        [entry_counts, *received, light, slab, tab, measured, moved],
        1,
        [window],
        name="gradient",
    )
    parts = [terms[0]] + [send(terms[s], lay.outward(s)) for s in range(1, n)]
    sums, halos = call(
        kernel_collect(lay),
        [(2, *block), (2, *halo_shape)],
        [offsets, entry_counts, *parts, velocity_old],
        2,
        name="collect",
    )
    sums, halos, strips = call(
        kernel_strips_back(lay),
        [(2, *block), (2, *halo_shape), (2, *halo_shape)],
        [sums, halos, cores(sums), cores(halos)],
        name="strips_back",
    )
    strips = columns(strips)
    updated, velocity, *rest = call(
        kernel_update(lay),
        [block] * (n + 3) + [halo_shape] * 2,
        [offsets, own, partner, own_halo, partner_halo, sums, halos, strips, cores(strips)],
        1,
        name="update",
    )
    blocks = rest[:n]
    received = [blocks[0]] + [send(blocks[s], lay.inward(s, True)) for s in range(1, n)]
    (amplitudes,) = call(
        kernel_predict(lay),
        [measured.shape],
        [entry_counts, *received, light, slab, tab],
        1,
        [window],
        name="predict",
    )
    return (
        updated.reshape(object_field.shape),
        velocity.reshape(momentum.shape),
        amplitudes,
    )


def solution(mesh):
    placed = (
        P(None, None, ("ty", "pos"), "tx"),
        P(None, None, ("ty", "pos"), "tx"),
        P("ty", "tx", "pos", None, None),
        P(),
        P(),
        P("ty", "tx", None, None),
        P("ty", "tx"),
    )
    return jax.shard_map(
        shards,
        mesh=mesh,
        in_specs=placed,
        out_specs=(
            P(None, None, ("ty", "pos"), "tx"),
            P(None, None, ("ty", "pos"), "tx"),
            P("ty", "tx", "pos", None, None),
        ),
        check_vma=False,
    )
```

time: 373 us -> 104 us (0.28)
  matrix products: 110 us -> 0 us
  waiting for transfers between devices: 134 us -> 35.1 us
  local copies, waits for them, and re-layouts: 47.5 us -> 7.41 us
  Pallas kernels: 0 us -> 23.7 us
  loops' own time: 20.1 us -> 0 us
  between operations: 15.7 us -> 1.4 us
  other arithmetic: 11.4 us -> 0.84 us
  starting transfers between devices: 30.2 us -> 34.2 us
    dot_general x72 -> x0, matrix products: 110 us -> none  [matmul(): return jnp.dot(left, right, precision=HIGHEST)]
    all_gather x2 -> x0, waiting for transfers between devices: 63.8 us -> none  [fetch(): full_tile = lax.all_gather(shard, 'pos', axis=1, tiled=True)]
    unnamed x4 -> x0, waiting for transfers between devices: 49 us -> none
    pallas_call x0 -> x8, Pallas kernels: none -> 23.7 us  [call(): pl.pallas_call(body, out_shape=tuple((jax.ShapeDtypeStruct(s, F32) for s...]
    another operation x2 -> x0, loops' own time: 20.1 us -> none  [the longest x1 10.6 us: shards(): lax.fori_loop(zero, last_slot, predict, jnp.zeros((own_measured.shape[0],...]
    slice x14 -> x0, local copies, waits for them, and re-layouts: 17.8 us -> none  [the longest x1 5.54 us: window_gradient(): toward = complex_product(window[2], -window[3], backward[0], backward[1])]
    ppermute x12 -> x17, waiting for transfers between devices: 21.1 us -> 35.1 us  [the longest x9 22.7 us: shards(): send = lambda x, pairs: lax.ppermute(x, ('ty', 'pos'), complete(pairs, n))]
    dynamic_update_slice x1 -> x0, local copies, waits for them, and re-layouts: 11.6 us -> none  [accumulate(): return lax.dynamic_update_slice(gradient, current + term, corner)]
  transfers between devices with their start and end apart: 15 -> 17, of which waited for: 10 -> 11; matrix products, arithmetic and copies ran while one was open for 3% -> 2% of each run, Pallas kernels for 0% -> 5%
where the time goes in v1:
time: 104 us; the launch traced here: 103 us
  waiting for transfers between devices  35.1 us (34%)
  starting transfers between devices  34.2 us (33%)
  Pallas kernels  23.7 us (23%)
  local copies, waits for them, and re-layouts  7.41 us (7%)
  between operations  1.4 us (1%)
    pallas_call x8, Pallas kernels, call(): pl.pallas_call(body, out_shape=tuple((jax.ShapeDtypeStruct(s, F32) for s...  23.7 us
    ppermute x9, waiting for transfers between devices, shards(): send = lambda x, pairs: lax.ppermute(x, ('ty', 'pos'), complete(pairs, n))  22.7 us
    ppermute x9, starting transfers between devices, shards(): send = lambda x, pairs: lax.ppermute(x, ('ty', 'pos'), complete(pairs, n))  20.5 us
    ppermute x2, waiting for transfers between devices, shards(): columns = lambda x: lax.ppermute(x, ('ty', 'tx'), ring)  7.35 us
    ppermute x2, starting transfers between devices, shards(): columns = lambda x: lax.ppermute(x, ('ty', 'tx'), ring)  6.58 us
    unnamed x41, local copies, waits for them, and re-layouts  6.46 us
    ppermute x5, starting transfers between devices, shards(): cores = lambda x: lax.ppermute(x, 'ty', [(0, 1), (1, 0)])  5.82 us
    ppermute x5, waiting for transfers between devices, shards(): cores = lambda x: lax.ppermute(x, 'ty', [(0, 1), (1, 0)])  5.02 us
  transfers between devices with their start and end apart: 17, of which 11 were waited for; matrix products, arithmetic and copies ran while one was open for 2% of the time, Pallas kernels for 5%

profile of v1, /device:TPU:1, one launch (start us, length us, event | category | flops | bytes accessed | tf_op | source)
XLA Modules:
  0.0 102.5 jit_solution(12567082960700960868)
XLA Ops:
  0.7 1.7 %collective-permute-done.prt_ref = f32[4,64,256]{2,1,0:T(8,128)S(1)} collective-permute-done((f32[4,64,256]{2,1,0:T(8,128)}, f32[4,64,256]{2,1,0:T(8,128)S(1)}, u32[]{:S(2)}, u32[]{:S(2)}) %collective-permute-start) | collective-permute-done | bytes 262176 | tf_op jit(solution)/shard_map/ppermute | solution.py:371
  3.2 2.0 %strips.1 = f32[4,64,128]{2,1,0:T(8,128)} custom-call(f32[4,64,256]{2,1,0:T(8,128)} %bitcast.9, f32[4,64,256]{2,1,0:T(8,128)} %copy-done), custom_call_target="tpu_custom_call" | custom-call | tf_op jit(solution)/shard_map/strips/pallas_call | solution.py:28
  5.1 4.4 %collective-permute-start.1 = (f32[4,64,128]{2,1,0:T(8,128)}, f32[4,64,128]{2,1,0:T(8,128)S(1)}, u32[]{:S(2)}, u32[]{:S(2)}) collective-permute-start(f32[4,64,128]{2,1,0:T(8,128)} %strips.1), channel_id=1, source_target_pairs={{0,4},{4,8},{8,12},{12,0},{16,28},{20,16},{24,20},{28,24},{1,5},{5... | collective-permute-start | bytes 393224 | tf_op jit(solution)/shard_map/ppermute | solution.py:373
  9.6 2.5 %collective-permute-done.1.mine_ref = f32[4,64,128]{2,1,0:T(8,128)S(1)} collective-permute-done((f32[4,64,128]{2,1,0:T(8,128)}, f32[4,64,128]{2,1,0:T(8,128)S(1)}, u32[]{:S(2)}, u32[]{:S(2)}) %collective-permute-start.1) | collective-permute-done | bytes 131104 | tf_op jit(solution)/shard_map/ppermute | solution.py:373
  12.1 2.3 %collective-permute-start.2 = (f32[4,64,128]{2,1,0:T(8,128)S(1)}, f32[4,64,128]{2,1,0:T(8,128)S(1)}, u32[]{:S(2)}, u32[]{:S(2)}) collective-permute-start(f32[4,64,128]{2,1,0:T(8,128)S(1)} %collective-permute-done.1.mine_ref), channel_id=1, source_target_pairs={{0,16},{16,0},{1,17},{17,1},{2,18},{18,2},{3,19},{19,3},{4,20},{20... | collective-permute-start | bytes 393224 | tf_op jit(solution)/shard_map/ppermute | solution.py:371
  14.4 1.2 %collective-permute-start.6 = (f32[1,1,1,256,256]{4,3,2,1,0:T(8,128)S(1)}, f32[1,1,1,256,256]{4,3,2,1,0:T(8,128)S(1)}, u32[]{:S(2)}, u32[]{:S(2)}) collective-permute-start(f32[1,1,1,256,256]{4,3,2,1,0:T(8,128)S(1)} %copy-done.3), channel_id=1, source_target_pairs={{0,2},{1,3},{2,0},{3,1},{4,6},{5,7},{6,4},{7,5},{8,10},{9,11},{10,... | collective-permute-start | bytes 786440 | tf_op jit(solution)/shard_map/ppermute | solution.py:376
  17.0 2.5 %probe_move.1.refs_4_ = f32[2,2,256,256]{3,2,1,0:T(8,128)} custom-call(s32[1,1,4,2]{3,2,1,0:T(4,128)} %copy.14.place_ref, f32[2,256,256]{2,1,0:T(8,128)} %light_ref.1), custom_call_target="tpu_custom_call" | custom-call | tf_op jit(solution)/shard_map/probe_move/pallas_call | solution.py:28
  20.1 2.5 %pack.1 = (f32[4,64,256]{2,1,0:T(8,128)}, f32[4,64,256]{2,1,0:T(8,128)}, f32[4,64,256]{2,1,0:T(8,128)}, f32[4,64,256]{2,1,0:T(8,128)}, f32[4,64,128]{2,1,0:T(8,128)}, /*index=5*/f32[4,64,128]{2,1,0:T(8,128)}) custom-call(s32[1,1,4,2]{3,2,1,0:T(4,128)} %copy.14.place_ref, f32[4,64,256]{2,1,0:T(8,128)} %bitcast.10, f32[4,64,256]{2,1,0:T(8,128)} %copy-done, ...), custom_call_target="tpu_custom_call" | custom-call | tf_op jit(solution)/shard_map/pack/pallas_call | solution.py:28
  23.3 2.7 %collective-permute-start.4 = (f32[4,64,256]{2,1,0:T(8,128)}, f32[4,64,256]{2,1,0:T(8,128)S(1)}, u32[]{:S(2)}, u32[]{:S(2)}) collective-permute-start(f32[4,64,256]{2,1,0:T(8,128)} %get-tuple-element.28), channel_id=1, source_target_pairs={{2,0},{3,1},{16,18},{17,19},{0,16},{1,17},{18,2},{19,3},{6,4},{7,5... | collective-permute-start | bytes 786440 | tf_op jit(solution)/shard_map/ppermute | solution.py:374
  26.0 0.9 cosine_bitcast_fusion
  27.0 0.8 pad_maximum_fusion.refs_5_
  27.8 3.5 %collective-permute-done.4.refs_2_ = f32[4,64,256]{2,1,0:T(8,128)S(1)} collective-permute-done((f32[4,64,256]{2,1,0:T(8,128)}, f32[4,64,256]{2,1,0:T(8,128)S(1)}, u32[]{:S(2)}, u32[]{:S(2)}) %collective-permute-start.4) | collective-permute-done | bytes 262176 | tf_op jit(solution)/shard_map/ppermute | solution.py:374
  32.6 3.0 %gradient.1 = (f32[4,64,256]{2,1,0:T(8,128)}, f32[4,64,256]{2,1,0:T(8,128)}, f32[4,64,256]{2,1,0:T(8,128)}, f32[4,64,256]{2,1,0:T(8,128)}) custom-call(s32[1,1]{1,0:T(1,128)S(6)} %copy.15.count_ref, f32[4,64,256]{2,1,0:T(8,128)} %get-tuple-element.26.refs_0_, f32[4,64,256]{2,1,0:T(8,128)} %copy-done.5, f32[4,64,256]{2,1,0:T(8,128)} %copy-done.6, ...), custom_call_target="tpu_custom_call" | custom-call | tf_op jit(solution)/shard_map/gradient/pallas_call | solution.py:28
  36.4 12.4 %collective-permute-start.8 = (f32[4,64,256]{2,1,0:T(8,128)}, f32[4,64,256]{2,1,0:T(8,128)S(1)}, u32[]{:S(2)}, u32[]{:S(2)}) collective-permute-start(f32[4,64,256]{2,1,0:T(8,128)} %get-tuple-element.32), channel_id=1, source_target_pairs={{0,2},{1,3},{18,16},{19,17},{2,18},{3,19},{16,0},{17,1},{4,6},{5,7... | collective-permute-start | bytes 786440 | tf_op jit(solution)/shard_map/ppermute | solution.py:374
  48.8 2.2 %collective-permute-done.8.refs_2_ = f32[4,64,256]{2,1,0:T(8,128)S(1)} collective-permute-done((f32[4,64,256]{2,1,0:T(8,128)}, f32[4,64,256]{2,1,0:T(8,128)S(1)}, u32[]{:S(2)}, u32[]{:S(2)}) %collective-permute-start.8) | collective-permute-done | bytes 262176 | tf_op jit(solution)/shard_map/ppermute | solution.py:374
  51.1 4.0 %collective-permute-done.9.refs_3_ = f32[4,64,256]{2,1,0:T(8,128)S(1)} collective-permute-done((f32[4,64,256]{2,1,0:T(8,128)}, f32[4,64,256]{2,1,0:T(8,128)S(1)}, u32[]{:S(2)}, u32[]{:S(2)}) %collective-permute-start.9) | collective-permute-done | bytes 262176 | tf_op jit(solution)/shard_map/ppermute | solution.py:374
  55.8 2.4 %collect.1 = (f32[2,4,64,256]{3,2,1,0:T(8,128)}, f32[2,4,64,128]{3,2,1,0:T(8,128)}) custom-call(s32[1,1,4,2]{3,2,1,0:T(4,128)} %copy.14.place_ref, s32[1,1]{1,0:T(1,128)S(6)} %copy.15.count_ref, f32[4,64,256]{2,1,0:T(8,128)} %get-tuple-element.30.refs_0_, f32[4,64,256]{2,1,0:T(8,128)} %copy-done.9, f32[4,64,256]{2,1,0:T(8,128)} %copy-done.10, ...), custom_call_target="tpu_custom_call" | custom-call | tf_op jit(solution)/shard_map/collect/pallas_call | solution.py:28
  58.2 0.8 collective-permute-start.10
  59.0 2.1 %collective-permute-done.11.their_halo_ref = f32[2,4,64,128]{3,2,1,0:T(8,128)S(1)} collective-permute-done((f32[2,4,64,128]{3,2,1,0:T(8,128)}, f32[2,4,64,128]{3,2,1,0:T(8,128)S(1)}, u32[]{:S(2)}, u32[]{:S(2)}) %collective-permute-start.11) | collective-permute-done | bytes 262176 | tf_op jit(solution)/shard_map/ppermute | solution.py:371
  61.8 0.8 copy-done.1
  62.6 2.4 %strips_back.1 = (f32[2,4,64,256]{3,2,1,0:T(8,128)}, f32[2,4,64,128]{3,2,1,0:T(8,128)}, f32[2,4,64,128]{3,2,1,0:T(8,128)}) custom-call(f32[2,4,64,256]{3,2,1,0:T(8,128)} %get-tuple-element.34.own_ref, f32[2,4,64,128]{3,2,1,0:T(8,128)} %get-tuple-element.35.halo_ref, f32[2,4,64,256]{3,2,1,0:T(8,128)} %copy-done.1, f32[2,4,64,128]{3,2,1,0:T(8,128)} %copy-done.13), custom_call_target="tpu_custom_call" | custom-call | tf_op jit(solution)/shard_map/strips_back/pallas_call | solution.py:28
  65.0 2.1 %collective-permute-start.12 = (f32[2,4,64,128]{3,2,1,0:T(8,128)}, f32[2,4,64,128]{3,2,1,0:T(8,128)S(1)}, u32[]{:S(2)}, u32[]{:S(2)}) collective-permute-start(f32[2,4,64,128]{3,2,1,0:T(8,128)} %get-tuple-element.38), channel_id=1, source_target_pairs={{0,4},{4,8},{8,12},{12,0},{16,28},{20,16},{24,20},{28,24},{1,5},{5... | collective-permute-start | bytes 786440 | tf_op jit(solution)/shard_map/ppermute | solution.py:373
  67.1 4.9 %collective-permute-done.12.mine_ref = f32[2,4,64,128]{3,2,1,0:T(8,128)S(1)} collective-permute-done((f32[2,4,64,128]{3,2,1,0:T(8,128)}, f32[2,4,64,128]{3,2,1,0:T(8,128)S(1)}, u32[]{:S(2)}, u32[]{:S(2)}) %collective-permute-start.12) | collective-permute-done | bytes 262176 | tf_op jit(solution)/shard_map/ppermute | solution.py:373
  72.0 2.6 %collective-permute-start.13 = (f32[2,4,64,128]{3,2,1,0:T(8,128)S(1)}, f32[2,4,64,128]{3,2,1,0:T(8,128)S(1)}, u32[]{:S(2)}, u32[]{:S(2)}) collective-permute-start(f32[2,4,64,128]{3,2,1,0:T(8,128)S(1)} %collective-permute-done.12.mine_ref), channel_id=1, source_target_pairs={{0,16},{16,0},{1,17},{17,1},{2,18},{18,2},{3,19},{19,3},{4,20},{20... | collective-permute-start | bytes 786440 | tf_op jit(solution)/shard_map/ppermute | solution.py:371
  74.6 1.2 %collective-permute-done.13.theirs_ref = f32[2,4,64,128]{3,2,1,0:T(8,128)S(1)} collective-permute-done((f32[2,4,64,128]{3,2,1,0:T(8,128)S(1)}, f32[2,4,64,128]{3,2,1,0:T(8,128)S(1)}, u32[]{:S(2)}, u32[]{:S(2)}) %collective-permute-start.13) | collective-permute-done | bytes 262176 | tf_op jit(solution)/shard_map/ppermute | solution.py:371
  76.5 3.0 %update.1 = (f32[4,64,256]{2,1,0:T(8,128)}, f32[4,64,256]{2,1,0:T(8,128)}, f32[4,64,256]{2,1,0:T(8,128)}, f32[4,64,256]{2,1,0:T(8,128)}, f32[4,64,256]{2,1,0:T(8...) custom-call(s32[1,1,4,2]{3,2,1,0:T(4,128)} %copy.14.place_ref, ...), custom_call_target="tpu_custom_call" | custom-call | tf_op jit(solution)/shard_map/update/pallas_call | solution.py:28
  79.4 1.4 %collective-permute-start.14 = (f32[4,64,256]{2,1,0:T(8,128)}, f32[4,64,256]{2,1,0:T(8,128)S(1)}, u32[]{:S(2)}, u32[]{:S(2)}) collective-permute-start(f32[4,64,256]{2,1,0:T(8,128)} %get-tuple-element.42), channel_id=1, source_target_pairs={{0,1},{1,0},{16,17},{17,16},{2,18},{3,19},{18,2},{19,3},{4,5},{5,4... | collective-permute-start | bytes 786440 | tf_op jit(solution)/shard_map/ppermute | solution.py:374
  80.9 1.3 %collective-permute-start.15 = (f32[4,64,256]{2,1,0:T(8,128)}, f32[4,64,256]{2,1,0:T(8,128)S(1)}, u32[]{:S(2)}, u32[]{:S(2)}) collective-permute-start(f32[4,64,256]{2,1,0:T(8,128)} %get-tuple-element.43), channel_id=1, source_target_pairs={{2,0},{3,1},{18,16},{19,17},{6,4},{7,5},{22,20},{23,21},{10,8},{11... | collective-permute-start | bytes 786440 | tf_op jit(solution)/shard_map/ppermute | solution.py:374
  82.2 1.3 %collective-permute-start.16 = (f32[4,64,256]{2,1,0:T(8,128)}, f32[4,64,256]{2,1,0:T(8,128)S(1)}, u32[]{:S(2)}, u32[]{:S(2)}) collective-permute-start(f32[4,64,256]{2,1,0:T(8,128)} %get-tuple-element.44), channel_id=1, source_target_pairs={{2,1},{3,0},{18,17},{19,16},{6,5},{7,4},{22,21},{23,20},{10,9},{11... | collective-permute-start | bytes 786440 | tf_op jit(solution)/shard_map/ppermute | solution.py:374
  83.5 3.7 %collective-permute-done.14.refs_1_ = f32[4,64,256]{2,1,0:T(8,128)S(1)} collective-permute-done((f32[4,64,256]{2,1,0:T(8,128)}, f32[4,64,256]{2,1,0:T(8,128)S(1)}, u32[]{:S(2)}, u32[]{:S(2)}) %collective-permute-start.14) | collective-permute-done | bytes 262176 | tf_op jit(solution)/shard_map/ppermute | solution.py:374
  87.2 8.6 %collective-permute-done.15.refs_2_ = f32[4,64,256]{2,1,0:T(8,128)S(1)} collective-permute-done((f32[4,64,256]{2,1,0:T(8,128)}, f32[4,64,256]{2,1,0:T(8,128)S(1)}, u32[]{:S(2)}, u32[]{:S(2)}) %collective-permute-start.15) | collective-permute-done | bytes 262176 | tf_op jit(solution)/shard_map/ppermute | solution.py:374
  96.6 5.9 %predict.1 = f32[1,1,1,256,256]{4,3,2,1,0:T(8,128)} custom-call(s32[1,1]{1,0:T(1,128)S(6)} %copy.15.count_ref, f32[4,64,256]{2,1,0:T(8,128)} %get-tuple-element.41.refs_0_, f32[4,64,256]{2,1,0:T(8,128)} %copy-done.14, f32[4,64,256]{2,1,0:T(8,128)} %copy-done.15, f32[4,64,256]{2,1,0:T(8,128)} %copy-done.16, f32[2,2,256,256]{3,2,1,0:T(8,128)} %probe_move.1.refs_4_, ...), custom_call_target="tpu_custom_call" | custom-call | tf_op jit(solution)/shard_map/predict/pallas_call | solution.py:28
  (53 shorter events, 7.9 us)
Async XLA Ops:
  0.6 13.8 %copy-start.3 = (f32[1,1,1,256,256]{4,3,2,1,0:T(8,128)S(1)}, f32[1,1,1,256,256]{4,3,2,1,0:T(8,128)}, u32[]{:S(2)}) copy-start(f32[1,1,1,256,256]{4,3,2,1,0:T(8,128)} %refs_7_.1) | copy-start | bytes 786436
  0.6 1.8 %collective-permute-start = (f32[4,64,256]{2,1,0:T(8,128)}, f32[4,64,256]{2,1,0:T(8,128)S(1)}, u32[]{:S(2)}, u32[]{:S(2)}) collective-permute-start(f32[4,64,256]{2,1,0:T(8,128)} %bitcast.8), channel_id=1, source_target_pairs={{0,16},{16,0},{1,17},{17,1},{2,18},{18,2},{3,19},{19,3},{4,20},{20... | collective-permute-start | bytes 786440 | tf_op jit(solution)/shard_map/ppermute | solution.py:371
  5.1 11.2 %copy-start.19 = (s32[1,1,4,2]{2,3,1,0:T(2,128)S(1)}, s32[1,1,4,2]{2,3,1,0:T(2,128)}, u32[]{:S(2)}) copy-start(s32[1,1,4,2]{2,3,1,0:T(2,128)} %param.13) | copy-start | bytes 100
  5.1 6.9 %collective-permute-start.1 = (f32[4,64,128]{2,1,0:T(8,128)}, f32[4,64,128]{2,1,0:T(8,128)S(1)}, u32[]{:S(2)}, u32[]{:S(2)}) collective-permute-start(f32[4,64,128]{2,1,0:T(8,128)} %strips.1), channel_id=1, source_target_pairs={{0,4},{4,8},{8,12},{12,0},{16,28},{20,16},{24,20},{28,24},{1,5},{5... | collective-permute-start | bytes 393224 | tf_op jit(solution)/shard_map/ppermute | solution.py:373
  12.1 7.4 %copy-start.17 = (f32[4,64,128]{2,1,0:T(8,128)}, f32[4,64,128]{2,1,0:T(8,128)S(1)}, u32[]{:S(2)}) copy-start(f32[4,64,128]{2,1,0:T(8,128)S(1)} %collective-permute-done.1.mine_ref) | copy-start | bytes 393220
  12.1 7.4 %collective-permute-start.2 = (f32[4,64,128]{2,1,0:T(8,128)S(1)}, f32[4,64,128]{2,1,0:T(8,128)S(1)}, u32[]{:S(2)}, u32[]{:S(2)}) collective-permute-start(f32[4,64,128]{2,1,0:T(8,128)S(1)} %collective-permute-done.1.mine_ref), channel_id=1, source_target_pairs={{0,16},{16,0},{1,17},{17,1},{2,18},{18,2},{3,19},{19,3},{4,20},{20... | collective-permute-start | bytes 393224 | tf_op jit(solution)/shard_map/ppermute | solution.py:371
  14.4 13.4 %collective-permute-start.6 = (f32[1,1,1,256,256]{4,3,2,1,0:T(8,128)S(1)}, f32[1,1,1,256,256]{4,3,2,1,0:T(8,128)S(1)}, u32[]{:S(2)}, u32[]{:S(2)}) collective-permute-start(f32[1,1,1,256,256]{4,3,2,1,0:T(8,128)S(1)} %copy-done.3), channel_id=1, source_target_pairs={{0,2},{1,3},{2,0},{3,1},{4,6},{5,7},{6,4},{7,5},{8,10},{9,11},{10,... | collective-permute-start | bytes 786440 | tf_op jit(solution)/shard_map/ppermute | solution.py:376
  19.5 6.5 %copy-start.2 = (f32[256,256]{1,0:T(8,128)S(1)}, f32[256,256]{1,0:T(8,128)}, u32[]{:S(2)}) copy-start(f32[256,256]{1,0:T(8,128)} %param.12) | copy-start | bytes 786436
  22.6 5.2 %collective-permute-start.3 = (f32[4,64,256]{2,1,0:T(8,128)}, f32[4,64,256]{2,1,0:T(8,128)S(1)}, u32[]{:S(2)}, u32[]{:S(2)}) collective-permute-start(f32[4,64,256]{2,1,0:T(8,128)} %get-tuple-element.27), channel_id=1, source_target_pairs={{0,1},{1,0},{18,19},{19,18},{4,5},{5,4},{22,23},{23,22},{8,9},{9,8... | collective-permute-start | bytes 786440 | tf_op jit(solution)/shard_map/ppermute | solution.py:374
  23.3 8.0 %collective-permute-start.4 = (f32[4,64,256]{2,1,0:T(8,128)}, f32[4,64,256]{2,1,0:T(8,128)S(1)}, u32[]{:S(2)}, u32[]{:S(2)}) collective-permute-start(f32[4,64,256]{2,1,0:T(8,128)} %get-tuple-element.28), channel_id=1, source_target_pairs={{2,0},{3,1},{16,18},{17,19},{0,16},{1,17},{18,2},{19,3},{6,4},{7,5... | collective-permute-start | bytes 786440 | tf_op jit(solution)/shard_map/ppermute | solution.py:374
  26.0 6.0 %collective-permute-start.5 = (f32[4,64,256]{2,1,0:T(8,128)}, f32[4,64,256]{2,1,0:T(8,128)S(1)}, u32[]{:S(2)}, u32[]{:S(2)}) collective-permute-start(f32[4,64,256]{2,1,0:T(8,128)} %get-tuple-element.29), channel_id=1, source_target_pairs={{2,1},{3,0},{16,19},{17,18},{0,16},{1,17},{18,2},{19,3},{6,5},{7,4... | collective-permute-start | bytes 786440 | tf_op jit(solution)/shard_map/ppermute | solution.py:374
  27.8 4.1 %copy-start.4 = (f32[1,1,1,256,256]{4,3,2,1,0:T(8,128)}, f32[1,1,1,256,256]{4,3,2,1,0:T(8,128)S(1)}, u32[]{:S(2)}) copy-start(f32[1,1,1,256,256]{4,3,2,1,0:T(8,128)S(1)} %collective-permute-done.6.refs_8_) | copy-start | bytes 786436
  27.8 4.1 %copy-start.5 = (f32[4,64,256]{2,1,0:T(8,128)}, f32[4,64,256]{2,1,0:T(8,128)S(1)}, u32[]{:S(2)}) copy-start(f32[4,64,256]{2,1,0:T(8,128)S(1)} %collective-permute-done.3.refs_1_) | copy-start | bytes 786436
  31.9 0.7 copy-start.7
  35.7 13.1 %collective-permute-start.7 = (f32[4,64,256]{2,1,0:T(8,128)}, f32[4,64,256]{2,1,0:T(8,128)S(1)}, u32[]{:S(2)}, u32[]{:S(2)}) collective-permute-start(f32[4,64,256]{2,1,0:T(8,128)} %get-tuple-element.31), channel_id=1, source_target_pairs={{1,0},{0,1},{19,18},{18,19},{5,4},{4,5},{23,22},{22,23},{9,8},{8,9... | collective-permute-start | bytes 786440 | tf_op jit(solution)/shard_map/ppermute | solution.py:374
  36.4 14.7 %collective-permute-start.8 = (f32[4,64,256]{2,1,0:T(8,128)}, f32[4,64,256]{2,1,0:T(8,128)S(1)}, u32[]{:S(2)}, u32[]{:S(2)}) collective-permute-start(f32[4,64,256]{2,1,0:T(8,128)} %get-tuple-element.32), channel_id=1, source_target_pairs={{0,2},{1,3},{18,16},{19,17},{2,18},{3,19},{16,0},{17,1},{4,6},{5,7... | collective-permute-start | bytes 786440 | tf_op jit(solution)/shard_map/ppermute | solution.py:374
  48.8 6.3 %collective-permute-start.9 = (f32[4,64,256]{2,1,0:T(8,128)}, f32[4,64,256]{2,1,0:T(8,128)S(1)}, u32[]{:S(2)}, u32[]{:S(2)}) collective-permute-start(f32[4,64,256]{2,1,0:T(8,128)} %get-tuple-element.33), channel_id=1, source_target_pairs={{1,2},{0,3},{19,16},{18,17},{2,18},{3,19},{16,0},{17,1},{5,6},{4,7... | collective-permute-start | bytes 786440 | tf_op jit(solution)/shard_map/ppermute | solution.py:374
  48.8 6.3 %copy-start.9 = (f32[4,64,256]{2,1,0:T(8,128)}, f32[4,64,256]{2,1,0:T(8,128)S(1)}, u32[]{:S(2)}) copy-start(f32[4,64,256]{2,1,0:T(8,128)S(1)} %collective-permute-done.7.refs_1_) | copy-start | bytes 786436
  51.1 4.0 %copy-start.10 = (f32[4,64,256]{2,1,0:T(8,128)}, f32[4,64,256]{2,1,0:T(8,128)S(1)}, u32[]{:S(2)}) copy-start(f32[4,64,256]{2,1,0:T(8,128)S(1)} %collective-permute-done.8.refs_2_) | copy-start | bytes 786436
  55.1 0.7 copy-start.12
  58.2 2.9 %collective-permute-start.10 = (f32[2,4,64,256]{3,2,1,0:T(8,128)}, f32[2,4,64,256]{3,2,1,0:T(8,128)S(1)}, u32[]{:S(2)}, u32[]{:S(2)}) collective-permute-start(f32[2,4,64,256]{3,2,1,0:T(8,128)} %get-tuple-element.34.own_ref), channel_id=1, source_target_pairs={{0,16},{16,0},{1,17},{17,1},{2,18},{18,2},{3,19},{19,3},{4,20},{20... | collective-permute-start | bytes 1572872 | tf_op jit(solution)/shard_map/ppermute | solution.py:371
  59.0 2.1 %collective-permute-start.11 = (f32[2,4,64,128]{3,2,1,0:T(8,128)}, f32[2,4,64,128]{3,2,1,0:T(8,128)S(1)}, u32[]{:S(2)}, u32[]{:S(2)}) collective-permute-start(f32[2,4,64,128]{3,2,1,0:T(8,128)} %get-tuple-element.35.halo_ref), channel_id=1, source_target_pairs={{0,16},{16,0},{1,17},{17,1},{2,18},{18,2},{3,19},{19,3},{4,20},{20... | collective-permute-start | bytes 786440 | tf_op jit(solution)/shard_map/ppermute | solution.py:371
  61.8 0.8 copy-start.1
  65.0 7.0 %collective-permute-start.12 = (f32[2,4,64,128]{3,2,1,0:T(8,128)}, f32[2,4,64,128]{3,2,1,0:T(8,128)S(1)}, u32[]{:S(2)}, u32[]{:S(2)}) collective-permute-start(f32[2,4,64,128]{3,2,1,0:T(8,128)} %get-tuple-element.38), channel_id=1, source_target_pairs={{0,4},{4,8},{8,12},{12,0},{16,28},{20,16},{24,20},{28,24},{1,5},{5... | collective-permute-start | bytes 786440 | tf_op jit(solution)/shard_map/ppermute | solution.py:373
  72.0 3.8 %copy-start.8 = (f32[2,4,64,128]{3,2,1,0:T(8,128)}, f32[2,4,64,128]{3,2,1,0:T(8,128)S(1)}, u32[]{:S(2)}) copy-start(f32[2,4,64,128]{3,2,1,0:T(8,128)S(1)} %collective-permute-done.12.mine_ref) | copy-start | bytes 786436
  72.0 3.8 %collective-permute-start.13 = (f32[2,4,64,128]{3,2,1,0:T(8,128)S(1)}, f32[2,4,64,128]{3,2,1,0:T(8,128)S(1)}, u32[]{:S(2)}, u32[]{:S(2)}) collective-permute-start(f32[2,4,64,128]{3,2,1,0:T(8,128)S(1)} %collective-permute-done.12.mine_ref), channel_id=1, source_target_pairs={{0,16},{16,0},{1,17},{17,1},{2,18},{18,2},{3,19},{19,3},{4,20},{20... | collective-permute-start | bytes 786440 | tf_op jit(solution)/shard_map/ppermute | solution.py:371
  79.4 7.7 %collective-permute-start.14 = (f32[4,64,256]{2,1,0:T(8,128)}, f32[4,64,256]{2,1,0:T(8,128)S(1)}, u32[]{:S(2)}, u32[]{:S(2)}) collective-permute-start(f32[4,64,256]{2,1,0:T(8,128)} %get-tuple-element.42), channel_id=1, source_target_pairs={{0,1},{1,0},{16,17},{17,16},{2,18},{3,19},{18,2},{19,3},{4,5},{5,4... | collective-permute-start | bytes 786440 | tf_op jit(solution)/shard_map/ppermute | solution.py:374
  80.9 14.9 %collective-permute-start.15 = (f32[4,64,256]{2,1,0:T(8,128)}, f32[4,64,256]{2,1,0:T(8,128)S(1)}, u32[]{:S(2)}, u32[]{:S(2)}) collective-permute-start(f32[4,64,256]{2,1,0:T(8,128)} %get-tuple-element.43), channel_id=1, source_target_pairs={{2,0},{3,1},{18,16},{19,17},{6,4},{7,5},{22,20},{23,21},{10,8},{11... | collective-permute-start | bytes 786440 | tf_op jit(solution)/shard_map/ppermute | solution.py:374
  82.2 13.6 %collective-permute-start.16 = (f32[4,64,256]{2,1,0:T(8,128)}, f32[4,64,256]{2,1,0:T(8,128)S(1)}, u32[]{:S(2)}, u32[]{:S(2)}) collective-permute-start(f32[4,64,256]{2,1,0:T(8,128)} %get-tuple-element.44), channel_id=1, source_target_pairs={{2,1},{3,0},{18,17},{19,16},{6,5},{7,4},{22,21},{23,20},{10,9},{11... | collective-permute-start | bytes 786440 | tf_op jit(solution)/shard_map/ppermute | solution.py:374
  87.2 8.6 %copy-start.14 = (f32[4,64,256]{2,1,0:T(8,128)}, f32[4,64,256]{2,1,0:T(8,128)S(1)}, u32[]{:S(2)}) copy-start(f32[4,64,256]{2,1,0:T(8,128)S(1)} %collective-permute-done.14.refs_1_) | copy-start | bytes 786436
  95.8 0.7 copy-start.15
  95.8 0.8 copy-start.16
  (5 other events, 3.4 us)

commit v2 on v1

--- a/solution.py
+++ b/solution.py
@@ -8,6 +8,7 @@
 from jax.experimental.pallas import tpu as pltpu
 from jax.sharding import PartitionSpec as P
 
+
 magnitude_floor = 0.5
 momentum_rate = 0.9
 step_length = 0.05
@@ -23,17 +24,17 @@
     return pl.BlockSpec(memory_space=pltpu.SMEM)
 
 
-def call(body, outs, args, scalars=0, scratch=(), name=None):
+def call(body, outs, args, scalars=0, scratch=(), limit=8, last=False):
     specs = [smem()] * scalars + [vmem()] * (len(args) - scalars)
+    placed = [pltpu.with_memory_space_constraint(x, pltpu.VMEM) for x in args[scalars:]]
     return pl.pallas_call(
         body,
-        out_shape=tuple(jax.ShapeDtypeStruct(s, F32) for s in outs),
+        out_shape=tuple((jax.ShapeDtypeStruct if last else pltpu.VMEM)(s, F32) for s in outs),
         in_specs=specs,
         out_specs=tuple(vmem() for _ in outs),
         scratch_shapes=list(scratch),
-        name=name,
-        compiler_params=pltpu.CompilerParams(vmem_limit_bytes=56 * 1024 * 1024),
-    )(*args)
+        compiler_params=pltpu.CompilerParams(vmem_limit_bytes=limit * 1024 * 1024),
+    )(*args[:scalars], *placed)
 
 
 def split_table(values):
@@ -124,8 +125,8 @@
 def masks(place_ref, k, a, p, lay):
     h, t, m = lay.h, lay.t, lay.m
     k = jnp.clip(k, 0, lay.slots - 1)
-    top = place_ref[0, 0, k, 0] - m
-    left = place_ref[0, 0, k, 1] - m
+    top = place_ref[0, 0, 0, k] - m
+    left = place_ref[0, 0, 1, k] - m
     rows = iota((h, t), 0) + p * h
     cols = iota((h, t), 1)
     above = rows >= top + t
@@ -195,12 +196,14 @@
 
 
 def kernel_probe(lay):
-    def body(place_ref, light_ref, out_ref):
+    def body(place_ref, light_ref, phase_ref, out_ref, slab_ref):
         a, _, p = where_am_i()
+        slab_ref[0] = jnp.cos(phase_ref[...])
+        slab_ref[1] = jnp.sin(phase_ref[...])
         for i, home in enumerate((False, True)):
             k = jnp.clip(lay.window_of(p, a, home), 0, lay.slots - 1)
-            down = (place_ref[0, 0, k, 0] + (lay.t - lay.m)) % lay.t
-            along = (place_ref[0, 0, k, 1] + (lay.t - lay.m)) % lay.t
+            down = (place_ref[0, 0, 0, k] + (lay.t - lay.m)) % lay.t
+            along = (place_ref[0, 0, 1, k] + (lay.t - lay.m)) % lay.t
             for c in range(2):
                 out_ref[i, c] = pltpu.roll(pltpu.roll(light_ref[c], down, 0), along, 1)
 
@@ -313,7 +316,7 @@
 
 
 def kernel_update(lay):
-    t, m = lay.t, lay.m
+    m = lay.m
 
     def body(place_ref, obj_ref, prt_ref, obj_halo_ref, prt_halo_ref, sum_ref, halo_sum_ref, mine_ref, theirs_ref, *outs):
         n = lay.n
@@ -362,34 +365,37 @@
     return body
 
 
-def shards(object_field, momentum, measured, illumination, slab_phase, offsets, entry_counts):
+def iteration(object_field, momentum, measured, illumination, slab_phase, offsets, entry_counts):
     lay = Layout(object_field, illumination, offsets)
     n, h, t, m = lay.n, lay.h, lay.t, lay.m
     own = object_field.reshape(4, h, t)
+    offsets = offsets.transpose(0, 1, 3, 2)
     velocity_old = momentum.reshape(4, h, t)
     block, halo_shape = (4, h, t), (4, h, 2 * m)
     cores = lambda x: lax.ppermute(x, "ty", [(0, 1), (1, 0)])
-    ring = [((a * lay.ntx + b), a * lay.ntx + (b + 1 - 2 * a) % lay.ntx) for a in range(2) for b in range(lay.ntx)]
-    columns = lambda x: lax.ppermute(x, ("ty", "tx"), ring)
-    send = lambda x, pairs: lax.ppermute(x, ("ty", "pos"), complete(pairs, n))
+    ntx = lay.ntx
+    shift = [(b, b + 1) for b in range(ntx - 1)] + [(ntx - 1, 2 * ntx - 1)]
+    shift += [(ntx + b + 1, ntx + b) for b in range(ntx - 1)] + [(ntx, 0)]
+    columns = lambda x: lax.ppermute(x, ("ty", "tx"), shift)
+
+    def exchange(values, pairs_of):
+        got = {0: values[0]}
+        for s in [*range(lay.half, n), *range(1, lay.half)]:
+            got[s] = lax.ppermute(values[s], ("ty", "pos"), complete(pairs_of(s), n))
+        return [got[s] for s in range(n)]
 
     moved = lax.ppermute(measured, "pos", [(p, p ^ lay.half) for p in range(n)])
     tab = jnp.asarray(dft_tables(t))
-    slab = jnp.stack([jnp.cos(slab_phase), jnp.sin(slab_phase)])
-    (light,) = call(kernel_probe(lay), [(2, 2, t, t)], [offsets, illumination], 1, name="probe_move")
+    light, slab = call(kernel_probe(lay), [(2, 2, t, t), (2, t, t)], [offsets, illumination, slab_phase], 1)
 
     partner = cores(own)
-    (strips,) = call(kernel_strips(lay), [halo_shape], [own, partner], name="strips")
+    (strips,) = call(kernel_strips(lay), [halo_shape], [own, partner])
     strips = columns(strips)
     strips_other = cores(strips)
     *blocks, own_halo, partner_halo = call(
-        kernel_pack(lay),
-        [block] * n + [halo_shape] * 2,
-        [offsets, own, partner, strips, strips_other],
-        1,
-        name="pack",
-    )
-    received = [blocks[0]] + [send(blocks[s], lay.inward(s, False)) for s in range(1, n)]
+        kernel_pack(lay), [block] * n + [halo_shape] * 2, [offsets, own, partner, strips, strips_other], 1
+    )
+    received = exchange(blocks, lambda s: lay.inward(s, False))
     window = pltpu.VMEM((4, t, t), F32)
     terms = call(
         kernel_gradient(lay),
@@ -397,21 +403,16 @@
         [entry_counts, *received, light, slab, tab, measured, moved],
         1,
         [window],
-        name="gradient",
-    )
-    parts = [terms[0]] + [send(terms[s], lay.outward(s)) for s in range(1, n)]
+        limit=24,
+    )
+    parts = exchange(terms, lay.outward)
     sums, halos = call(
-        kernel_collect(lay),
-        [(2, *block), (2, *halo_shape)],
-        [offsets, entry_counts, *parts, velocity_old],
-        2,
-        name="collect",
+        kernel_collect(lay), [(2, *block), (2, *halo_shape)], [offsets, entry_counts, *parts, velocity_old], 2
     )
     sums, halos, strips = call(
         kernel_strips_back(lay),
         [(2, *block), (2, *halo_shape), (2, *halo_shape)],
         [sums, halos, cores(sums), cores(halos)],
-        name="strips_back",
     )
     strips = columns(strips)
     updated, velocity, *rest = call(
@@ -419,17 +420,17 @@
         [block] * (n + 3) + [halo_shape] * 2,
         [offsets, own, partner, own_halo, partner_halo, sums, halos, strips, cores(strips)],
         1,
-        name="update",
     )
     blocks = rest[:n]
-    received = [blocks[0]] + [send(blocks[s], lay.inward(s, True)) for s in range(1, n)]
+    received = exchange(blocks, lambda s: lay.inward(s, True))
     (amplitudes,) = call(
         kernel_predict(lay),
         [measured.shape],
         [entry_counts, *received, light, slab, tab],
         1,
         [window],
-        name="predict",
+        limit=24,
+        last=True,
     )
     return (
         updated.reshape(object_field.shape),
@@ -449,7 +450,7 @@
         P("ty", "tx"),
     )
     return jax.shard_map(
-        shards,
+        iteration,
         mesh=mesh,
         in_specs=placed,
         out_specs=(

time: 104 us -> 74.4 us (0.72)
  the two profiles are of different devices: /device:TPU:1 before, /device:TPU:0 now
where the time goes in v2:
time: 74.4 us; the launch traced here: 74.1 us
  waiting for transfers between devices  33.5 us (45%)
  starting transfers between devices  19.9 us (27%)
  Pallas kernels  17 us (23%)
  local copies, waits for them, and re-layouts  2.38 us (3%)
  between operations  1.43 us (2%)
    ppermute x9, waiting for transfers between devices, exchange(): got[s] = lax.ppermute(values[s], ('ty', 'pos'), complete(pairs_of(s), n))  22.3 us
    pallas_call x8, Pallas kernels, call(): pl.pallas_call(body, out_shape=tuple(((jax.ShapeDtypeStruct if last else...  17 us
    ppermute x9, starting transfers between devices, exchange(): got[s] = lax.ppermute(values[s], ('ty', 'pos'), complete(pairs_of(s), n))  11.7 us
    ppermute x2, waiting for transfers between devices, iteration(): columns = lambda x: lax.ppermute(x, ('ty', 'tx'), shift)  6.41 us
    ppermute x2, starting transfers between devices, iteration(): columns = lambda x: lax.ppermute(x, ('ty', 'tx'), shift)  5.42 us
    ppermute x5, waiting for transfers between devices, iteration(): cores = lambda x: lax.ppermute(x, 'ty', [(0, 1), (1, 0)])  4.73 us
    unnamed x18, local copies, waits for them, and re-layouts  2.38 us
    ppermute x1, starting transfers between devices, iteration(): moved = lax.ppermute(measured, 'pos', [(p, p ^ lay.half) for p in range(n)])  1.52 us
  transfers between devices with their start and end apart: 17, of which 11 were waited for; matrix products, arithmetic and copies ran while one was open for 2% of the time, Pallas kernels for 5%

profile of v2, /device:TPU:0, one launch (start us, length us, event | category | flops | bytes accessed | tf_op | source)
XLA Modules:
  0.0 74.1 jit_solution(17530225516034360775)
XLA Ops:
  0.6 0.6 collective-permute-start
  1.2 1.4 %collective-permute-done.prt_ref = f32[4,64,256]{2,1,0:T(8,128)S(1)} collective-permute-done((f32[4,64,256]{2,1,0:T(8,128)}, f32[4,64,256]{2,1,0:T(8,128)S(1)}, u32[]{:S(2)}, u32[]{:S(2)}) %collective-permute-start) | collective-permute-done | bytes 262176 | tf_op jit(solution)/shard_map/ppermute | solution.py:375
  2.6 0.9 %copy-done.1 = f32[2,2,64,256]{3,2,1,0:T(8,128)S(1)} copy-done((f32[2,2,64,256]{3,2,1,0:T(8,128)S(1)}, f32[2,2,64,256]{3,2,1,0:T(8,128)}, u32[]{:S(2)}) %copy-start.1) | copy-done | bytes 262168
  3.8 2.9 %collective-permute-start.1 = (f32[4,64,128]{2,1,0:T(8,128)S(1)}, f32[4,64,128]{2,1,0:T(8,128)S(1)}, u32[]{:S(2)}, u32[]{:S(2)}) collective-permute-start(f32[4,64,128]{2,1,0:T(8,128)S(1)} %shard_map.103), channel_id=1, source_target_pairs={{0,4},{4,8},{8,12},{12,28},{20,16},{24,20},{28,24},{16,0},{1,5},{5... | collective-permute-start | bytes 393224 | tf_op jit(solution)/shard_map/ppermute | solution.py:379
  6.8 2.5 %collective-permute-done.1.mine_ref = f32[4,64,128]{2,1,0:T(8,128)S(1)} collective-permute-done((f32[4,64,128]{2,1,0:T(8,128)S(1)}, f32[4,64,128]{2,1,0:T(8,128)S(1)}, u32[]{:S(2)}, u32[]{:S(2)}) %collective-permute-start.1) | collective-permute-done | bytes 131104 | tf_op jit(solution)/shard_map/ppermute | solution.py:379
  9.3 1.5 %collective-permute-start.6 = (f32[1,1,1,256,256]{4,3,2,1,0:T(8,128)S(1)}, f32[1,1,1,256,256]{4,3,2,1,0:T(8,128)S(1)}, u32[]{:S(2)}, u32[]{:S(2)}) collective-permute-start(f32[1,1,1,256,256]{4,3,2,1,0:T(8,128)S(1)} %copy-done.4), channel_id=1, source_target_pairs={{0,2},{1,3},{2,0},{3,1},{4,6},{5,7},{6,4},{7,5},{8,10},{9,11},{10,... | collective-permute-start | bytes 786440 | tf_op jit(solution)/shard_map/ppermute | solution.py:387
  10.8 0.9 %shard_map.104 = (f32[4,64,256]{2,1,0:T(8,128)S(1)}, f32[4,64,256]{2,1,0:T(8,128)S(1)}, f32[4,64,256]{2,1,0:T(8,128)S(1)}, f32[4,64,256]{2,1,0:T(8,128)S(1)}, f3...) custom-call(s32[1,1,2,4]{3,2,1,0:T(2,128)S(1)} %bitcast.12, f32[4,64,256]{2,1,0:T(8,128)S(1)} %bitcast.9, ...), custom_call_target="tpu_custom_call" | custom-call | tf_op jit(solution)/shard_map/pallas_call | solution.py:30
  11.7 3.4 %collective-permute-start.3 = (f32[4,64,256]{2,1,0:T(8,128)S(1)}, f32[4,64,256]{2,1,0:T(8,128)S(1)}, u32[]{:S(2)}, u32[]{:S(2)}) collective-permute-start(f32[4,64,256]{2,1,0:T(8,128)S(1)} %get-tuple-element.29), channel_id=1, source_target_pairs={{0,1},{1,0},{18,19},{19,18},{4,5},{5,4},{22,23},{23,22},{8,9},{9,8... | collective-permute-start | bytes 786440 | tf_op jit(solution)/shard_map/ppermute | solution.py:384
  15.2 0.9 %collective-permute-start.5 = (f32[4,64,256]{2,1,0:T(8,128)S(1)}, f32[4,64,256]{2,1,0:T(8,128)S(1)}, u32[]{:S(2)}, u32[]{:S(2)}) collective-permute-start(f32[4,64,256]{2,1,0:T(8,128)S(1)} %get-tuple-element.31), channel_id=1, source_target_pairs={{2,1},{3,0},{16,19},{17,18},{0,16},{1,17},{18,2},{19,3},{6,5},{7,4... | collective-permute-start | bytes 786440 | tf_op jit(solution)/shard_map/ppermute | solution.py:384
  16.7 2.6 %shard_map.105 = (f32[2,2,256,256]{3,2,1,0:T(8,128)S(1)}, f32[2,256,256]{2,1,0:T(8,128)S(1)}) custom-call(s32[1,1,2,4]{3,2,1,0:T(2,128)S(1)} %bitcast.13, f32[2,256,256]{2,1,0:T(8,128)S(1)} %copy-done.3, f32[256,256]{1,0:T(8,128)S(1)} %copy-done.5), custom_call_target="tpu_custom_call" | custom-call | tf_op jit(solution)/shard_map/pallas_call | solution.py:30
  19.3 2.2 %collective-permute-done.3.refs_1_ = f32[4,64,256]{2,1,0:T(8,128)S(1)} collective-permute-done((f32[4,64,256]{2,1,0:T(8,128)S(1)}, f32[4,64,256]{2,1,0:T(8,128)S(1)}, u32[]{:S(2)}, u32[]{:S(2)}) %collective-permute-start.3) | collective-permute-done | bytes 262176 | tf_op jit(solution)/shard_map/ppermute | solution.py:384
  21.5 2.8 %collective-permute-done.4.refs_2_ = f32[4,64,256]{2,1,0:T(8,128)S(1)} collective-permute-done((f32[4,64,256]{2,1,0:T(8,128)S(1)}, f32[4,64,256]{2,1,0:T(8,128)S(1)}, u32[]{:S(2)}, u32[]{:S(2)}) %collective-permute-start.4) | collective-permute-done | bytes 262176 | tf_op jit(solution)/shard_map/ppermute | solution.py:384
  24.3 6.7 %shard_map.106 = (f32[4,64,256]{2,1,0:T(8,128)S(1)}, f32[4,64,256]{2,1,0:T(8,128)S(1)}, f32[4,64,256]{2,1,0:T(8,128)S(1)}, f32[4,64,256]{2,1,0:T(8,128)S(1)}) custom-call(s32[1,1]{1,0:T(1,128)S(6)} %copy.13.count_ref, f32[4,64,256]{2,1,0:T(8,128)S(1)} %get-tuple-element.28.refs_0_, f32[4,64,256]{2,1,0:T(8,128)S(1)} %collective-permute-done.3.refs_1_, ...), custom_call_target="tpu_custom_call" | custom-call | tf_op jit(solution)/shard_map/pallas_call | solution.py:30
  31.0 2.7 %collective-permute-start.7 = (f32[4,64,256]{2,1,0:T(8,128)S(1)}, f32[4,64,256]{2,1,0:T(8,128)S(1)}, u32[]{:S(2)}, u32[]{:S(2)}) collective-permute-start(f32[4,64,256]{2,1,0:T(8,128)S(1)} %get-tuple-element.35), channel_id=1, source_target_pairs={{1,0},{0,1},{19,18},{18,19},{5,4},{4,5},{23,22},{22,23},{9,8},{8,9... | collective-permute-start | bytes 786440 | tf_op jit(solution)/shard_map/ppermute | solution.py:384
  33.8 1.0 %collective-permute-start.9 = (f32[4,64,256]{2,1,0:T(8,128)S(1)}, f32[4,64,256]{2,1,0:T(8,128)S(1)}, u32[]{:S(2)}, u32[]{:S(2)}) collective-permute-start(f32[4,64,256]{2,1,0:T(8,128)S(1)} %get-tuple-element.37), channel_id=1, source_target_pairs={{1,2},{0,3},{19,16},{18,17},{2,18},{3,19},{16,0},{17,1},{5,6},{4,7... | collective-permute-start | bytes 786440 | tf_op jit(solution)/shard_map/ppermute | solution.py:384
  34.9 4.5 %collective-permute-done.7.refs_1_ = f32[4,64,256]{2,1,0:T(8,128)S(1)} collective-permute-done((f32[4,64,256]{2,1,0:T(8,128)S(1)}, f32[4,64,256]{2,1,0:T(8,128)S(1)}, u32[]{:S(2)}, u32[]{:S(2)}) %collective-permute-start.7) | collective-permute-done | bytes 262176 | tf_op jit(solution)/shard_map/ppermute | solution.py:384
  39.3 1.2 %collective-permute-done.9.refs_3_ = f32[4,64,256]{2,1,0:T(8,128)S(1)} collective-permute-done((f32[4,64,256]{2,1,0:T(8,128)S(1)}, f32[4,64,256]{2,1,0:T(8,128)S(1)}, u32[]{:S(2)}, u32[]{:S(2)}) %collective-permute-start.9) | collective-permute-done | bytes 262176 | tf_op jit(solution)/shard_map/ppermute | solution.py:384
  40.5 0.9 %shard_map.107 = (f32[2,4,64,256]{3,2,1,0:T(8,128)S(1)}, f32[2,4,64,128]{3,2,1,0:T(8,128)S(1)}) custom-call(s32[1,1,2,4]{3,2,1,0:T(2,128)S(1)} %bitcast.14, s32[1,1]{1,0:T(1,128)S(6)} %copy.13.count_ref, f32[4,64,256]{2,1,0:T(8,128)S(1)} %get-tuple-element.34.refs_0_, f32[4,64,256]{2,1,0:T(8,128)S(1)} %collective-permute-done.7.refs_1_, ...), custom_call_target="tpu_custom_call" | custom-call | tf_op jit(solution)/shard_map/pallas_call | solution.py:30
  41.4 0.6 collective-permute-start.10
  42.0 1.8 %collective-permute-done.11.their_halo_ref = f32[2,4,64,128]{3,2,1,0:T(8,128)S(1)} collective-permute-done((f32[2,4,64,128]{3,2,1,0:T(8,128)S(1)}, f32[2,4,64,128]{3,2,1,0:T(8,128)S(1)}, u32[]{:S(2)}, u32[]{:S(2)}) %collective-permute-start.11) | collective-permute-done | bytes 262176 | tf_op jit(solution)/shard_map/ppermute | solution.py:375
  44.0 2.5 %collective-permute-start.12 = (f32[2,4,64,128]{3,2,1,0:T(8,128)S(1)}, f32[2,4,64,128]{3,2,1,0:T(8,128)S(1)}, u32[]{:S(2)}, u32[]{:S(2)}) collective-permute-start(f32[2,4,64,128]{3,2,1,0:T(8,128)S(1)} %get-tuple-element.42), channel_id=1, source_target_pairs={{0,4},{4,8},{8,12},{12,28},{20,16},{24,20},{28,24},{16,0},{1,5},{5... | collective-permute-start | bytes 786440 | tf_op jit(solution)/shard_map/ppermute | solution.py:379
  46.4 3.9 %collective-permute-done.12.mine_ref = f32[2,4,64,128]{3,2,1,0:T(8,128)S(1)} collective-permute-done((f32[2,4,64,128]{3,2,1,0:T(8,128)S(1)}, f32[2,4,64,128]{3,2,1,0:T(8,128)S(1)}, u32[]{:S(2)}, u32[]{:S(2)}) %collective-permute-start.12) | collective-permute-done | bytes 262176 | tf_op jit(solution)/shard_map/ppermute | solution.py:379
  50.3 1.5 %collective-permute-done.13.theirs_ref = f32[2,4,64,128]{3,2,1,0:T(8,128)S(1)} collective-permute-done((f32[2,4,64,128]{3,2,1,0:T(8,128)S(1)}, f32[2,4,64,128]{3,2,1,0:T(8,128)S(1)}, u32[]{:S(2)}, u32[]{:S(2)}) %collective-permute-start.13) | collective-permute-done | bytes 262176 | tf_op jit(solution)/shard_map/ppermute | solution.py:375
  51.9 1.5 %shard_map.109 = (f32[4,64,256]{2,1,0:T(8,128)S(1)}, f32[4,64,256]{2,1,0:T(8,128)S(1)}, f32[4,64,256]{2,1,0:T(8,128)S(1)}, f32[4,64,256]{2,1,0:T(8,128)S(1)}, f3...) custom-call(s32[1,1,2,4]{3,2,1,0:T(2,128)S(1)} %bitcast.15, ...), custom_call_target="tpu_custom_call" | custom-call | tf_op jit(solution)/shard_map/pallas_call | solution.py:30
  53.4 1.0 %collective-permute-start.14 = (f32[4,64,256]{2,1,0:T(8,128)S(1)}, f32[4,64,256]{2,1,0:T(8,128)S(1)}, u32[]{:S(2)}, u32[]{:S(2)}) collective-permute-start(f32[4,64,256]{2,1,0:T(8,128)S(1)} %get-tuple-element.46), channel_id=1, source_target_pairs={{0,1},{1,0},{16,17},{17,16},{2,18},{3,19},{18,2},{19,3},{4,5},{5,4... | collective-permute-start | bytes 786440 | tf_op jit(solution)/shard_map/ppermute | solution.py:384
  54.4 1.3 %collective-permute-start.15 = (f32[4,64,256]{2,1,0:T(8,128)S(1)}, f32[4,64,256]{2,1,0:T(8,128)S(1)}, u32[]{:S(2)}, u32[]{:S(2)}) collective-permute-start(f32[4,64,256]{2,1,0:T(8,128)S(1)} %get-tuple-element.47), channel_id=1, source_target_pairs={{2,0},{3,1},{18,16},{19,17},{6,4},{7,5},{22,20},{23,21},{10,8},{11... | collective-permute-start | bytes 786440 | tf_op jit(solution)/shard_map/ppermute | solution.py:384
  55.7 1.3 %collective-permute-start.16 = (f32[4,64,256]{2,1,0:T(8,128)S(1)}, f32[4,64,256]{2,1,0:T(8,128)S(1)}, u32[]{:S(2)}, u32[]{:S(2)}) collective-permute-start(f32[4,64,256]{2,1,0:T(8,128)S(1)} %get-tuple-element.48), channel_id=1, source_target_pairs={{2,1},{3,0},{18,17},{19,16},{6,5},{7,4},{22,21},{23,20},{10,9},{11... | collective-permute-start | bytes 786440 | tf_op jit(solution)/shard_map/ppermute | solution.py:384
  57.0 0.7 copy.11
  57.7 0.7 copy.12
  58.4 3.3 %collective-permute-done.14.refs_1_ = f32[4,64,256]{2,1,0:T(8,128)S(1)} collective-permute-done((f32[4,64,256]{2,1,0:T(8,128)S(1)}, f32[4,64,256]{2,1,0:T(8,128)S(1)}, u32[]{:S(2)}, u32[]{:S(2)}) %collective-permute-start.14) | collective-permute-done | bytes 262176 | tf_op jit(solution)/shard_map/ppermute | solution.py:384
  61.7 8.4 %collective-permute-done.15.refs_2_ = f32[4,64,256]{2,1,0:T(8,128)S(1)} collective-permute-done((f32[4,64,256]{2,1,0:T(8,128)S(1)}, f32[4,64,256]{2,1,0:T(8,128)S(1)}, u32[]{:S(2)}, u32[]{:S(2)}) %collective-permute-start.15) | collective-permute-done | bytes 262176 | tf_op jit(solution)/shard_map/ppermute | solution.py:384
  70.1 4.0 %shard_map.110 = f32[1,1,1,256,256]{4,3,2,1,0:T(8,128)} custom-call(s32[1,1]{1,0:T(1,128)S(6)} %copy.13.count_ref, f32[4,64,256]{2,1,0:T(8,128)S(1)} %get-tuple-element.45.refs_0_, f32[4,64,256]{2,1,0:T(8,128)S(1)} %collective-permute-done.14.refs_1_, f32[4,64,256]{2,1,0:T(8,128)S(1)} %collective-permute-done.15.refs_2_, ...), custom_call_target="tpu_custom_call" | custom-call | tf_op jit(solution)/shard_map/pallas_call | solution.py:30
  (28 shorter events, 0.6 us)
Async XLA Ops:
  0.6 1.9 %collective-permute-start = (f32[4,64,256]{2,1,0:T(8,128)}, f32[4,64,256]{2,1,0:T(8,128)S(1)}, u32[]{:S(2)}, u32[]{:S(2)}) collective-permute-start(f32[4,64,256]{2,1,0:T(8,128)} %bitcast.7), channel_id=1, source_target_pairs={{0,16},{16,0},{1,17},{17,1},{2,18},{18,2},{3,19},{19,3},{4,20},{20... | collective-permute-start | bytes 786440 | tf_op jit(solution)/shard_map/ppermute | solution.py:375
  2.6 0.9 %copy-start.1 = (f32[2,2,64,256]{3,2,1,0:T(8,128)S(1)}, f32[2,2,64,256]{3,2,1,0:T(8,128)}, u32[]{:S(2)}) copy-start(f32[2,2,64,256]{3,2,1,0:T(8,128)} %param.8) | copy-start | bytes 786436
  3.5 5.8 %copy-start.4 = (f32[1,1,1,256,256]{4,3,2,1,0:T(8,128)S(1)}, f32[1,1,1,256,256]{4,3,2,1,0:T(8,128)}, u32[]{:S(2)}) copy-start(f32[1,1,1,256,256]{4,3,2,1,0:T(8,128)} %refs_7_.1) | copy-start | bytes 786436
  3.5 7.3 %copy-start.7 = (s32[1,1,4,2]{2,3,1,0:T(2,128)S(1)}, s32[1,1,4,2]{2,3,1,0:T(2,128)}, u32[]{:S(2)}) copy-start(s32[1,1,4,2]{2,3,1,0:T(2,128)} %param.13) | copy-start | bytes 100
  3.5 13.2 %copy-start.5 = (f32[256,256]{1,0:T(8,128)S(1)}, f32[256,256]{1,0:T(8,128)}, u32[]{:S(2)}) copy-start(f32[256,256]{1,0:T(8,128)} %phase_ref.1) | copy-start | bytes 786436
  3.8 12.9 %copy-start.3 = (f32[2,256,256]{2,1,0:T(8,128)S(1)}, f32[2,256,256]{2,1,0:T(8,128)}, u32[]{:S(2)}) copy-start(f32[2,256,256]{2,1,0:T(8,128)} %light_ref.1) | copy-start | bytes 1572868
  3.8 5.5 %collective-permute-start.1 = (f32[4,64,128]{2,1,0:T(8,128)S(1)}, f32[4,64,128]{2,1,0:T(8,128)S(1)}, u32[]{:S(2)}, u32[]{:S(2)}) collective-permute-start(f32[4,64,128]{2,1,0:T(8,128)S(1)} %shard_map.103), channel_id=1, source_target_pairs={{0,4},{4,8},{8,12},{12,28},{20,16},{24,20},{28,24},{16,0},{1,5},{5... | collective-permute-start | bytes 393224 | tf_op jit(solution)/shard_map/ppermute | solution.py:379
  9.3 1.5 %collective-permute-start.2 = (f32[4,64,128]{2,1,0:T(8,128)S(1)}, f32[4,64,128]{2,1,0:T(8,128)S(1)}, u32[]{:S(2)}, u32[]{:S(2)}) collective-permute-start(f32[4,64,128]{2,1,0:T(8,128)S(1)} %collective-permute-done.1.mine_ref), channel_id=1, source_target_pairs={{0,16},{16,0},{1,17},{17,1},{2,18},{18,2},{3,19},{19,3},{4,20},{20... | collective-permute-start | bytes 393224 | tf_op jit(solution)/shard_map/ppermute | solution.py:375
  9.3 10.0 %collective-permute-start.6 = (f32[1,1,1,256,256]{4,3,2,1,0:T(8,128)S(1)}, f32[1,1,1,256,256]{4,3,2,1,0:T(8,128)S(1)}, u32[]{:S(2)}, u32[]{:S(2)}) collective-permute-start(f32[1,1,1,256,256]{4,3,2,1,0:T(8,128)S(1)} %copy-done.4), channel_id=1, source_target_pairs={{0,2},{1,3},{2,0},{3,1},{4,6},{5,7},{6,4},{7,5},{8,10},{9,11},{10,... | collective-permute-start | bytes 786440 | tf_op jit(solution)/shard_map/ppermute | solution.py:387
  10.8 13.5 %copy-start = (bf16[6,256,256]{2,1,0:T(8,128)(2,1)S(1)}, bf16[6,256,256]{2,1,0:T(8,128)(2,1)}, u32[]{:S(2)}) copy-start(bf16[6,256,256]{2,1,0:T(8,128)(2,1)} %constant.2.clone.refs_6_) | copy-start | bytes 2359300
  11.7 9.8 %collective-permute-start.3 = (f32[4,64,256]{2,1,0:T(8,128)S(1)}, f32[4,64,256]{2,1,0:T(8,128)S(1)}, u32[]{:S(2)}, u32[]{:S(2)}) collective-permute-start(f32[4,64,256]{2,1,0:T(8,128)S(1)} %get-tuple-element.29), channel_id=1, source_target_pairs={{0,1},{1,0},{18,19},{19,18},{4,5},{5,4},{22,23},{23,22},{8,9},{9,8... | collective-permute-start | bytes 786440 | tf_op jit(solution)/shard_map/ppermute | solution.py:384
  15.1 9.2 %collective-permute-start.4 = (f32[4,64,256]{2,1,0:T(8,128)S(1)}, f32[4,64,256]{2,1,0:T(8,128)S(1)}, u32[]{:S(2)}, u32[]{:S(2)}) collective-permute-start(f32[4,64,256]{2,1,0:T(8,128)S(1)} %get-tuple-element.30), channel_id=1, source_target_pairs={{2,0},{3,1},{16,18},{17,19},{0,16},{1,17},{18,2},{19,3},{6,4},{7,5... | collective-permute-start | bytes 786440 | tf_op jit(solution)/shard_map/ppermute | solution.py:384
  15.2 9.2 %collective-permute-start.5 = (f32[4,64,256]{2,1,0:T(8,128)S(1)}, f32[4,64,256]{2,1,0:T(8,128)S(1)}, u32[]{:S(2)}, u32[]{:S(2)}) collective-permute-start(f32[4,64,256]{2,1,0:T(8,128)S(1)} %get-tuple-element.31), channel_id=1, source_target_pairs={{2,1},{3,0},{16,19},{17,18},{0,16},{1,17},{18,2},{19,3},{6,5},{7,4... | collective-permute-start | bytes 786440 | tf_op jit(solution)/shard_map/ppermute | solution.py:384
  24.3 16.2 %copy-start.6 = (f32[2,2,64,256]{3,2,1,0:T(8,128)S(1)}, f32[2,2,64,256]{3,2,1,0:T(8,128)}, u32[]{:S(2)}) copy-start(f32[2,2,64,256]{3,2,1,0:T(8,128)} %param.9) | copy-start | bytes 786436
  31.0 8.3 %collective-permute-start.7 = (f32[4,64,256]{2,1,0:T(8,128)S(1)}, f32[4,64,256]{2,1,0:T(8,128)S(1)}, u32[]{:S(2)}, u32[]{:S(2)}) collective-permute-start(f32[4,64,256]{2,1,0:T(8,128)S(1)} %get-tuple-element.35), channel_id=1, source_target_pairs={{1,0},{0,1},{19,18},{18,19},{5,4},{4,5},{23,22},{22,23},{9,8},{8,9... | collective-permute-start | bytes 786440 | tf_op jit(solution)/shard_map/ppermute | solution.py:384
  33.8 5.5 %collective-permute-start.8 = (f32[4,64,256]{2,1,0:T(8,128)S(1)}, f32[4,64,256]{2,1,0:T(8,128)S(1)}, u32[]{:S(2)}, u32[]{:S(2)}) collective-permute-start(f32[4,64,256]{2,1,0:T(8,128)S(1)} %get-tuple-element.36), channel_id=1, source_target_pairs={{0,2},{1,3},{18,16},{19,17},{2,18},{3,19},{16,0},{17,1},{4,6},{5,7... | collective-permute-start | bytes 786440 | tf_op jit(solution)/shard_map/ppermute | solution.py:384
  33.8 6.6 %collective-permute-start.9 = (f32[4,64,256]{2,1,0:T(8,128)S(1)}, f32[4,64,256]{2,1,0:T(8,128)S(1)}, u32[]{:S(2)}, u32[]{:S(2)}) collective-permute-start(f32[4,64,256]{2,1,0:T(8,128)S(1)} %get-tuple-element.37), channel_id=1, source_target_pairs={{1,2},{0,3},{19,16},{18,17},{2,18},{3,19},{16,0},{17,1},{5,6},{4,7... | collective-permute-start | bytes 786440 | tf_op jit(solution)/shard_map/ppermute | solution.py:384
  41.4 2.5 %collective-permute-start.10 = (f32[2,4,64,256]{3,2,1,0:T(8,128)S(1)}, f32[2,4,64,256]{3,2,1,0:T(8,128)S(1)}, u32[]{:S(2)}, u32[]{:S(2)}) collective-permute-start(f32[2,4,64,256]{3,2,1,0:T(8,128)S(1)} %get-tuple-element.38.own_ref), channel_id=1, source_target_pairs={{0,16},{16,0},{1,17},{17,1},{2,18},{18,2},{3,19},{19,3},{4,20},{20... | collective-permute-start | bytes 1572872 | tf_op jit(solution)/shard_map/ppermute | solution.py:375
  41.9 9.9 %copy-start.2 = (f32[2,2,64,256]{3,2,1,0:T(8,128)S(1)}, f32[2,2,64,256]{3,2,1,0:T(8,128)}, u32[]{:S(2)}) copy-start(f32[2,2,64,256]{3,2,1,0:T(8,128)} %param.8) | copy-start | bytes 786436
  41.9 1.9 %collective-permute-start.11 = (f32[2,4,64,128]{3,2,1,0:T(8,128)S(1)}, f32[2,4,64,128]{3,2,1,0:T(8,128)S(1)}, u32[]{:S(2)}, u32[]{:S(2)}) collective-permute-start(f32[2,4,64,128]{3,2,1,0:T(8,128)S(1)} %get-tuple-element.39.halo_ref), channel_id=1, source_target_pairs={{0,16},{16,0},{1,17},{17,1},{2,18},{18,2},{3,19},{19,3},{4,20},{20... | collective-permute-start | bytes 786440 | tf_op jit(solution)/shard_map/ppermute | solution.py:375
  44.0 6.4 %collective-permute-start.12 = (f32[2,4,64,128]{3,2,1,0:T(8,128)S(1)}, f32[2,4,64,128]{3,2,1,0:T(8,128)S(1)}, u32[]{:S(2)}, u32[]{:S(2)}) collective-permute-start(f32[2,4,64,128]{3,2,1,0:T(8,128)S(1)} %get-tuple-element.42), channel_id=1, source_target_pairs={{0,4},{4,8},{8,12},{12,28},{20,16},{24,20},{28,24},{16,0},{1,5},{5... | collective-permute-start | bytes 786440 | tf_op jit(solution)/shard_map/ppermute | solution.py:379
  50.3 1.5 %collective-permute-start.13 = (f32[2,4,64,128]{3,2,1,0:T(8,128)S(1)}, f32[2,4,64,128]{3,2,1,0:T(8,128)S(1)}, u32[]{:S(2)}, u32[]{:S(2)}) collective-permute-start(f32[2,4,64,128]{3,2,1,0:T(8,128)S(1)} %collective-permute-done.12.mine_ref), channel_id=1, source_target_pairs={{0,16},{16,0},{1,17},{17,1},{2,18},{18,2},{3,19},{19,3},{4,20},{20... | collective-permute-start | bytes 786440 | tf_op jit(solution)/shard_map/ppermute | solution.py:375
  53.4 8.3 %collective-permute-start.14 = (f32[4,64,256]{2,1,0:T(8,128)S(1)}, f32[4,64,256]{2,1,0:T(8,128)S(1)}, u32[]{:S(2)}, u32[]{:S(2)}) collective-permute-start(f32[4,64,256]{2,1,0:T(8,128)S(1)} %get-tuple-element.46), channel_id=1, source_target_pairs={{0,1},{1,0},{16,17},{17,16},{2,18},{3,19},{18,2},{19,3},{4,5},{5,4... | collective-permute-start | bytes 786440 | tf_op jit(solution)/shard_map/ppermute | solution.py:384
  54.4 15.7 %collective-permute-start.15 = (f32[4,64,256]{2,1,0:T(8,128)S(1)}, f32[4,64,256]{2,1,0:T(8,128)S(1)}, u32[]{:S(2)}, u32[]{:S(2)}) collective-permute-start(f32[4,64,256]{2,1,0:T(8,128)S(1)} %get-tuple-element.47), channel_id=1, source_target_pairs={{2,0},{3,1},{18,16},{19,17},{6,4},{7,5},{22,20},{23,21},{10,8},{11... | collective-permute-start | bytes 786440 | tf_op jit(solution)/shard_map/ppermute | solution.py:384
  55.7 14.4 %collective-permute-start.16 = (f32[4,64,256]{2,1,0:T(8,128)S(1)}, f32[4,64,256]{2,1,0:T(8,128)S(1)}, u32[]{:S(2)}, u32[]{:S(2)}) collective-permute-start(f32[4,64,256]{2,1,0:T(8,128)S(1)} %get-tuple-element.48), channel_id=1, source_target_pairs={{2,1},{3,0},{18,17},{19,16},{6,5},{7,4},{22,21},{23,20},{10,9},{11... | collective-permute-start | bytes 786440 | tf_op jit(solution)/shard_map/ppermute | solution.py:384

commit v3 on v2

--- a/solution.py
+++ b/solution.py
@@ -145,7 +145,11 @@
         for c in range(4):
             mine = jnp.where(halo, spread(own_halo[c], lay), own[c])
             theirs = jnp.where(halo, spread(prt_halo[c], lay), prt[c])
-            out_refs[s][c] = jnp.where(partner, theirs, jnp.where(outside, 0.0, mine))
+            value = jnp.where(partner, theirs, jnp.where(outside, 0.0, mine))
+            if home:
+                out_refs[c // 2 * lay.n + s][c % 2] = value
+            else:
+                out_refs[s][c] = value
 
 
 def spread(halo, lay):
@@ -195,11 +199,36 @@
     return body
 
 
+def load(*arrays):
+    count = len(arrays)
+
+    def body(*refs):
+        sources, targets, sems = refs[:count], refs[count : 2 * count], refs[2 * count]
+        copies = [pltpu.make_async_copy(x, y, sems.at[i]) for i, (x, y) in enumerate(zip(sources, targets))]
+        for copy in copies:
+            copy.start()
+        for copy in copies:
+            copy.wait()
+
+    return pl.pallas_call(
+        body,
+        out_shape=tuple(pltpu.VMEM(x.shape, x.dtype) for x in arrays),
+        in_specs=[pl.BlockSpec(memory_space=pl.ANY)] * count,
+        out_specs=tuple(vmem() for _ in arrays),
+        scratch_shapes=[pltpu.SemaphoreType.DMA((count,))],
+        name="load_kernel",
+        compiler_params=pltpu.CompilerParams(vmem_limit_bytes=2 * 1024 * 1024),
+    )(*[pltpu.with_memory_space_constraint(x, pltpu.HBM) for x in arrays])
+
+
+def kernel_slab(phase_ref, slab_ref):
+    slab_ref[0] = jnp.cos(phase_ref[...])
+    slab_ref[1] = jnp.sin(phase_ref[...])
+
+
 def kernel_probe(lay):
-    def body(place_ref, light_ref, phase_ref, out_ref, slab_ref):
+    def body(place_ref, light_ref, out_ref):
         a, _, p = where_am_i()
-        slab_ref[0] = jnp.cos(phase_ref[...])
-        slab_ref[1] = jnp.sin(phase_ref[...])
         for i, home in enumerate((False, True)):
             k = jnp.clip(lay.window_of(p, a, home), 0, lay.slots - 1)
             down = (place_ref[0, 0, 0, k] + (lay.t - lay.m)) % lay.t
@@ -214,18 +243,15 @@
     p = lax.axis_index("pos")
     for s in range(lay.n):
         start = pl.multiple_of((p ^ s) * lay.h, lay.h)
-        for c in range(4):
+        for c in range(window_ref.shape[0]):
             window_ref[c, pl.ds(start, lay.h), :] = blocks[s][c]
 
 
-def forward(window_ref, light_ref, which, slab_ref, tab):
-    o1r, o1i, o2r, o2i = (window_ref[c] for c in range(4))
+def propagate(o1r, o1i, light_ref, which, slab_ref, tab):
     er, ei = cmul(light_ref[which, 0], light_ref[which, 1], o1r, o1i)
     sr, si = transform(er, ei, tab, False)
     sr, si = cmul(sr, si, slab_ref[0], slab_ref[1])
-    br, bi = transform(sr, si, tab, True)
-    lr, li = cmul(br, bi, o2r, o2i)
-    return br, bi, transform(lr, li, tab, False)
+    return transform(sr, si, tab, True)
 
 
 def kernel_gradient(lay):
@@ -239,7 +265,9 @@
         @pl.when((k >= 0) & (k < count_ref[0, 0]))
         def _():
             assemble(blocks, window_ref, lay)
-            br, bi, (fr, fi) = forward(window_ref, light_ref, 0, slab_ref, tab)
+            br, bi = propagate(window_ref[0], window_ref[1], light_ref, 0, slab_ref, tab)
+            lr, li = cmul(br, bi, window_ref[2], window_ref[3])
+            fr, fi = transform(lr, li, tab, False)
             seen = jnp.where(a == 0, meas_ref[0, 0, 0], moved_ref[0, 0, 0])
             keeping = 1.0 - seen / jnp.maximum(jnp.sqrt(fr * fr + fi * fi), magnitude_floor)
             kr, ki = transform(fr * keeping, fi * keeping, tab, True)
@@ -320,7 +348,8 @@
 
     def body(place_ref, obj_ref, prt_ref, obj_halo_ref, prt_halo_ref, sum_ref, halo_sum_ref, mine_ref, theirs_ref, *outs):
         n = lay.n
-        new_ref, vel_ref, blocks, prt_new, own_halo, prt_halo = outs[0], outs[1], outs[2 : n + 2], *outs[n + 2 :]
+        new_ref, vel_ref, *blocks = outs[: 2 * n + 2]
+        prt_new, own_halo, prt_halo = outs[2 * n + 2 :]
         a, b, _ = where_am_i()
         low = iota((lay.h, 2 * m), 1) < m
         not_first, not_last = b > 0, b < lay.ntx - 1
@@ -346,19 +375,33 @@
     return body
 
 
+def kernel_between(lay):
+    def body(count_ref, *refs):
+        n = lay.n
+        blocks, (light_ref, slab_ref, tab), out_ref, window_ref = refs[:n], refs[n : n + 3], refs[n + 3], refs[n + 4]
+
+        @pl.when(lax.axis_index("pos") < count_ref[0, 0])
+        def _():
+            assemble(blocks, window_ref, lay)
+            out_ref[0], out_ref[1] = propagate(window_ref[0], window_ref[1], light_ref, 1, slab_ref, tab)
+
+    return body
+
+
 def kernel_predict(lay):
     def body(count_ref, *refs):
         n = lay.n
-        blocks, (light_ref, slab_ref, tab), out_ref, window_ref = refs[:n], refs[n : n + 3], refs[n + 3], refs[n + 4]
-        p = lax.axis_index("pos")
-
-        @pl.when(p < count_ref[0, 0])
+        blocks, (between_ref, tab), out_ref, window_ref = refs[:n], refs[n : n + 2], refs[n + 2], refs[n + 3]
+        live = lax.axis_index("pos") < count_ref[0, 0]
+
+        @pl.when(live)
         def _():
             assemble(blocks, window_ref, lay)
-            _, _, (fr, fi) = forward(window_ref, light_ref, 1, slab_ref, tab)
+            lr, li = cmul(between_ref[0], between_ref[1], window_ref[0], window_ref[1])
+            fr, fi = transform(lr, li, tab, False)
             out_ref[0, 0, 0] = jnp.sqrt(fr * fr + fi * fi)
 
-        @pl.when(p >= count_ref[0, 0])
+        @pl.when(jnp.logical_not(live))
         def _():
             out_ref[...] = jnp.zeros(out_ref.shape, F32)
 
@@ -372,23 +415,27 @@
     offsets = offsets.transpose(0, 1, 3, 2)
     velocity_old = momentum.reshape(4, h, t)
     block, halo_shape = (4, h, t), (4, h, 2 * m)
+    tab = jnp.asarray(dft_tables(t))
     cores = lambda x: lax.ppermute(x, "ty", [(0, 1), (1, 0)])
+    partner = cores(own)
+    own, velocity_old, measured, illumination, slab_phase, tab = load(
+        own, velocity_old, measured, illumination, slab_phase, tab
+    )
     ntx = lay.ntx
     shift = [(b, b + 1) for b in range(ntx - 1)] + [(ntx - 1, 2 * ntx - 1)]
     shift += [(ntx + b + 1, ntx + b) for b in range(ntx - 1)] + [(ntx, 0)]
     columns = lambda x: lax.ppermute(x, ("ty", "tx"), shift)
 
     def exchange(values, pairs_of):
-        got = {0: values[0]}
-        for s in [*range(lay.half, n), *range(1, lay.half)]:
-            got[s] = lax.ppermute(values[s], ("ty", "pos"), complete(pairs_of(s), n))
-        return [got[s] for s in range(n)]
+        got = [values[0]]
+        for s in range(1, n):
+            got.append(lax.ppermute(values[s], ("ty", "pos"), complete(pairs_of(s), n)))
+        return got
 
     moved = lax.ppermute(measured, "pos", [(p, p ^ lay.half) for p in range(n)])
-    tab = jnp.asarray(dft_tables(t))
-    light, slab = call(kernel_probe(lay), [(2, 2, t, t), (2, t, t)], [offsets, illumination, slab_phase], 1)
-
-    partner = cores(own)
+    (slab,) = call(kernel_slab, [(2, t, t)], [slab_phase])
+    (light,) = call(kernel_probe(lay), [(2, 2, t, t)], [offsets, illumination], 1)
+
     (strips,) = call(kernel_strips(lay), [halo_shape], [own, partner])
     strips = columns(strips)
     strips_other = cores(strips)
@@ -417,18 +464,23 @@
     strips = columns(strips)
     updated, velocity, *rest = call(
         kernel_update(lay),
-        [block] * (n + 3) + [halo_shape] * 2,
+        [block] * 2 + [(2, h, t)] * (2 * n),
         [offsets, own, partner, own_halo, partner_halo, sums, halos, strips, cores(strips)],
         1,
-    )
-    blocks = rest[:n]
-    received = exchange(blocks, lambda s: lay.inward(s, True))
+        [pltpu.VMEM(block, F32), pltpu.VMEM(halo_shape, F32), pltpu.VMEM(halo_shape, F32)],
+    )
+    first = exchange(rest[:n], lambda s: lay.inward(s, True))
+    second = exchange(rest[n : 2 * n], lambda s: lay.inward(s, True))
+    half_window = pltpu.VMEM((2, t, t), F32)
+    (between,) = call(
+        kernel_between(lay), [(2, t, t)], [entry_counts, *first, light, slab, tab], 1, [half_window], limit=24
+    )
     (amplitudes,) = call(
         kernel_predict(lay),
         [measured.shape],
-        [entry_counts, *received, light, slab, tab],
+        [entry_counts, *second, between, tab],
         1,
-        [window],
+        [half_window],
         limit=24,
         last=True,
     )

time: 74.4 us -> 71.4 us (0.960)
  the two profiles are of different devices: /device:TPU:0 before, /device:TPU:1 now
where the time goes in v3:
time: 71.4 us; the launch traced here: 70.2 us
  waiting for transfers between devices  30 us (42%)
  starting transfers between devices  26 us (36%)
  Pallas kernels  11.4 us (16%)
  between operations  1.43 us (2%)
  local copies, waits for them, and re-layouts  1.41 us (2%)
    ppermute x12, starting transfers between devices, exchange(): got.append(lax.ppermute(values[s], ('ty', 'pos'), complete(pairs_of(s), n)))  22.4 us
    ppermute x12, waiting for transfers between devices, exchange(): got.append(lax.ppermute(values[s], ('ty', 'pos'), complete(pairs_of(s), n)))  16.5 us
    ppermute x2, waiting for transfers between devices, iteration(): columns = lambda x: lax.ppermute(x, ('ty', 'tx'), shift)  10.4 us
    pallas_call x10, Pallas kernels, call(): pl.pallas_call(body, out_shape=tuple(((jax.ShapeDtypeStruct if last else...  9.73 us
    ppermute x5, waiting for transfers between devices, iteration(): cores = lambda x: lax.ppermute(x, 'ty', [(0, 1), (1, 0)])  3 us
    ppermute x5, starting transfers between devices, iteration(): cores = lambda x: lax.ppermute(x, 'ty', [(0, 1), (1, 0)])  1.71 us
    pallas_call x1, Pallas kernels, load(): pl.pallas_call(body, out_shape=tuple((pltpu.VMEM(x.shape, x.dtype) for x...  1.66 us
  transfers between devices with their start and end apart: 20, of which 10 were waited for; matrix products, arithmetic and copies ran while one was open for 2% of the time, Pallas kernels for 10%

profile of v3, /device:TPU:1, one launch (start us, length us, event | category | flops | bytes accessed | tf_op | source)
XLA Modules:
  0.0 70.2 jit_solution(12480002983561950617)
XLA Ops:
  0.7 1.7 %load_kernel.1 = (f32[4,64,256]{2,1,0:T(8,128)S(1)}, f32[4,64,256]{2,1,0:T(8,128)S(1)}, f32[1,1,1,256,256]{4,3,2,1,0:T(8,128)S(1)}, f32[2,256,256]{2,1,0:T(8,128...) custom-call(f32[4,64,256]{2,1,0:T(8,128)} %bitcast.13, f32[4,64,256]{2,1,0:T(8,128)} %bitcast.11, ...), custom_call_target="tpu_custom_call" | custom-call | tf_op jit(solution)/shard_map/load_kernel/pallas_call | solution.py:213
  3.2 4.6 %collective-permute-done.1.mine_ref = f32[4,64,128]{2,1,0:T(8,128)S(1)} collective-permute-done((f32[4,64,128]{2,1,0:T(8,128)S(1)}, f32[4,64,128]{2,1,0:T(8,128)S(1)}, u32[]{:S(2)}, u32[]{:S(2)}) %collective-permute-start.1) | collective-permute-done | bytes 131104 | tf_op jit(solution)/shard_map/ppermute | solution.py:427
  7.8 0.5 collective-permute-start.2
  8.3 1.2 %collective-permute-start.6 = (f32[1,1,1,256,256]{4,3,2,1,0:T(8,128)S(1)}, f32[1,1,1,256,256]{4,3,2,1,0:T(8,128)S(1)}, u32[]{:S(2)}, u32[]{:S(2)}) collective-permute-start(f32[1,1,1,256,256]{4,3,2,1,0:T(8,128)S(1)} %get-tuple-element.44.refs_7_), channel_id=1, source_target_pairs={{0,2},{1,3},{2,0},{3,1},{4,6},{5,7},{6,4},{7,5},{8,10},{9,11},{10,... | collective-permute-start | bytes 786440 | tf_op jit(solution)/shard_map/ppermute | solution.py:435
  9.6 0.9 %shard_map.104 = (f32[4,64,256]{2,1,0:T(8,128)S(1)}, f32[4,64,256]{2,1,0:T(8,128)S(1)}, f32[4,64,256]{2,1,0:T(8,128)S(1)}, f32[4,64,256]{2,1,0:T(8,128)S(1)}, f3...) custom-call(s32[1,1,2,4]{3,2,1,0:T(2,128)S(1)} %bitcast.7, f32[4,64,256]{2,1,0:T(8,128)S(1)} %get-tuple-element.34.own_ref.obj_ref, ...), custom_call_target="tpu_custom_call" | custom-call | tf_op jit(solution)/shard_map/pallas_call | solution.py:30
  10.5 0.7 collective-permute-start.3
  11.2 3.5 %collective-permute-start.4 = (f32[4,64,256]{2,1,0:T(8,128)S(1)}, f32[4,64,256]{2,1,0:T(8,128)S(1)}, u32[]{:S(2)}, u32[]{:S(2)}) collective-permute-start(f32[4,64,256]{2,1,0:T(8,128)S(1)} %get-tuple-element.39), channel_id=1, source_target_pairs={{2,0},{3,1},{16,18},{17,19},{0,16},{1,17},{18,2},{19,3},{6,4},{7,5... | collective-permute-start | bytes 786440 | tf_op jit(solution)/shard_map/ppermute | solution.py:432
  15.3 1.0 %shard_map.105.refs_4_ = f32[2,2,256,256]{3,2,1,0:T(8,128)S(1)} custom-call(s32[1,1,2,4]{3,2,1,0:T(2,128)S(1)} %bitcast.8, f32[2,256,256]{2,1,0:T(8,128)S(1)} %get-tuple-element.41.light_ref), custom_call_target="tpu_custom_call" | custom-call | tf_op jit(solution)/shard_map/pallas_call | solution.py:30
  16.3 1.7 %shard_map.106.refs_5_ = f32[2,256,256]{2,1,0:T(8,128)S(1)} custom-call(f32[256,256]{1,0:T(8,128)S(1)} %get-tuple-element.42.phase_ref), custom_call_target="tpu_custom_call" | custom-call | tf_op jit(solution)/shard_map/pallas_call | solution.py:30
  18.0 3.3 %collective-permute-done.4.refs_2_ = f32[4,64,256]{2,1,0:T(8,128)S(1)} collective-permute-done((f32[4,64,256]{2,1,0:T(8,128)S(1)}, f32[4,64,256]{2,1,0:T(8,128)S(1)}, u32[]{:S(2)}, u32[]{:S(2)}) %collective-permute-start.4) | collective-permute-done | bytes 262176 | tf_op jit(solution)/shard_map/ppermute | solution.py:432
  21.3 0.7 collective-permute-start.7
  22.0 10.8 %collective-permute-start.8 = (f32[4,64,256]{2,1,0:T(8,128)S(1)}, f32[4,64,256]{2,1,0:T(8,128)S(1)}, u32[]{:S(2)}, u32[]{:S(2)}) collective-permute-start(f32[4,64,256]{2,1,0:T(8,128)S(1)} %get-tuple-element.47), channel_id=1, source_target_pairs={{0,2},{1,3},{18,16},{19,17},{2,18},{3,19},{16,0},{17,1},{4,6},{5,7... | collective-permute-start | bytes 786440 | tf_op jit(solution)/shard_map/ppermute | solution.py:432
  32.9 3.0 %collective-permute-done.8.refs_2_ = f32[4,64,256]{2,1,0:T(8,128)S(1)} collective-permute-done((f32[4,64,256]{2,1,0:T(8,128)S(1)}, f32[4,64,256]{2,1,0:T(8,128)S(1)}, u32[]{:S(2)}, u32[]{:S(2)}) %collective-permute-start.8) | collective-permute-done | bytes 262176 | tf_op jit(solution)/shard_map/ppermute | solution.py:432
  36.0 3.6 %collective-permute-done.9.refs_3_ = f32[4,64,256]{2,1,0:T(8,128)S(1)} collective-permute-done((f32[4,64,256]{2,1,0:T(8,128)S(1)}, f32[4,64,256]{2,1,0:T(8,128)S(1)}, u32[]{:S(2)}, u32[]{:S(2)}) %collective-permute-start.9) | collective-permute-done | bytes 262176 | tf_op jit(solution)/shard_map/ppermute | solution.py:432
  39.6 0.8 %shard_map.108 = (f32[2,4,64,256]{3,2,1,0:T(8,128)S(1)}, f32[2,4,64,128]{3,2,1,0:T(8,128)S(1)}) custom-call(s32[1,1,2,4]{3,2,1,0:T(2,128)S(1)} %bitcast.9, s32[1,1]{1,0:T(1,128)S(6)} %copy.13.count_ref, f32[4,64,256]{2,1,0:T(8,128)S(1)} %get-tuple-element.45.refs_0_, f32[4,64,256]{2,1,0:T(8,128)S(1)} %collective-permute-done.7.refs_1_, ...), custom_call_target="tpu_custom_call" | custom-call | tf_op jit(solution)/shard_map/pallas_call | solution.py:30
  40.9 1.8 %collective-permute-done.11.their_halo_ref = f32[2,4,64,128]{3,2,1,0:T(8,128)S(1)} collective-permute-done((f32[2,4,64,128]{3,2,1,0:T(8,128)S(1)}, f32[2,4,64,128]{3,2,1,0:T(8,128)S(1)}, u32[]{:S(2)}, u32[]{:S(2)}) %collective-permute-start.11) | collective-permute-done | bytes 262176 | tf_op jit(solution)/shard_map/ppermute | solution.py:419
  43.0 5.8 %collective-permute-done.12.mine_ref = f32[2,4,64,128]{3,2,1,0:T(8,128)S(1)} collective-permute-done((f32[2,4,64,128]{3,2,1,0:T(8,128)S(1)}, f32[2,4,64,128]{3,2,1,0:T(8,128)S(1)}, u32[]{:S(2)}, u32[]{:S(2)}) %collective-permute-start.12) | collective-permute-done | bytes 262176 | tf_op jit(solution)/shard_map/ppermute | solution.py:427
  48.8 0.6 collective-permute-start.13
  49.3 1.2 %collective-permute-done.13.theirs_ref = f32[2,4,64,128]{3,2,1,0:T(8,128)S(1)} collective-permute-done((f32[2,4,64,128]{3,2,1,0:T(8,128)S(1)}, f32[2,4,64,128]{3,2,1,0:T(8,128)S(1)}, u32[]{:S(2)}, u32[]{:S(2)}) %collective-permute-start.13) | collective-permute-done | bytes 262176 | tf_op jit(solution)/shard_map/ppermute | solution.py:419
  50.5 1.0 %shard_map.110 = (f32[4,64,256]{2,1,0:T(8,128)S(1)}, f32[4,64,256]{2,1,0:T(8,128)S(1)}, f32[2,64,256]{2,1,0:T(8,128)S(1)}, f32[2,64,256]{2,1,0:T(8,128)S(1)}, f3...) custom-call(s32[1,1,2,4]{3,2,1,0:T(2,128)S(1)} %bitcast.10, ...), custom_call_target="tpu_custom_call" | custom-call | tf_op jit(solution)/shard_map/pallas_call | solution.py:30
  51.5 0.8 %collective-permute-start.17 = (f32[2,64,256]{2,1,0:T(8,128)S(1)}, f32[2,64,256]{2,1,0:T(8,128)S(1)}, u32[]{:S(2)}, u32[]{:S(2)}) collective-permute-start(f32[2,64,256]{2,1,0:T(8,128)S(1)} %get-tuple-element.62), channel_id=1, source_target_pairs={{0,1},{1,0},{16,17},{17,16},{2,18},{3,19},{18,2},{19,3},{4,5},{5,4... | collective-permute-start | bytes 393224 | tf_op jit(solution)/shard_map/ppermute | solution.py:432
  52.3 0.7 collective-permute-start.14
  53.0 1.3 %collective-permute-start.18 = (f32[2,64,256]{2,1,0:T(8,128)S(1)}, f32[2,64,256]{2,1,0:T(8,128)S(1)}, u32[]{:S(2)}, u32[]{:S(2)}) collective-permute-start(f32[2,64,256]{2,1,0:T(8,128)S(1)} %get-tuple-element.63), channel_id=1, source_target_pairs={{2,0},{3,1},{18,16},{19,17},{6,4},{7,5},{22,20},{23,21},{10,8},{11... | collective-permute-start | bytes 393224 | tf_op jit(solution)/shard_map/ppermute | solution.py:432
  54.3 1.3 %collective-permute-start.19 = (f32[2,64,256]{2,1,0:T(8,128)S(1)}, f32[2,64,256]{2,1,0:T(8,128)S(1)}, u32[]{:S(2)}, u32[]{:S(2)}) collective-permute-start(f32[2,64,256]{2,1,0:T(8,128)S(1)} %get-tuple-element.64), channel_id=1, source_target_pairs={{2,1},{3,0},{18,17},{19,16},{6,5},{7,4},{22,21},{23,20},{10,9},{11... | collective-permute-start | bytes 393224 | tf_op jit(solution)/shard_map/ppermute | solution.py:432
  55.6 1.3 %collective-permute-start.15 = (f32[2,64,256]{2,1,0:T(8,128)S(1)}, f32[2,64,256]{2,1,0:T(8,128)S(1)}, u32[]{:S(2)}, u32[]{:S(2)}) collective-permute-start(f32[2,64,256]{2,1,0:T(8,128)S(1)} %get-tuple-element.59), channel_id=1, source_target_pairs={{2,0},{3,1},{18,16},{19,17},{6,4},{7,5},{22,20},{23,21},{10,8},{11... | collective-permute-start | bytes 393224 | tf_op jit(solution)/shard_map/ppermute | solution.py:432
  56.9 1.3 %collective-permute-start.16 = (f32[2,64,256]{2,1,0:T(8,128)S(1)}, f32[2,64,256]{2,1,0:T(8,128)S(1)}, u32[]{:S(2)}, u32[]{:S(2)}) collective-permute-start(f32[2,64,256]{2,1,0:T(8,128)S(1)} %get-tuple-element.60), channel_id=1, source_target_pairs={{2,1},{3,0},{18,17},{19,16},{6,5},{7,4},{22,21},{23,20},{10,9},{11... | collective-permute-start | bytes 393224 | tf_op jit(solution)/shard_map/ppermute | solution.py:432
  58.2 0.7 %copy.11 = f32[2,2,64,256]{3,2,1,0:T(8,128)} copy(f32[2,2,64,256]{3,2,1,0:T(8,128)S(1)} %bitcast.6) | data formatting | bytes 524288
  58.9 0.7 %copy.12 = f32[2,2,64,256]{3,2,1,0:T(8,128)} copy(f32[2,2,64,256]{3,2,1,0:T(8,128)S(1)} %bitcast.5) | data formatting | bytes 524288
  59.6 1.7 %collective-permute-done.19.refs_3_ = f32[2,64,256]{2,1,0:T(8,128)S(1)} collective-permute-done((f32[2,64,256]{2,1,0:T(8,128)S(1)}, f32[2,64,256]{2,1,0:T(8,128)S(1)}, u32[]{:S(2)}, u32[]{:S(2)}) %collective-permute-start.19) | collective-permute-done | bytes 131104 | tf_op jit(solution)/shard_map/ppermute | solution.py:432
  61.3 2.2 %shard_map.111.refs_4_ = f32[2,256,256]{2,1,0:T(8,128)S(1)} custom-call(s32[1,1]{1,0:T(1,128)S(6)} %copy.13.count_ref, f32[2,64,256]{2,1,0:T(8,128)S(1)} %get-tuple-element.61.refs_0_, f32[2,64,256]{2,1,0:T(8,128)S(1)} %collective-permute-done.17.refs_1_, f32[2,64,256]{2,1,0:T(8,128)S(1)} %collective-permute-done.18.refs_2_, ...), custom_call_target="tpu_custom_call" | custom-call | tf_op jit(solution)/shard_map/pallas_call | solution.py:30
  63.5 4.8 %collective-permute-done.15.refs_2_ = f32[2,64,256]{2,1,0:T(8,128)S(1)} collective-permute-done((f32[2,64,256]{2,1,0:T(8,128)S(1)}, f32[2,64,256]{2,1,0:T(8,128)S(1)}, u32[]{:S(2)}, u32[]{:S(2)}) %collective-permute-start.15) | collective-permute-done | bytes 131104 | tf_op jit(solution)/shard_map/ppermute | solution.py:432
  68.3 1.9 %shard_map.112 = f32[1,1,1,256,256]{4,3,2,1,0:T(8,128)} custom-call(s32[1,1]{1,0:T(1,128)S(6)} %copy.13.count_ref, f32[2,64,256]{2,1,0:T(8,128)S(1)} %get-tuple-element.57.refs_0_, f32[2,64,256]{2,1,0:T(8,128)S(1)} %collective-permute-done.14.refs_1_, f32[2,64,256]{2,1,0:T(8,128)S(1)} %collective-permute-done.15.refs_2_, ...), custom_call_target="tpu_custom_call" | custom-call | tf_op jit(solution)/shard_map/pallas_call | solution.py:30
  (23 shorter events, 1.9 us)
Async XLA Ops:
  0.6 1.8 %collective-permute-start = (f32[4,64,256]{2,1,0:T(8,128)}, f32[4,64,256]{2,1,0:T(8,128)S(1)}, u32[]{:S(2)}, u32[]{:S(2)}) collective-permute-start(f32[4,64,256]{2,1,0:T(8,128)} %bitcast.12), channel_id=1, source_target_pairs={{0,16},{16,0},{1,17},{17,1},{2,18},{18,2},{3,19},{19,3},{4,20},{20... | collective-permute-start | bytes 786440 | tf_op jit(solution)/shard_map/ppermute | solution.py:419
  2.7 5.1 %collective-permute-start.1 = (f32[4,64,128]{2,1,0:T(8,128)S(1)}, f32[4,64,128]{2,1,0:T(8,128)S(1)}, u32[]{:S(2)}, u32[]{:S(2)}) collective-permute-start(f32[4,64,128]{2,1,0:T(8,128)S(1)} %shard_map.103), channel_id=1, source_target_pairs={{0,4},{4,8},{8,12},{12,28},{20,16},{24,20},{28,24},{16,0},{1,5},{5... | collective-permute-start | bytes 393224 | tf_op jit(solution)/shard_map/ppermute | solution.py:427
  7.8 1.7 %collective-permute-start.2 = (f32[4,64,128]{2,1,0:T(8,128)S(1)}, f32[4,64,128]{2,1,0:T(8,128)S(1)}, u32[]{:S(2)}, u32[]{:S(2)}) collective-permute-start(f32[4,64,128]{2,1,0:T(8,128)S(1)} %collective-permute-done.1.mine_ref), channel_id=1, source_target_pairs={{0,16},{16,0},{1,17},{17,1},{2,18},{18,2},{3,19},{19,3},{4,20},{20... | collective-permute-start | bytes 393224 | tf_op jit(solution)/shard_map/ppermute | solution.py:419
  8.3 1.2 %copy-start = (s32[1,1,4,2]{2,3,1,0:T(2,128)S(1)}, s32[1,1,4,2]{2,3,1,0:T(2,128)}, u32[]{:S(2)}) copy-start(s32[1,1,4,2]{2,3,1,0:T(2,128)} %param.13) | copy-start | bytes 100
  8.3 9.6 %collective-permute-start.6 = (f32[1,1,1,256,256]{4,3,2,1,0:T(8,128)S(1)}, f32[1,1,1,256,256]{4,3,2,1,0:T(8,128)S(1)}, u32[]{:S(2)}, u32[]{:S(2)}) collective-permute-start(f32[1,1,1,256,256]{4,3,2,1,0:T(8,128)S(1)} %get-tuple-element.44.refs_7_), channel_id=1, source_target_pairs={{0,2},{1,3},{2,0},{3,1},{4,6},{5,7},{6,4},{7,5},{8,10},{9,11},{10,... | collective-permute-start | bytes 786440 | tf_op jit(solution)/shard_map/ppermute | solution.py:435
  10.5 7.5 %collective-permute-start.3 = (f32[4,64,256]{2,1,0:T(8,128)S(1)}, f32[4,64,256]{2,1,0:T(8,128)S(1)}, u32[]{:S(2)}, u32[]{:S(2)}) collective-permute-start(f32[4,64,256]{2,1,0:T(8,128)S(1)} %get-tuple-element.38), channel_id=1, source_target_pairs={{0,1},{1,0},{18,19},{19,18},{4,5},{5,4},{22,23},{23,22},{8,9},{9,8... | collective-permute-start | bytes 786440 | tf_op jit(solution)/shard_map/ppermute | solution.py:432
  11.2 10.2 %collective-permute-start.4 = (f32[4,64,256]{2,1,0:T(8,128)S(1)}, f32[4,64,256]{2,1,0:T(8,128)S(1)}, u32[]{:S(2)}, u32[]{:S(2)}) collective-permute-start(f32[4,64,256]{2,1,0:T(8,128)S(1)} %get-tuple-element.39), channel_id=1, source_target_pairs={{2,0},{3,1},{16,18},{17,19},{0,16},{1,17},{18,2},{19,3},{6,4},{7,5... | collective-permute-start | bytes 786440 | tf_op jit(solution)/shard_map/ppermute | solution.py:432
  14.6 6.7 %collective-permute-start.5 = (f32[4,64,256]{2,1,0:T(8,128)S(1)}, f32[4,64,256]{2,1,0:T(8,128)S(1)}, u32[]{:S(2)}, u32[]{:S(2)}) collective-permute-start(f32[4,64,256]{2,1,0:T(8,128)S(1)} %get-tuple-element.40), channel_id=1, source_target_pairs={{2,1},{3,0},{16,19},{17,18},{0,16},{1,17},{18,2},{19,3},{6,5},{7,4... | collective-permute-start | bytes 786440 | tf_op jit(solution)/shard_map/ppermute | solution.py:432
  21.3 11.6 %collective-permute-start.7 = (f32[4,64,256]{2,1,0:T(8,128)S(1)}, f32[4,64,256]{2,1,0:T(8,128)S(1)}, u32[]{:S(2)}, u32[]{:S(2)}) collective-permute-start(f32[4,64,256]{2,1,0:T(8,128)S(1)} %get-tuple-element.46), channel_id=1, source_target_pairs={{1,0},{0,1},{19,18},{18,19},{5,4},{4,5},{23,22},{22,23},{9,8},{8,9... | collective-permute-start | bytes 786440 | tf_op jit(solution)/shard_map/ppermute | solution.py:432
  22.0 14.0 %collective-permute-start.8 = (f32[4,64,256]{2,1,0:T(8,128)S(1)}, f32[4,64,256]{2,1,0:T(8,128)S(1)}, u32[]{:S(2)}, u32[]{:S(2)}) collective-permute-start(f32[4,64,256]{2,1,0:T(8,128)S(1)} %get-tuple-element.47), channel_id=1, source_target_pairs={{0,2},{1,3},{18,16},{19,17},{2,18},{3,19},{16,0},{17,1},{4,6},{5,7... | collective-permute-start | bytes 786440 | tf_op jit(solution)/shard_map/ppermute | solution.py:432
  32.8 6.8 %collective-permute-start.9 = (f32[4,64,256]{2,1,0:T(8,128)S(1)}, f32[4,64,256]{2,1,0:T(8,128)S(1)}, u32[]{:S(2)}, u32[]{:S(2)}) collective-permute-start(f32[4,64,256]{2,1,0:T(8,128)S(1)} %get-tuple-element.48), channel_id=1, source_target_pairs={{1,2},{0,3},{19,16},{18,17},{2,18},{3,19},{16,0},{17,1},{5,6},{4,7... | collective-permute-start | bytes 786440 | tf_op jit(solution)/shard_map/ppermute | solution.py:432
  40.4 2.4 %collective-permute-start.10 = (f32[2,4,64,256]{3,2,1,0:T(8,128)S(1)}, f32[2,4,64,256]{3,2,1,0:T(8,128)S(1)}, u32[]{:S(2)}, u32[]{:S(2)}) collective-permute-start(f32[2,4,64,256]{3,2,1,0:T(8,128)S(1)} %get-tuple-element.50.own_ref), channel_id=1, source_target_pairs={{0,16},{16,0},{1,17},{17,1},{2,18},{18,2},{3,19},{19,3},{4,20},{20... | collective-permute-start | bytes 1572872 | tf_op jit(solution)/shard_map/ppermute | solution.py:419
  40.5 2.3 %collective-permute-start.11 = (f32[2,4,64,128]{3,2,1,0:T(8,128)S(1)}, f32[2,4,64,128]{3,2,1,0:T(8,128)S(1)}, u32[]{:S(2)}, u32[]{:S(2)}) collective-permute-start(f32[2,4,64,128]{3,2,1,0:T(8,128)S(1)} %get-tuple-element.51.halo_ref), channel_id=1, source_target_pairs={{0,16},{16,0},{1,17},{17,1},{2,18},{18,2},{3,19},{19,3},{4,20},{20... | collective-permute-start | bytes 786440 | tf_op jit(solution)/shard_map/ppermute | solution.py:419
  42.8 5.9 %collective-permute-start.12 = (f32[2,4,64,128]{3,2,1,0:T(8,128)S(1)}, f32[2,4,64,128]{3,2,1,0:T(8,128)S(1)}, u32[]{:S(2)}, u32[]{:S(2)}) collective-permute-start(f32[2,4,64,128]{3,2,1,0:T(8,128)S(1)} %get-tuple-element.54), channel_id=1, source_target_pairs={{0,4},{4,8},{8,12},{12,28},{20,16},{24,20},{28,24},{16,0},{1,5},{5... | collective-permute-start | bytes 786440 | tf_op jit(solution)/shard_map/ppermute | solution.py:427
  48.8 1.7 %collective-permute-start.13 = (f32[2,4,64,128]{3,2,1,0:T(8,128)S(1)}, f32[2,4,64,128]{3,2,1,0:T(8,128)S(1)}, u32[]{:S(2)}, u32[]{:S(2)}) collective-permute-start(f32[2,4,64,128]{3,2,1,0:T(8,128)S(1)} %collective-permute-done.12.mine_ref), channel_id=1, source_target_pairs={{0,16},{16,0},{1,17},{17,1},{2,18},{18,2},{3,19},{19,3},{4,20},{20... | collective-permute-start | bytes 786440 | tf_op jit(solution)/shard_map/ppermute | solution.py:419
  51.5 5.4 %collective-permute-start.17 = (f32[2,64,256]{2,1,0:T(8,128)S(1)}, f32[2,64,256]{2,1,0:T(8,128)S(1)}, u32[]{:S(2)}, u32[]{:S(2)}) collective-permute-start(f32[2,64,256]{2,1,0:T(8,128)S(1)} %get-tuple-element.62), channel_id=1, source_target_pairs={{0,1},{1,0},{16,17},{17,16},{2,18},{3,19},{18,2},{19,3},{4,5},{5,4... | collective-permute-start | bytes 393224 | tf_op jit(solution)/shard_map/ppermute | solution.py:432
  52.3 11.2 %collective-permute-start.14 = (f32[2,64,256]{2,1,0:T(8,128)S(1)}, f32[2,64,256]{2,1,0:T(8,128)S(1)}, u32[]{:S(2)}, u32[]{:S(2)}) collective-permute-start(f32[2,64,256]{2,1,0:T(8,128)S(1)} %get-tuple-element.58), channel_id=1, source_target_pairs={{0,1},{1,0},{16,17},{17,16},{2,18},{3,19},{18,2},{19,3},{4,5},{5,4... | collective-permute-start | bytes 393224 | tf_op jit(solution)/shard_map/ppermute | solution.py:432
  53.0 6.6 %collective-permute-start.18 = (f32[2,64,256]{2,1,0:T(8,128)S(1)}, f32[2,64,256]{2,1,0:T(8,128)S(1)}, u32[]{:S(2)}, u32[]{:S(2)}) collective-permute-start(f32[2,64,256]{2,1,0:T(8,128)S(1)} %get-tuple-element.63), channel_id=1, source_target_pairs={{2,0},{3,1},{18,16},{19,17},{6,4},{7,5},{22,20},{23,21},{10,8},{11... | collective-permute-start | bytes 393224 | tf_op jit(solution)/shard_map/ppermute | solution.py:432
  54.3 7.0 %collective-permute-start.19 = (f32[2,64,256]{2,1,0:T(8,128)S(1)}, f32[2,64,256]{2,1,0:T(8,128)S(1)}, u32[]{:S(2)}, u32[]{:S(2)}) collective-permute-start(f32[2,64,256]{2,1,0:T(8,128)S(1)} %get-tuple-element.64), channel_id=1, source_target_pairs={{2,1},{3,0},{18,17},{19,16},{6,5},{7,4},{22,21},{23,20},{10,9},{11... | collective-permute-start | bytes 393224 | tf_op jit(solution)/shard_map/ppermute | solution.py:432
  55.6 12.7 %collective-permute-start.15 = (f32[2,64,256]{2,1,0:T(8,128)S(1)}, f32[2,64,256]{2,1,0:T(8,128)S(1)}, u32[]{:S(2)}, u32[]{:S(2)}) collective-permute-start(f32[2,64,256]{2,1,0:T(8,128)S(1)} %get-tuple-element.59), channel_id=1, source_target_pairs={{2,0},{3,1},{18,16},{19,17},{6,4},{7,5},{22,20},{23,21},{10,8},{11... | collective-permute-start | bytes 393224 | tf_op jit(solution)/shard_map/ppermute | solution.py:432
  56.9 11.4 %collective-permute-start.16 = (f32[2,64,256]{2,1,0:T(8,128)S(1)}, f32[2,64,256]{2,1,0:T(8,128)S(1)}, u32[]{:S(2)}, u32[]{:S(2)}) collective-permute-start(f32[2,64,256]{2,1,0:T(8,128)S(1)} %get-tuple-element.60), channel_id=1, source_target_pairs={{2,1},{3,0},{18,17},{19,16},{6,5},{7,4},{22,21},{23,20},{10,9},{11... | collective-permute-start | bytes 393224 | tf_op jit(solution)/shard_map/ppermute | solution.py:432

commit v4 on v3

--- a/solution.py
+++ b/solution.py
@@ -199,8 +199,10 @@
     return body
 
 
-def load(*arrays):
+def move(target, *arrays):
     count = len(arrays)
+    inward = target is pltpu.VMEM
+    here, there = vmem(), pl.BlockSpec(memory_space=pl.ANY)
 
     def body(*refs):
         sources, targets, sems = refs[:count], refs[count : 2 * count], refs[2 * count]
@@ -212,13 +214,12 @@
 
     return pl.pallas_call(
         body,
-        out_shape=tuple(pltpu.VMEM(x.shape, x.dtype) for x in arrays),
-        in_specs=[pl.BlockSpec(memory_space=pl.ANY)] * count,
-        out_specs=tuple(vmem() for _ in arrays),
+        out_shape=tuple(target(x.shape, x.dtype) for x in arrays),
+        in_specs=[there if inward else here] * count,
+        out_specs=tuple(here if inward else there for _ in arrays),
         scratch_shapes=[pltpu.SemaphoreType.DMA((count,))],
-        name="load_kernel",
         compiler_params=pltpu.CompilerParams(vmem_limit_bytes=2 * 1024 * 1024),
-    )(*[pltpu.with_memory_space_constraint(x, pltpu.HBM) for x in arrays])
+    )(*[pltpu.with_memory_space_constraint(x, pltpu.HBM if inward else pltpu.VMEM) for x in arrays])
 
 
 def kernel_slab(phase_ref, slab_ref):
@@ -418,8 +419,8 @@
     tab = jnp.asarray(dft_tables(t))
     cores = lambda x: lax.ppermute(x, "ty", [(0, 1), (1, 0)])
     partner = cores(own)
-    own, velocity_old, measured, illumination, slab_phase, tab = load(
-        own, velocity_old, measured, illumination, slab_phase, tab
+    own, velocity_old, measured, illumination, slab_phase, tab = move(
+        pltpu.VMEM, own, velocity_old, measured, illumination, slab_phase, tab
     )
     ntx = lay.ntx
     shift = [(b, b + 1) for b in range(ntx - 1)] + [(ntx - 1, 2 * ntx - 1)]
@@ -471,6 +472,7 @@
     )
     first = exchange(rest[:n], lambda s: lay.inward(s, True))
     second = exchange(rest[n : 2 * n], lambda s: lay.inward(s, True))
+    updated, velocity = move(pltpu.HBM, updated, velocity)
     half_window = pltpu.VMEM((2, t, t), F32)
     (between,) = call(
         kernel_between(lay), [(2, t, t)], [entry_counts, *first, light, slab, tab], 1, [half_window], limit=24

time: 71.4 us -> 71.4 us (level)
  local copies, waits for them, and re-layouts: 1.41 us -> 0.01 us
  Pallas kernels: 11.4 us -> 12.2 us
    unnamed x4 -> x2, local copies, waits for them, and re-layouts: 1.41 us -> 0.01 us
    pallas_call x1 -> x2, Pallas kernels: 1.66 us -> 2.47 us  [move(): pl.pallas_call(body, out_shape=tuple((target(x.shape, x.dtype) for x in a...]
  transfers between devices with their start and end apart: 20 -> 20, of which waited for: 10 -> 10; matrix products, arithmetic and copies ran while one was open for 2% -> 0% of each run, Pallas kernels for 10% -> 12%
where the time goes in v4:
time: 71.4 us; the launch traced here: 70.2 us
  waiting for transfers between devices  30.5 us (43%)
  starting transfers between devices  26 us (36%)
  Pallas kernels  12.2 us (17%)
  between operations  1.45 us (2%)
    ppermute x12, starting transfers between devices, exchange(): got.append(lax.ppermute(values[s], ('ty', 'pos'), complete(pairs_of(s), n)))  22.4 us
    ppermute x12, waiting for transfers between devices, exchange(): got.append(lax.ppermute(values[s], ('ty', 'pos'), complete(pairs_of(s), n)))  17.1 us
    ppermute x2, waiting for transfers between devices, iteration(): columns = lambda x: lax.ppermute(x, ('ty', 'tx'), shift)  10.4 us
    pallas_call x10, Pallas kernels, call(): pl.pallas_call(body, out_shape=tuple(((jax.ShapeDtypeStruct if last else...  9.73 us
    ppermute x5, waiting for transfers between devices, iteration(): cores = lambda x: lax.ppermute(x, 'ty', [(0, 1), (1, 0)])  3 us
    pallas_call x2, Pallas kernels, move(): pl.pallas_call(body, out_shape=tuple((target(x.shape, x.dtype) for x in a...  2.47 us
    ppermute x5, starting transfers between devices, iteration(): cores = lambda x: lax.ppermute(x, 'ty', [(0, 1), (1, 0)])  1.71 us
  transfers between devices with their start and end apart: 20, of which 10 were waited for; matrix products, arithmetic and copies ran while one was open for 0% of the time, Pallas kernels for 12%

profile of v4, /device:TPU:1, one launch (start us, length us, event | category | flops | bytes accessed | tf_op | source)
XLA Modules:
  0.0 70.2 jit_solution(8264142282153757904)
XLA Ops:
  0.7 1.7 %shard_map.103 = (f32[4,64,256]{2,1,0:T(8,128)S(1)}, f32[4,64,256]{2,1,0:T(8,128)S(1)}, f32[1,1,1,256,256]{4,3,2,1,0:T(8,128)S(1)}, f32[2,256,256]{2,1,0:T(8,128...) custom-call(f32[4,64,256]{2,1,0:T(8,128)} %bitcast.11, f32[4,64,256]{2,1,0:T(8,128)} %bitcast.9, ...), custom_call_target="tpu_custom_call" | custom-call | tf_op jit(solution)/shard_map/pallas_call | solution.py:215
  3.2 4.6 %collective-permute-done.1.mine_ref = f32[4,64,128]{2,1,0:T(8,128)S(1)} collective-permute-done((f32[4,64,128]{2,1,0:T(8,128)S(1)}, f32[4,64,128]{2,1,0:T(8,128)S(1)}, u32[]{:S(2)}, u32[]{:S(2)}) %collective-permute-start.1) | collective-permute-done | bytes 131104 | tf_op jit(solution)/shard_map/ppermute | solution.py:428
  7.8 0.5 collective-permute-start.2
  8.3 1.2 %collective-permute-start.6 = (f32[1,1,1,256,256]{4,3,2,1,0:T(8,128)S(1)}, f32[1,1,1,256,256]{4,3,2,1,0:T(8,128)S(1)}, u32[]{:S(2)}, u32[]{:S(2)}) collective-permute-start(f32[1,1,1,256,256]{4,3,2,1,0:T(8,128)S(1)} %get-tuple-element.46.refs_7_), channel_id=1, source_target_pairs={{0,2},{1,3},{2,0},{3,1},{4,6},{5,7},{6,4},{7,5},{8,10},{9,11},{10,... | collective-permute-start | bytes 786440 | tf_op jit(solution)/shard_map/ppermute | solution.py:436
  9.6 0.9 %shard_map.105 = (f32[4,64,256]{2,1,0:T(8,128)S(1)}, f32[4,64,256]{2,1,0:T(8,128)S(1)}, f32[4,64,256]{2,1,0:T(8,128)S(1)}, f32[4,64,256]{2,1,0:T(8,128)S(1)}, f3...) custom-call(s32[1,1,2,4]{3,2,1,0:T(2,128)S(1)} %bitcast.5, f32[4,64,256]{2,1,0:T(8,128)S(1)} %get-tuple-element.36.own_ref.obj_ref, ...), custom_call_target="tpu_custom_call" | custom-call | tf_op jit(solution)/shard_map/pallas_call | solution.py:30
  10.5 0.7 collective-permute-start.3
  11.2 3.5 %collective-permute-start.4 = (f32[4,64,256]{2,1,0:T(8,128)S(1)}, f32[4,64,256]{2,1,0:T(8,128)S(1)}, u32[]{:S(2)}, u32[]{:S(2)}) collective-permute-start(f32[4,64,256]{2,1,0:T(8,128)S(1)} %get-tuple-element.41), channel_id=1, source_target_pairs={{2,0},{3,1},{16,18},{17,19},{0,16},{1,17},{18,2},{19,3},{6,4},{7,5... | collective-permute-start | bytes 786440 | tf_op jit(solution)/shard_map/ppermute | solution.py:433
  15.3 1.0 %shard_map.106.refs_4_ = f32[2,2,256,256]{3,2,1,0:T(8,128)S(1)} custom-call(s32[1,1,2,4]{3,2,1,0:T(2,128)S(1)} %bitcast.6, f32[2,256,256]{2,1,0:T(8,128)S(1)} %get-tuple-element.43.light_ref), custom_call_target="tpu_custom_call" | custom-call | tf_op jit(solution)/shard_map/pallas_call | solution.py:30
  16.3 1.7 %shard_map.107.refs_5_ = f32[2,256,256]{2,1,0:T(8,128)S(1)} custom-call(f32[256,256]{1,0:T(8,128)S(1)} %get-tuple-element.44.phase_ref), custom_call_target="tpu_custom_call" | custom-call | tf_op jit(solution)/shard_map/pallas_call | solution.py:30
  18.0 3.3 %collective-permute-done.4.refs_2_ = f32[4,64,256]{2,1,0:T(8,128)S(1)} collective-permute-done((f32[4,64,256]{2,1,0:T(8,128)S(1)}, f32[4,64,256]{2,1,0:T(8,128)S(1)}, u32[]{:S(2)}, u32[]{:S(2)}) %collective-permute-start.4) | collective-permute-done | bytes 262176 | tf_op jit(solution)/shard_map/ppermute | solution.py:433
  21.3 0.7 collective-permute-start.7
  22.0 10.8 %collective-permute-start.8 = (f32[4,64,256]{2,1,0:T(8,128)S(1)}, f32[4,64,256]{2,1,0:T(8,128)S(1)}, u32[]{:S(2)}, u32[]{:S(2)}) collective-permute-start(f32[4,64,256]{2,1,0:T(8,128)S(1)} %get-tuple-element.49), channel_id=1, source_target_pairs={{0,2},{1,3},{18,16},{19,17},{2,18},{3,19},{16,0},{17,1},{4,6},{5,7... | collective-permute-start | bytes 786440 | tf_op jit(solution)/shard_map/ppermute | solution.py:433
  32.9 3.0 %collective-permute-done.8.refs_2_ = f32[4,64,256]{2,1,0:T(8,128)S(1)} collective-permute-done((f32[4,64,256]{2,1,0:T(8,128)S(1)}, f32[4,64,256]{2,1,0:T(8,128)S(1)}, u32[]{:S(2)}, u32[]{:S(2)}) %collective-permute-start.8) | collective-permute-done | bytes 262176 | tf_op jit(solution)/shard_map/ppermute | solution.py:433
  36.0 3.6 %collective-permute-done.9.refs_3_ = f32[4,64,256]{2,1,0:T(8,128)S(1)} collective-permute-done((f32[4,64,256]{2,1,0:T(8,128)S(1)}, f32[4,64,256]{2,1,0:T(8,128)S(1)}, u32[]{:S(2)}, u32[]{:S(2)}) %collective-permute-start.9) | collective-permute-done | bytes 262176 | tf_op jit(solution)/shard_map/ppermute | solution.py:433
  39.6 0.8 %shard_map.109 = (f32[2,4,64,256]{3,2,1,0:T(8,128)S(1)}, f32[2,4,64,128]{3,2,1,0:T(8,128)S(1)}) custom-call(s32[1,1,2,4]{3,2,1,0:T(2,128)S(1)} %bitcast.7, s32[1,1]{1,0:T(1,128)S(6)} %copy.11.count_ref, f32[4,64,256]{2,1,0:T(8,128)S(1)} %get-tuple-element.47.refs_0_, f32[4,64,256]{2,1,0:T(8,128)S(1)} %collective-permute-done.7.refs_1_, ...), custom_call_target="tpu_custom_call" | custom-call | tf_op jit(solution)/shard_map/pallas_call | solution.py:30
  40.5 0.5 collective-permute-start.11
  40.9 1.8 %collective-permute-done.11.their_halo_ref = f32[2,4,64,128]{3,2,1,0:T(8,128)S(1)} collective-permute-done((f32[2,4,64,128]{3,2,1,0:T(8,128)S(1)}, f32[2,4,64,128]{3,2,1,0:T(8,128)S(1)}, u32[]{:S(2)}, u32[]{:S(2)}) %collective-permute-start.11) | collective-permute-done | bytes 262176 | tf_op jit(solution)/shard_map/ppermute | solution.py:420
  43.0 5.8 %collective-permute-done.12.mine_ref = f32[2,4,64,128]{3,2,1,0:T(8,128)S(1)} collective-permute-done((f32[2,4,64,128]{3,2,1,0:T(8,128)S(1)}, f32[2,4,64,128]{3,2,1,0:T(8,128)S(1)}, u32[]{:S(2)}, u32[]{:S(2)}) %collective-permute-start.12) | collective-permute-done | bytes 262176 | tf_op jit(solution)/shard_map/ppermute | solution.py:428
  48.8 0.6 collective-permute-start.13
  49.3 1.2 %collective-permute-done.13.theirs_ref = f32[2,4,64,128]{3,2,1,0:T(8,128)S(1)} collective-permute-done((f32[2,4,64,128]{3,2,1,0:T(8,128)S(1)}, f32[2,4,64,128]{3,2,1,0:T(8,128)S(1)}, u32[]{:S(2)}, u32[]{:S(2)}) %collective-permute-start.13) | collective-permute-done | bytes 262176 | tf_op jit(solution)/shard_map/ppermute | solution.py:420
  50.5 1.0 %shard_map.111 = (f32[4,64,256]{2,1,0:T(8,128)S(1)}, f32[4,64,256]{2,1,0:T(8,128)S(1)}, f32[2,64,256]{2,1,0:T(8,128)S(1)}, f32[2,64,256]{2,1,0:T(8,128)S(1)}, f3...) custom-call(s32[1,1,2,4]{3,2,1,0:T(2,128)S(1)} %bitcast.8, ...), custom_call_target="tpu_custom_call" | custom-call | tf_op jit(solution)/shard_map/pallas_call | solution.py:30
  51.5 0.8 %collective-permute-start.17 = (f32[2,64,256]{2,1,0:T(8,128)S(1)}, f32[2,64,256]{2,1,0:T(8,128)S(1)}, u32[]{:S(2)}, u32[]{:S(2)}) collective-permute-start(f32[2,64,256]{2,1,0:T(8,128)S(1)} %get-tuple-element.66), channel_id=1, source_target_pairs={{0,1},{1,0},{16,17},{17,16},{2,18},{3,19},{18,2},{19,3},{4,5},{5,4... | collective-permute-start | bytes 393224 | tf_op jit(solution)/shard_map/ppermute | solution.py:433
  52.3 0.7 collective-permute-start.14
  53.0 1.3 %collective-permute-start.18 = (f32[2,64,256]{2,1,0:T(8,128)S(1)}, f32[2,64,256]{2,1,0:T(8,128)S(1)}, u32[]{:S(2)}, u32[]{:S(2)}) collective-permute-start(f32[2,64,256]{2,1,0:T(8,128)S(1)} %get-tuple-element.67), channel_id=1, source_target_pairs={{2,0},{3,1},{18,16},{19,17},{6,4},{7,5},{22,20},{23,21},{10,8},{11... | collective-permute-start | bytes 393224 | tf_op jit(solution)/shard_map/ppermute | solution.py:433
  54.3 1.3 %collective-permute-start.19 = (f32[2,64,256]{2,1,0:T(8,128)S(1)}, f32[2,64,256]{2,1,0:T(8,128)S(1)}, u32[]{:S(2)}, u32[]{:S(2)}) collective-permute-start(f32[2,64,256]{2,1,0:T(8,128)S(1)} %get-tuple-element.68), channel_id=1, source_target_pairs={{2,1},{3,0},{18,17},{19,16},{6,5},{7,4},{22,21},{23,20},{10,9},{11... | collective-permute-start | bytes 393224 | tf_op jit(solution)/shard_map/ppermute | solution.py:433
  55.6 1.3 %collective-permute-start.15 = (f32[2,64,256]{2,1,0:T(8,128)S(1)}, f32[2,64,256]{2,1,0:T(8,128)S(1)}, u32[]{:S(2)}, u32[]{:S(2)}) collective-permute-start(f32[2,64,256]{2,1,0:T(8,128)S(1)} %get-tuple-element.63), channel_id=1, source_target_pairs={{2,0},{3,1},{18,16},{19,17},{6,4},{7,5},{22,20},{23,21},{10,8},{11... | collective-permute-start | bytes 393224 | tf_op jit(solution)/shard_map/ppermute | solution.py:433
  56.9 1.3 %collective-permute-start.16 = (f32[2,64,256]{2,1,0:T(8,128)S(1)}, f32[2,64,256]{2,1,0:T(8,128)S(1)}, u32[]{:S(2)}, u32[]{:S(2)}) collective-permute-start(f32[2,64,256]{2,1,0:T(8,128)S(1)} %get-tuple-element.64), channel_id=1, source_target_pairs={{2,1},{3,0},{18,17},{19,16},{6,5},{7,4},{22,21},{23,20},{10,9},{11... | collective-permute-start | bytes 393224 | tf_op jit(solution)/shard_map/ppermute | solution.py:433
  58.2 0.8 %shard_map.112 = (f32[4,64,256]{2,1,0:T(8,128)}, f32[4,64,256]{2,1,0:T(8,128)}) custom-call(f32[4,64,256]{2,1,0:T(8,128)S(1)} %get-tuple-element.57.refs_0_, f32[4,64,256]{2,1,0:T(8,128)S(1)} %get-tuple-element.58.refs_1_), custom_call_target="tpu_custom_call" | custom-call | tf_op jit(solution)/shard_map/pallas_call | solution.py:215
  59.0 2.3 %collective-permute-done.19.refs_3_ = f32[2,64,256]{2,1,0:T(8,128)S(1)} collective-permute-done((f32[2,64,256]{2,1,0:T(8,128)S(1)}, f32[2,64,256]{2,1,0:T(8,128)S(1)}, u32[]{:S(2)}, u32[]{:S(2)}) %collective-permute-start.19) | collective-permute-done | bytes 131104 | tf_op jit(solution)/shard_map/ppermute | solution.py:433
  61.3 2.2 %shard_map.113.refs_4_ = f32[2,256,256]{2,1,0:T(8,128)S(1)} custom-call(s32[1,1]{1,0:T(1,128)S(6)} %copy.11.count_ref, f32[2,64,256]{2,1,0:T(8,128)S(1)} %get-tuple-element.65.refs_0_, f32[2,64,256]{2,1,0:T(8,128)S(1)} %collective-permute-done.17.refs_1_, f32[2,64,256]{2,1,0:T(8,128)S(1)} %collective-permute-done.18.refs_2_, ...), custom_call_target="tpu_custom_call" | custom-call | tf_op jit(solution)/shard_map/pallas_call | solution.py:30
  63.5 4.8 %collective-permute-done.15.refs_2_ = f32[2,64,256]{2,1,0:T(8,128)S(1)} collective-permute-done((f32[2,64,256]{2,1,0:T(8,128)S(1)}, f32[2,64,256]{2,1,0:T(8,128)S(1)}, u32[]{:S(2)}, u32[]{:S(2)}) %collective-permute-start.15) | collective-permute-done | bytes 131104 | tf_op jit(solution)/shard_map/ppermute | solution.py:433
  68.3 1.9 %shard_map.114 = f32[1,1,1,256,256]{4,3,2,1,0:T(8,128)} custom-call(s32[1,1]{1,0:T(1,128)S(6)} %copy.11.count_ref, f32[2,64,256]{2,1,0:T(8,128)S(1)} %get-tuple-element.61.refs_0_, f32[2,64,256]{2,1,0:T(8,128)S(1)} %collective-permute-done.14.refs_1_, f32[2,64,256]{2,1,0:T(8,128)S(1)} %collective-permute-done.15.refs_2_, ...), custom_call_target="tpu_custom_call" | custom-call | tf_op jit(solution)/shard_map/pallas_call | solution.py:30
  (22 shorter events, 1.4 us)
Async XLA Ops:
  0.6 1.8 %collective-permute-start = (f32[4,64,256]{2,1,0:T(8,128)}, f32[4,64,256]{2,1,0:T(8,128)S(1)}, u32[]{:S(2)}, u32[]{:S(2)}) collective-permute-start(f32[4,64,256]{2,1,0:T(8,128)} %bitcast.10), channel_id=1, source_target_pairs={{0,16},{16,0},{1,17},{17,1},{2,18},{18,2},{3,19},{19,3},{4,20},{20... | collective-permute-start | bytes 786440 | tf_op jit(solution)/shard_map/ppermute | solution.py:420
  2.7 5.1 %collective-permute-start.1 = (f32[4,64,128]{2,1,0:T(8,128)S(1)}, f32[4,64,128]{2,1,0:T(8,128)S(1)}, u32[]{:S(2)}, u32[]{:S(2)}) collective-permute-start(f32[4,64,128]{2,1,0:T(8,128)S(1)} %shard_map.104), channel_id=1, source_target_pairs={{0,4},{4,8},{8,12},{12,28},{20,16},{24,20},{28,24},{16,0},{1,5},{5... | collective-permute-start | bytes 393224 | tf_op jit(solution)/shard_map/ppermute | solution.py:428
  7.8 1.7 %collective-permute-start.2 = (f32[4,64,128]{2,1,0:T(8,128)S(1)}, f32[4,64,128]{2,1,0:T(8,128)S(1)}, u32[]{:S(2)}, u32[]{:S(2)}) collective-permute-start(f32[4,64,128]{2,1,0:T(8,128)S(1)} %collective-permute-done.1.mine_ref), channel_id=1, source_target_pairs={{0,16},{16,0},{1,17},{17,1},{2,18},{18,2},{3,19},{19,3},{4,20},{20... | collective-permute-start | bytes 393224 | tf_op jit(solution)/shard_map/ppermute | solution.py:420
  8.3 1.2 %copy-start = (s32[1,1,4,2]{2,3,1,0:T(2,128)S(1)}, s32[1,1,4,2]{2,3,1,0:T(2,128)}, u32[]{:S(2)}) copy-start(s32[1,1,4,2]{2,3,1,0:T(2,128)} %param.13) | copy-start | bytes 100
  8.3 9.6 %collective-permute-start.6 = (f32[1,1,1,256,256]{4,3,2,1,0:T(8,128)S(1)}, f32[1,1,1,256,256]{4,3,2,1,0:T(8,128)S(1)}, u32[]{:S(2)}, u32[]{:S(2)}) collective-permute-start(f32[1,1,1,256,256]{4,3,2,1,0:T(8,128)S(1)} %get-tuple-element.46.refs_7_), channel_id=1, source_target_pairs={{0,2},{1,3},{2,0},{3,1},{4,6},{5,7},{6,4},{7,5},{8,10},{9,11},{10,... | collective-permute-start | bytes 786440 | tf_op jit(solution)/shard_map/ppermute | solution.py:436
  10.5 7.5 %collective-permute-start.3 = (f32[4,64,256]{2,1,0:T(8,128)S(1)}, f32[4,64,256]{2,1,0:T(8,128)S(1)}, u32[]{:S(2)}, u32[]{:S(2)}) collective-permute-start(f32[4,64,256]{2,1,0:T(8,128)S(1)} %get-tuple-element.40), channel_id=1, source_target_pairs={{0,1},{1,0},{18,19},{19,18},{4,5},{5,4},{22,23},{23,22},{8,9},{9,8... | collective-permute-start | bytes 786440 | tf_op jit(solution)/shard_map/ppermute | solution.py:433
  11.2 10.2 %collective-permute-start.4 = (f32[4,64,256]{2,1,0:T(8,128)S(1)}, f32[4,64,256]{2,1,0:T(8,128)S(1)}, u32[]{:S(2)}, u32[]{:S(2)}) collective-permute-start(f32[4,64,256]{2,1,0:T(8,128)S(1)} %get-tuple-element.41), channel_id=1, source_target_pairs={{2,0},{3,1},{16,18},{17,19},{0,16},{1,17},{18,2},{19,3},{6,4},{7,5... | collective-permute-start | bytes 786440 | tf_op jit(solution)/shard_map/ppermute | solution.py:433
  14.6 6.7 %collective-permute-start.5 = (f32[4,64,256]{2,1,0:T(8,128)S(1)}, f32[4,64,256]{2,1,0:T(8,128)S(1)}, u32[]{:S(2)}, u32[]{:S(2)}) collective-permute-start(f32[4,64,256]{2,1,0:T(8,128)S(1)} %get-tuple-element.42), channel_id=1, source_target_pairs={{2,1},{3,0},{16,19},{17,18},{0,16},{1,17},{18,2},{19,3},{6,5},{7,4... | collective-permute-start | bytes 786440 | tf_op jit(solution)/shard_map/ppermute | solution.py:433
  21.3 11.6 %collective-permute-start.7 = (f32[4,64,256]{2,1,0:T(8,128)S(1)}, f32[4,64,256]{2,1,0:T(8,128)S(1)}, u32[]{:S(2)}, u32[]{:S(2)}) collective-permute-start(f32[4,64,256]{2,1,0:T(8,128)S(1)} %get-tuple-element.48), channel_id=1, source_target_pairs={{1,0},{0,1},{19,18},{18,19},{5,4},{4,5},{23,22},{22,23},{9,8},{8,9... | collective-permute-start | bytes 786440 | tf_op jit(solution)/shard_map/ppermute | solution.py:433
  22.0 14.0 %collective-permute-start.8 = (f32[4,64,256]{2,1,0:T(8,128)S(1)}, f32[4,64,256]{2,1,0:T(8,128)S(1)}, u32[]{:S(2)}, u32[]{:S(2)}) collective-permute-start(f32[4,64,256]{2,1,0:T(8,128)S(1)} %get-tuple-element.49), channel_id=1, source_target_pairs={{0,2},{1,3},{18,16},{19,17},{2,18},{3,19},{16,0},{17,1},{4,6},{5,7... | collective-permute-start | bytes 786440 | tf_op jit(solution)/shard_map/ppermute | solution.py:433
  32.8 6.8 %collective-permute-start.9 = (f32[4,64,256]{2,1,0:T(8,128)S(1)}, f32[4,64,256]{2,1,0:T(8,128)S(1)}, u32[]{:S(2)}, u32[]{:S(2)}) collective-permute-start(f32[4,64,256]{2,1,0:T(8,128)S(1)} %get-tuple-element.50), channel_id=1, source_target_pairs={{1,2},{0,3},{19,16},{18,17},{2,18},{3,19},{16,0},{17,1},{5,6},{4,7... | collective-permute-start | bytes 786440 | tf_op jit(solution)/shard_map/ppermute | solution.py:433
  40.4 2.4 %collective-permute-start.10 = (f32[2,4,64,256]{3,2,1,0:T(8,128)S(1)}, f32[2,4,64,256]{3,2,1,0:T(8,128)S(1)}, u32[]{:S(2)}, u32[]{:S(2)}) collective-permute-start(f32[2,4,64,256]{3,2,1,0:T(8,128)S(1)} %get-tuple-element.52.own_ref), channel_id=1, source_target_pairs={{0,16},{16,0},{1,17},{17,1},{2,18},{18,2},{3,19},{19,3},{4,20},{20... | collective-permute-start | bytes 1572872 | tf_op jit(solution)/shard_map/ppermute | solution.py:420
  40.5 2.3 %collective-permute-start.11 = (f32[2,4,64,128]{3,2,1,0:T(8,128)S(1)}, f32[2,4,64,128]{3,2,1,0:T(8,128)S(1)}, u32[]{:S(2)}, u32[]{:S(2)}) collective-permute-start(f32[2,4,64,128]{3,2,1,0:T(8,128)S(1)} %get-tuple-element.53.halo_ref), channel_id=1, source_target_pairs={{0,16},{16,0},{1,17},{17,1},{2,18},{18,2},{3,19},{19,3},{4,20},{20... | collective-permute-start | bytes 786440 | tf_op jit(solution)/shard_map/ppermute | solution.py:420
  42.8 5.9 %collective-permute-start.12 = (f32[2,4,64,128]{3,2,1,0:T(8,128)S(1)}, f32[2,4,64,128]{3,2,1,0:T(8,128)S(1)}, u32[]{:S(2)}, u32[]{:S(2)}) collective-permute-start(f32[2,4,64,128]{3,2,1,0:T(8,128)S(1)} %get-tuple-element.56), channel_id=1, source_target_pairs={{0,4},{4,8},{8,12},{12,28},{20,16},{24,20},{28,24},{16,0},{1,5},{5... | collective-permute-start | bytes 786440 | tf_op jit(solution)/shard_map/ppermute | solution.py:428
  48.8 1.7 %collective-permute-start.13 = (f32[2,4,64,128]{3,2,1,0:T(8,128)S(1)}, f32[2,4,64,128]{3,2,1,0:T(8,128)S(1)}, u32[]{:S(2)}, u32[]{:S(2)}) collective-permute-start(f32[2,4,64,128]{3,2,1,0:T(8,128)S(1)} %collective-permute-done.12.mine_ref), channel_id=1, source_target_pairs={{0,16},{16,0},{1,17},{17,1},{2,18},{18,2},{3,19},{19,3},{4,20},{20... | collective-permute-start | bytes 786440 | tf_op jit(solution)/shard_map/ppermute | solution.py:420
  51.5 5.4 %collective-permute-start.17 = (f32[2,64,256]{2,1,0:T(8,128)S(1)}, f32[2,64,256]{2,1,0:T(8,128)S(1)}, u32[]{:S(2)}, u32[]{:S(2)}) collective-permute-start(f32[2,64,256]{2,1,0:T(8,128)S(1)} %get-tuple-element.66), channel_id=1, source_target_pairs={{0,1},{1,0},{16,17},{17,16},{2,18},{3,19},{18,2},{19,3},{4,5},{5,4... | collective-permute-start | bytes 393224 | tf_op jit(solution)/shard_map/ppermute | solution.py:433
  52.3 11.2 %collective-permute-start.14 = (f32[2,64,256]{2,1,0:T(8,128)S(1)}, f32[2,64,256]{2,1,0:T(8,128)S(1)}, u32[]{:S(2)}, u32[]{:S(2)}) collective-permute-start(f32[2,64,256]{2,1,0:T(8,128)S(1)} %get-tuple-element.62), channel_id=1, source_target_pairs={{0,1},{1,0},{16,17},{17,16},{2,18},{3,19},{18,2},{19,3},{4,5},{5,4... | collective-permute-start | bytes 393224 | tf_op jit(solution)/shard_map/ppermute | solution.py:433
  53.0 6.0 %collective-permute-start.18 = (f32[2,64,256]{2,1,0:T(8,128)S(1)}, f32[2,64,256]{2,1,0:T(8,128)S(1)}, u32[]{:S(2)}, u32[]{:S(2)}) collective-permute-start(f32[2,64,256]{2,1,0:T(8,128)S(1)} %get-tuple-element.67), channel_id=1, source_target_pairs={{2,0},{3,1},{18,16},{19,17},{6,4},{7,5},{22,20},{23,21},{10,8},{11... | collective-permute-start | bytes 393224 | tf_op jit(solution)/shard_map/ppermute | solution.py:433
  54.3 7.0 %collective-permute-start.19 = (f32[2,64,256]{2,1,0:T(8,128)S(1)}, f32[2,64,256]{2,1,0:T(8,128)S(1)}, u32[]{:S(2)}, u32[]{:S(2)}) collective-permute-start(f32[2,64,256]{2,1,0:T(8,128)S(1)} %get-tuple-element.68), channel_id=1, source_target_pairs={{2,1},{3,0},{18,17},{19,16},{6,5},{7,4},{22,21},{23,20},{10,9},{11... | collective-permute-start | bytes 393224 | tf_op jit(solution)/shard_map/ppermute | solution.py:433
  55.6 12.7 %collective-permute-start.15 = (f32[2,64,256]{2,1,0:T(8,128)S(1)}, f32[2,64,256]{2,1,0:T(8,128)S(1)}, u32[]{:S(2)}, u32[]{:S(2)}) collective-permute-start(f32[2,64,256]{2,1,0:T(8,128)S(1)} %get-tuple-element.63), channel_id=1, source_target_pairs={{2,0},{3,1},{18,16},{19,17},{6,4},{7,5},{22,20},{23,21},{10,8},{11... | collective-permute-start | bytes 393224 | tf_op jit(solution)/shard_map/ppermute | solution.py:433
  56.9 11.4 %collective-permute-start.16 = (f32[2,64,256]{2,1,0:T(8,128)S(1)}, f32[2,64,256]{2,1,0:T(8,128)S(1)}, u32[]{:S(2)}, u32[]{:S(2)}) collective-permute-start(f32[2,64,256]{2,1,0:T(8,128)S(1)} %get-tuple-element.64), channel_id=1, source_target_pairs={{2,1},{3,0},{18,17},{19,16},{6,5},{7,4},{22,21},{23,20},{10,9},{11... | collective-permute-start | bytes 393224 | tf_op jit(solution)/shard_map/ppermute | solution.py:433

commit v5 on v4

--- a/solution.py
+++ b/solution.py
@@ -73,11 +73,10 @@
     plus, minus = ((tab[4], tab[5]), (tab[2], tab[3])) if inverse else ((tab[2], tab[3]), (tab[4], tab[5]))
     both = mul3(split(real + imag), cos)
     right_imag = both - mul3(split(real), plus)
+    left_low = mul3(minus, split(right_imag))
     right_real = both - mul3(split(imag), minus)
     both = mul3(cos, split(right_real + right_imag))
-    left_imag = both - mul3(plus, split(right_real))
-    left_real = both - mul3(minus, split(right_imag))
-    return left_real, left_imag
+    return both - left_low, both - mul3(plus, split(right_real))
 
 
 def cmul(ar, ai, br, bi):

time: 71.4 us -> 70 us (0.980)
  starting transfers between devices: 26 us -> 24.8 us
    ppermute x12, starting transfers between devices: 22.4 us -> 21.2 us  [exchange(): got.append(lax.ppermute(values[s], ('ty', 'pos'), complete(pairs_of(s), n)))]
  transfers between devices with their start and end apart: 20 -> 20, of which waited for: 10 -> 10; matrix products, arithmetic and copies ran while one was open for 0% -> 0% of each run, Pallas kernels for 12% -> 11%
where the time goes in v5:
time: 70 us; the launch traced here: 68.8 us
  waiting for transfers between devices  31 us (44%)
  starting transfers between devices  24.8 us (35%)
  Pallas kernels  11.6 us (17%)
  between operations  1.45 us (2%)
    ppermute x12, starting transfers between devices, exchange(): got.append(lax.ppermute(values[s], ('ty', 'pos'), complete(pairs_of(s), n)))  21.2 us
    ppermute x12, waiting for transfers between devices, exchange(): got.append(lax.ppermute(values[s], ('ty', 'pos'), complete(pairs_of(s), n)))  17.5 us
    ppermute x2, waiting for transfers between devices, iteration(): columns = lambda x: lax.ppermute(x, ('ty', 'tx'), shift)  10.4 us
    pallas_call x10, Pallas kernels, call(): pl.pallas_call(body, out_shape=tuple(((jax.ShapeDtypeStruct if last else...  9.1 us
    ppermute x5, waiting for transfers between devices, iteration(): cores = lambda x: lax.ppermute(x, 'ty', [(0, 1), (1, 0)])  3 us
    pallas_call x2, Pallas kernels, move(): pl.pallas_call(body, out_shape=tuple((target(x.shape, x.dtype) for x in a...  2.47 us
    ppermute x5, starting transfers between devices, iteration(): cores = lambda x: lax.ppermute(x, 'ty', [(0, 1), (1, 0)])  1.71 us
  transfers between devices with their start and end apart: 20, of which 10 were waited for; matrix products, arithmetic and copies ran while one was open for 0% of the time, Pallas kernels for 11%

profile of v5, /device:TPU:1, one launch (start us, length us, event | category | flops | bytes accessed | tf_op | source)
XLA Modules:
  0.0 68.8 jit_solution(2000876346532779827)
XLA Ops:
  0.7 1.7 %shard_map.103 = (f32[4,64,256]{2,1,0:T(8,128)S(1)}, f32[4,64,256]{2,1,0:T(8,128)S(1)}, f32[1,1,1,256,256]{4,3,2,1,0:T(8,128)S(1)}, f32[2,256,256]{2,1,0:T(8,128...) custom-call(f32[4,64,256]{2,1,0:T(8,128)} %bitcast.11, f32[4,64,256]{2,1,0:T(8,128)} %bitcast.9, ...), custom_call_target="tpu_custom_call" | custom-call | tf_op jit(solution)/shard_map/pallas_call | solution.py:214
  3.2 4.6 %collective-permute-done.1.mine_ref = f32[4,64,128]{2,1,0:T(8,128)S(1)} collective-permute-done((f32[4,64,128]{2,1,0:T(8,128)S(1)}, f32[4,64,128]{2,1,0:T(8,128)S(1)}, u32[]{:S(2)}, u32[]{:S(2)}) %collective-permute-start.1) | collective-permute-done | bytes 131104 | tf_op jit(solution)/shard_map/ppermute | solution.py:427
  7.8 0.5 collective-permute-start.2
  8.3 1.2 %collective-permute-start.6 = (f32[1,1,1,256,256]{4,3,2,1,0:T(8,128)S(1)}, f32[1,1,1,256,256]{4,3,2,1,0:T(8,128)S(1)}, u32[]{:S(2)}, u32[]{:S(2)}) collective-permute-start(f32[1,1,1,256,256]{4,3,2,1,0:T(8,128)S(1)} %get-tuple-element.46.refs_7_), channel_id=1, source_target_pairs={{0,2},{1,3},{2,0},{3,1},{4,6},{5,7},{6,4},{7,5},{8,10},{9,11},{10,... | collective-permute-start | bytes 786440 | tf_op jit(solution)/shard_map/ppermute | solution.py:435
  9.6 0.9 %shard_map.105 = (f32[4,64,256]{2,1,0:T(8,128)S(1)}, f32[4,64,256]{2,1,0:T(8,128)S(1)}, f32[4,64,256]{2,1,0:T(8,128)S(1)}, f32[4,64,256]{2,1,0:T(8,128)S(1)}, f3...) custom-call(s32[1,1,2,4]{3,2,1,0:T(2,128)S(1)} %bitcast.5, f32[4,64,256]{2,1,0:T(8,128)S(1)} %get-tuple-element.36.own_ref.obj_ref, ...), custom_call_target="tpu_custom_call" | custom-call | tf_op jit(solution)/shard_map/pallas_call | solution.py:30
  10.5 0.7 collective-permute-start.3
  11.2 3.5 %collective-permute-start.4 = (f32[4,64,256]{2,1,0:T(8,128)S(1)}, f32[4,64,256]{2,1,0:T(8,128)S(1)}, u32[]{:S(2)}, u32[]{:S(2)}) collective-permute-start(f32[4,64,256]{2,1,0:T(8,128)S(1)} %get-tuple-element.41), channel_id=1, source_target_pairs={{2,0},{3,1},{16,18},{17,19},{0,16},{1,17},{18,2},{19,3},{6,4},{7,5... | collective-permute-start | bytes 786440 | tf_op jit(solution)/shard_map/ppermute | solution.py:432
  15.3 1.0 %shard_map.106.refs_4_ = f32[2,2,256,256]{3,2,1,0:T(8,128)S(1)} custom-call(s32[1,1,2,4]{3,2,1,0:T(2,128)S(1)} %bitcast.6, f32[2,256,256]{2,1,0:T(8,128)S(1)} %get-tuple-element.43.light_ref), custom_call_target="tpu_custom_call" | custom-call | tf_op jit(solution)/shard_map/pallas_call | solution.py:30
  16.3 1.7 %shard_map.107.refs_5_ = f32[2,256,256]{2,1,0:T(8,128)S(1)} custom-call(f32[256,256]{1,0:T(8,128)S(1)} %get-tuple-element.44.phase_ref), custom_call_target="tpu_custom_call" | custom-call | tf_op jit(solution)/shard_map/pallas_call | solution.py:30
  18.0 3.3 %collective-permute-done.4.refs_2_ = f32[4,64,256]{2,1,0:T(8,128)S(1)} collective-permute-done((f32[4,64,256]{2,1,0:T(8,128)S(1)}, f32[4,64,256]{2,1,0:T(8,128)S(1)}, u32[]{:S(2)}, u32[]{:S(2)}) %collective-permute-start.4) | collective-permute-done | bytes 262176 | tf_op jit(solution)/shard_map/ppermute | solution.py:432
  21.3 0.7 collective-permute-start.7
  22.0 9.6 %collective-permute-start.8 = (f32[4,64,256]{2,1,0:T(8,128)S(1)}, f32[4,64,256]{2,1,0:T(8,128)S(1)}, u32[]{:S(2)}, u32[]{:S(2)}) collective-permute-start(f32[4,64,256]{2,1,0:T(8,128)S(1)} %get-tuple-element.49), channel_id=1, source_target_pairs={{0,2},{1,3},{18,16},{19,17},{2,18},{3,19},{16,0},{17,1},{4,6},{5,7... | collective-permute-start | bytes 786440 | tf_op jit(solution)/shard_map/ppermute | solution.py:432
  31.7 3.0 %collective-permute-done.8.refs_2_ = f32[4,64,256]{2,1,0:T(8,128)S(1)} collective-permute-done((f32[4,64,256]{2,1,0:T(8,128)S(1)}, f32[4,64,256]{2,1,0:T(8,128)S(1)}, u32[]{:S(2)}, u32[]{:S(2)}) %collective-permute-start.8) | collective-permute-done | bytes 262176 | tf_op jit(solution)/shard_map/ppermute | solution.py:432
  34.7 3.6 %collective-permute-done.9.refs_3_ = f32[4,64,256]{2,1,0:T(8,128)S(1)} collective-permute-done((f32[4,64,256]{2,1,0:T(8,128)S(1)}, f32[4,64,256]{2,1,0:T(8,128)S(1)}, u32[]{:S(2)}, u32[]{:S(2)}) %collective-permute-start.9) | collective-permute-done | bytes 262176 | tf_op jit(solution)/shard_map/ppermute | solution.py:432
  38.4 0.8 %shard_map.109 = (f32[2,4,64,256]{3,2,1,0:T(8,128)S(1)}, f32[2,4,64,128]{3,2,1,0:T(8,128)S(1)}) custom-call(s32[1,1,2,4]{3,2,1,0:T(2,128)S(1)} %bitcast.7, s32[1,1]{1,0:T(1,128)S(6)} %copy.11.count_ref, f32[4,64,256]{2,1,0:T(8,128)S(1)} %get-tuple-element.47.refs_0_, f32[4,64,256]{2,1,0:T(8,128)S(1)} %collective-permute-done.7.refs_1_, ...), custom_call_target="tpu_custom_call" | custom-call | tf_op jit(solution)/shard_map/pallas_call | solution.py:30
  39.2 0.5 collective-permute-start.11
  39.7 1.8 %collective-permute-done.11.their_halo_ref = f32[2,4,64,128]{3,2,1,0:T(8,128)S(1)} collective-permute-done((f32[2,4,64,128]{3,2,1,0:T(8,128)S(1)}, f32[2,4,64,128]{3,2,1,0:T(8,128)S(1)}, u32[]{:S(2)}, u32[]{:S(2)}) %collective-permute-start.11) | collective-permute-done | bytes 262176 | tf_op jit(solution)/shard_map/ppermute | solution.py:419
  41.8 5.8 %collective-permute-done.12.mine_ref = f32[2,4,64,128]{3,2,1,0:T(8,128)S(1)} collective-permute-done((f32[2,4,64,128]{3,2,1,0:T(8,128)S(1)}, f32[2,4,64,128]{3,2,1,0:T(8,128)S(1)}, u32[]{:S(2)}, u32[]{:S(2)}) %collective-permute-start.12) | collective-permute-done | bytes 262176 | tf_op jit(solution)/shard_map/ppermute | solution.py:427
  47.6 0.6 collective-permute-start.13
  48.1 1.2 %collective-permute-done.13.theirs_ref = f32[2,4,64,128]{3,2,1,0:T(8,128)S(1)} collective-permute-done((f32[2,4,64,128]{3,2,1,0:T(8,128)S(1)}, f32[2,4,64,128]{3,2,1,0:T(8,128)S(1)}, u32[]{:S(2)}, u32[]{:S(2)}) %collective-permute-start.13) | collective-permute-done | bytes 262176 | tf_op jit(solution)/shard_map/ppermute | solution.py:419
  49.3 1.0 %shard_map.111 = (f32[4,64,256]{2,1,0:T(8,128)S(1)}, f32[4,64,256]{2,1,0:T(8,128)S(1)}, f32[2,64,256]{2,1,0:T(8,128)S(1)}, f32[2,64,256]{2,1,0:T(8,128)S(1)}, f3...) custom-call(s32[1,1,2,4]{3,2,1,0:T(2,128)S(1)} %bitcast.8, ...), custom_call_target="tpu_custom_call" | custom-call | tf_op jit(solution)/shard_map/pallas_call | solution.py:30
  50.3 0.8 %collective-permute-start.17 = (f32[2,64,256]{2,1,0:T(8,128)S(1)}, f32[2,64,256]{2,1,0:T(8,128)S(1)}, u32[]{:S(2)}, u32[]{:S(2)}) collective-permute-start(f32[2,64,256]{2,1,0:T(8,128)S(1)} %get-tuple-element.66), channel_id=1, source_target_pairs={{0,1},{1,0},{16,17},{17,16},{2,18},{3,19},{18,2},{19,3},{4,5},{5,4... | collective-permute-start | bytes 393224 | tf_op jit(solution)/shard_map/ppermute | solution.py:432
  51.1 0.7 %collective-permute-start.14 = (f32[2,64,256]{2,1,0:T(8,128)S(1)}, f32[2,64,256]{2,1,0:T(8,128)S(1)}, u32[]{:S(2)}, u32[]{:S(2)}) collective-permute-start(f32[2,64,256]{2,1,0:T(8,128)S(1)} %get-tuple-element.62), channel_id=1, source_target_pairs={{0,1},{1,0},{16,17},{17,16},{2,18},{3,19},{18,2},{19,3},{4,5},{5,4... | collective-permute-start | bytes 393224 | tf_op jit(solution)/shard_map/ppermute | solution.py:432
  51.8 1.3 %collective-permute-start.18 = (f32[2,64,256]{2,1,0:T(8,128)S(1)}, f32[2,64,256]{2,1,0:T(8,128)S(1)}, u32[]{:S(2)}, u32[]{:S(2)}) collective-permute-start(f32[2,64,256]{2,1,0:T(8,128)S(1)} %get-tuple-element.67), channel_id=1, source_target_pairs={{2,0},{3,1},{18,16},{19,17},{6,4},{7,5},{22,20},{23,21},{10,8},{11... | collective-permute-start | bytes 393224 | tf_op jit(solution)/shard_map/ppermute | solution.py:432
  53.1 1.3 %collective-permute-start.19 = (f32[2,64,256]{2,1,0:T(8,128)S(1)}, f32[2,64,256]{2,1,0:T(8,128)S(1)}, u32[]{:S(2)}, u32[]{:S(2)}) collective-permute-start(f32[2,64,256]{2,1,0:T(8,128)S(1)} %get-tuple-element.68), channel_id=1, source_target_pairs={{2,1},{3,0},{18,17},{19,16},{6,5},{7,4},{22,21},{23,20},{10,9},{11... | collective-permute-start | bytes 393224 | tf_op jit(solution)/shard_map/ppermute | solution.py:432
  54.4 1.3 %collective-permute-start.15 = (f32[2,64,256]{2,1,0:T(8,128)S(1)}, f32[2,64,256]{2,1,0:T(8,128)S(1)}, u32[]{:S(2)}, u32[]{:S(2)}) collective-permute-start(f32[2,64,256]{2,1,0:T(8,128)S(1)} %get-tuple-element.63), channel_id=1, source_target_pairs={{2,0},{3,1},{18,16},{19,17},{6,4},{7,5},{22,20},{23,21},{10,8},{11... | collective-permute-start | bytes 393224 | tf_op jit(solution)/shard_map/ppermute | solution.py:432
  55.7 1.3 %collective-permute-start.16 = (f32[2,64,256]{2,1,0:T(8,128)S(1)}, f32[2,64,256]{2,1,0:T(8,128)S(1)}, u32[]{:S(2)}, u32[]{:S(2)}) collective-permute-start(f32[2,64,256]{2,1,0:T(8,128)S(1)} %get-tuple-element.64), channel_id=1, source_target_pairs={{2,1},{3,0},{18,17},{19,16},{6,5},{7,4},{22,21},{23,20},{10,9},{11... | collective-permute-start | bytes 393224 | tf_op jit(solution)/shard_map/ppermute | solution.py:432
  57.0 0.8 %shard_map.112 = (f32[4,64,256]{2,1,0:T(8,128)}, f32[4,64,256]{2,1,0:T(8,128)}) custom-call(f32[4,64,256]{2,1,0:T(8,128)S(1)} %get-tuple-element.57.refs_0_, f32[4,64,256]{2,1,0:T(8,128)S(1)} %get-tuple-element.58.refs_1_), custom_call_target="tpu_custom_call" | custom-call | tf_op jit(solution)/shard_map/pallas_call | solution.py:214
  57.8 2.3 %collective-permute-done.19.refs_3_ = f32[2,64,256]{2,1,0:T(8,128)S(1)} collective-permute-done((f32[2,64,256]{2,1,0:T(8,128)S(1)}, f32[2,64,256]{2,1,0:T(8,128)S(1)}, u32[]{:S(2)}, u32[]{:S(2)}) %collective-permute-start.19) | collective-permute-done | bytes 131104 | tf_op jit(solution)/shard_map/ppermute | solution.py:432
  60.1 1.8 %shard_map.113.refs_4_ = f32[2,256,256]{2,1,0:T(8,128)S(1)} custom-call(s32[1,1]{1,0:T(1,128)S(6)} %copy.11.count_ref, f32[2,64,256]{2,1,0:T(8,128)S(1)} %get-tuple-element.65.refs_0_, f32[2,64,256]{2,1,0:T(8,128)S(1)} %collective-permute-done.17.refs_1_, f32[2,64,256]{2,1,0:T(8,128)S(1)} %collective-permute-done.18.refs_2_, ...), custom_call_target="tpu_custom_call" | custom-call | tf_op jit(solution)/shard_map/pallas_call | solution.py:30
  61.9 5.2 %collective-permute-done.15.refs_2_ = f32[2,64,256]{2,1,0:T(8,128)S(1)} collective-permute-done((f32[2,64,256]{2,1,0:T(8,128)S(1)}, f32[2,64,256]{2,1,0:T(8,128)S(1)}, u32[]{:S(2)}, u32[]{:S(2)}) %collective-permute-start.15) | collective-permute-done | bytes 131104 | tf_op jit(solution)/shard_map/ppermute | solution.py:432
  67.1 1.7 %shard_map.114 = f32[1,1,1,256,256]{4,3,2,1,0:T(8,128)} custom-call(s32[1,1]{1,0:T(1,128)S(6)} %copy.11.count_ref, f32[2,64,256]{2,1,0:T(8,128)S(1)} %get-tuple-element.61.refs_0_, f32[2,64,256]{2,1,0:T(8,128)S(1)} %collective-permute-done.14.refs_1_, f32[2,64,256]{2,1,0:T(8,128)S(1)} %collective-permute-done.15.refs_2_, ...), custom_call_target="tpu_custom_call" | custom-call | tf_op jit(solution)/shard_map/pallas_call | solution.py:30
  (22 shorter events, 1.4 us)
Async XLA Ops:
  0.6 1.8 %collective-permute-start = (f32[4,64,256]{2,1,0:T(8,128)}, f32[4,64,256]{2,1,0:T(8,128)S(1)}, u32[]{:S(2)}, u32[]{:S(2)}) collective-permute-start(f32[4,64,256]{2,1,0:T(8,128)} %bitcast.10), channel_id=1, source_target_pairs={{0,16},{16,0},{1,17},{17,1},{2,18},{18,2},{3,19},{19,3},{4,20},{20... | collective-permute-start | bytes 786440 | tf_op jit(solution)/shard_map/ppermute | solution.py:419
  2.7 5.1 %collective-permute-start.1 = (f32[4,64,128]{2,1,0:T(8,128)S(1)}, f32[4,64,128]{2,1,0:T(8,128)S(1)}, u32[]{:S(2)}, u32[]{:S(2)}) collective-permute-start(f32[4,64,128]{2,1,0:T(8,128)S(1)} %shard_map.104), channel_id=1, source_target_pairs={{0,4},{4,8},{8,12},{12,28},{20,16},{24,20},{28,24},{16,0},{1,5},{5... | collective-permute-start | bytes 393224 | tf_op jit(solution)/shard_map/ppermute | solution.py:427
  7.8 1.7 %collective-permute-start.2 = (f32[4,64,128]{2,1,0:T(8,128)S(1)}, f32[4,64,128]{2,1,0:T(8,128)S(1)}, u32[]{:S(2)}, u32[]{:S(2)}) collective-permute-start(f32[4,64,128]{2,1,0:T(8,128)S(1)} %collective-permute-done.1.mine_ref), channel_id=1, source_target_pairs={{0,16},{16,0},{1,17},{17,1},{2,18},{18,2},{3,19},{19,3},{4,20},{20... | collective-permute-start | bytes 393224 | tf_op jit(solution)/shard_map/ppermute | solution.py:419
  8.3 1.2 %copy-start = (s32[1,1,4,2]{2,3,1,0:T(2,128)S(1)}, s32[1,1,4,2]{2,3,1,0:T(2,128)}, u32[]{:S(2)}) copy-start(s32[1,1,4,2]{2,3,1,0:T(2,128)} %param.13) | copy-start | bytes 100
  8.3 9.6 %collective-permute-start.6 = (f32[1,1,1,256,256]{4,3,2,1,0:T(8,128)S(1)}, f32[1,1,1,256,256]{4,3,2,1,0:T(8,128)S(1)}, u32[]{:S(2)}, u32[]{:S(2)}) collective-permute-start(f32[1,1,1,256,256]{4,3,2,1,0:T(8,128)S(1)} %get-tuple-element.46.refs_7_), channel_id=1, source_target_pairs={{0,2},{1,3},{2,0},{3,1},{4,6},{5,7},{6,4},{7,5},{8,10},{9,11},{10,... | collective-permute-start | bytes 786440 | tf_op jit(solution)/shard_map/ppermute | solution.py:435
  10.5 7.5 %collective-permute-start.3 = (f32[4,64,256]{2,1,0:T(8,128)S(1)}, f32[4,64,256]{2,1,0:T(8,128)S(1)}, u32[]{:S(2)}, u32[]{:S(2)}) collective-permute-start(f32[4,64,256]{2,1,0:T(8,128)S(1)} %get-tuple-element.40), channel_id=1, source_target_pairs={{0,1},{1,0},{18,19},{19,18},{4,5},{5,4},{22,23},{23,22},{8,9},{9,8... | collective-permute-start | bytes 786440 | tf_op jit(solution)/shard_map/ppermute | solution.py:432
  11.2 10.2 %collective-permute-start.4 = (f32[4,64,256]{2,1,0:T(8,128)S(1)}, f32[4,64,256]{2,1,0:T(8,128)S(1)}, u32[]{:S(2)}, u32[]{:S(2)}) collective-permute-start(f32[4,64,256]{2,1,0:T(8,128)S(1)} %get-tuple-element.41), channel_id=1, source_target_pairs={{2,0},{3,1},{16,18},{17,19},{0,16},{1,17},{18,2},{19,3},{6,4},{7,5... | collective-permute-start | bytes 786440 | tf_op jit(solution)/shard_map/ppermute | solution.py:432
  14.6 6.7 %collective-permute-start.5 = (f32[4,64,256]{2,1,0:T(8,128)S(1)}, f32[4,64,256]{2,1,0:T(8,128)S(1)}, u32[]{:S(2)}, u32[]{:S(2)}) collective-permute-start(f32[4,64,256]{2,1,0:T(8,128)S(1)} %get-tuple-element.42), channel_id=1, source_target_pairs={{2,1},{3,0},{16,19},{17,18},{0,16},{1,17},{18,2},{19,3},{6,5},{7,4... | collective-permute-start | bytes 786440 | tf_op jit(solution)/shard_map/ppermute | solution.py:432
  21.3 10.4 %collective-permute-start.7 = (f32[4,64,256]{2,1,0:T(8,128)S(1)}, f32[4,64,256]{2,1,0:T(8,128)S(1)}, u32[]{:S(2)}, u32[]{:S(2)}) collective-permute-start(f32[4,64,256]{2,1,0:T(8,128)S(1)} %get-tuple-element.48), channel_id=1, source_target_pairs={{1,0},{0,1},{19,18},{18,19},{5,4},{4,5},{23,22},{22,23},{9,8},{8,9... | collective-permute-start | bytes 786440 | tf_op jit(solution)/shard_map/ppermute | solution.py:432
  22.0 12.7 %collective-permute-start.8 = (f32[4,64,256]{2,1,0:T(8,128)S(1)}, f32[4,64,256]{2,1,0:T(8,128)S(1)}, u32[]{:S(2)}, u32[]{:S(2)}) collective-permute-start(f32[4,64,256]{2,1,0:T(8,128)S(1)} %get-tuple-element.49), channel_id=1, source_target_pairs={{0,2},{1,3},{18,16},{19,17},{2,18},{3,19},{16,0},{17,1},{4,6},{5,7... | collective-permute-start | bytes 786440 | tf_op jit(solution)/shard_map/ppermute | solution.py:432
  31.6 6.8 %collective-permute-start.9 = (f32[4,64,256]{2,1,0:T(8,128)S(1)}, f32[4,64,256]{2,1,0:T(8,128)S(1)}, u32[]{:S(2)}, u32[]{:S(2)}) collective-permute-start(f32[4,64,256]{2,1,0:T(8,128)S(1)} %get-tuple-element.50), channel_id=1, source_target_pairs={{1,2},{0,3},{19,16},{18,17},{2,18},{3,19},{16,0},{17,1},{5,6},{4,7... | collective-permute-start | bytes 786440 | tf_op jit(solution)/shard_map/ppermute | solution.py:432
  39.1 2.4 %collective-permute-start.10 = (f32[2,4,64,256]{3,2,1,0:T(8,128)S(1)}, f32[2,4,64,256]{3,2,1,0:T(8,128)S(1)}, u32[]{:S(2)}, u32[]{:S(2)}) collective-permute-start(f32[2,4,64,256]{3,2,1,0:T(8,128)S(1)} %get-tuple-element.52.own_ref), channel_id=1, source_target_pairs={{0,16},{16,0},{1,17},{17,1},{2,18},{18,2},{3,19},{19,3},{4,20},{20... | collective-permute-start | bytes 1572872 | tf_op jit(solution)/shard_map/ppermute | solution.py:419
  39.2 2.3 %collective-permute-start.11 = (f32[2,4,64,128]{3,2,1,0:T(8,128)S(1)}, f32[2,4,64,128]{3,2,1,0:T(8,128)S(1)}, u32[]{:S(2)}, u32[]{:S(2)}) collective-permute-start(f32[2,4,64,128]{3,2,1,0:T(8,128)S(1)} %get-tuple-element.53.halo_ref), channel_id=1, source_target_pairs={{0,16},{16,0},{1,17},{17,1},{2,18},{18,2},{3,19},{19,3},{4,20},{20... | collective-permute-start | bytes 786440 | tf_op jit(solution)/shard_map/ppermute | solution.py:419
  41.6 5.9 %collective-permute-start.12 = (f32[2,4,64,128]{3,2,1,0:T(8,128)S(1)}, f32[2,4,64,128]{3,2,1,0:T(8,128)S(1)}, u32[]{:S(2)}, u32[]{:S(2)}) collective-permute-start(f32[2,4,64,128]{3,2,1,0:T(8,128)S(1)} %get-tuple-element.56), channel_id=1, source_target_pairs={{0,4},{4,8},{8,12},{12,28},{20,16},{24,20},{28,24},{16,0},{1,5},{5... | collective-permute-start | bytes 786440 | tf_op jit(solution)/shard_map/ppermute | solution.py:427
  47.6 1.7 %collective-permute-start.13 = (f32[2,4,64,128]{3,2,1,0:T(8,128)S(1)}, f32[2,4,64,128]{3,2,1,0:T(8,128)S(1)}, u32[]{:S(2)}, u32[]{:S(2)}) collective-permute-start(f32[2,4,64,128]{3,2,1,0:T(8,128)S(1)} %collective-permute-done.12.mine_ref), channel_id=1, source_target_pairs={{0,16},{16,0},{1,17},{17,1},{2,18},{18,2},{3,19},{19,3},{4,20},{20... | collective-permute-start | bytes 786440 | tf_op jit(solution)/shard_map/ppermute | solution.py:419
  50.3 5.4 %collective-permute-start.17 = (f32[2,64,256]{2,1,0:T(8,128)S(1)}, f32[2,64,256]{2,1,0:T(8,128)S(1)}, u32[]{:S(2)}, u32[]{:S(2)}) collective-permute-start(f32[2,64,256]{2,1,0:T(8,128)S(1)} %get-tuple-element.66), channel_id=1, source_target_pairs={{0,1},{1,0},{16,17},{17,16},{2,18},{3,19},{18,2},{19,3},{4,5},{5,4... | collective-permute-start | bytes 393224 | tf_op jit(solution)/shard_map/ppermute | solution.py:432
  51.1 10.8 %collective-permute-start.14 = (f32[2,64,256]{2,1,0:T(8,128)S(1)}, f32[2,64,256]{2,1,0:T(8,128)S(1)}, u32[]{:S(2)}, u32[]{:S(2)}) collective-permute-start(f32[2,64,256]{2,1,0:T(8,128)S(1)} %get-tuple-element.62), channel_id=1, source_target_pairs={{0,1},{1,0},{16,17},{17,16},{2,18},{3,19},{18,2},{19,3},{4,5},{5,4... | collective-permute-start | bytes 393224 | tf_op jit(solution)/shard_map/ppermute | solution.py:432
  51.8 6.0 %collective-permute-start.18 = (f32[2,64,256]{2,1,0:T(8,128)S(1)}, f32[2,64,256]{2,1,0:T(8,128)S(1)}, u32[]{:S(2)}, u32[]{:S(2)}) collective-permute-start(f32[2,64,256]{2,1,0:T(8,128)S(1)} %get-tuple-element.67), channel_id=1, source_target_pairs={{2,0},{3,1},{18,16},{19,17},{6,4},{7,5},{22,20},{23,21},{10,8},{11... | collective-permute-start | bytes 393224 | tf_op jit(solution)/shard_map/ppermute | solution.py:432
  53.1 7.0 %collective-permute-start.19 = (f32[2,64,256]{2,1,0:T(8,128)S(1)}, f32[2,64,256]{2,1,0:T(8,128)S(1)}, u32[]{:S(2)}, u32[]{:S(2)}) collective-permute-start(f32[2,64,256]{2,1,0:T(8,128)S(1)} %get-tuple-element.68), channel_id=1, source_target_pairs={{2,1},{3,0},{18,17},{19,16},{6,5},{7,4},{22,21},{23,20},{10,9},{11... | collective-permute-start | bytes 393224 | tf_op jit(solution)/shard_map/ppermute | solution.py:432
  54.4 12.7 %collective-permute-start.15 = (f32[2,64,256]{2,1,0:T(8,128)S(1)}, f32[2,64,256]{2,1,0:T(8,128)S(1)}, u32[]{:S(2)}, u32[]{:S(2)}) collective-permute-start(f32[2,64,256]{2,1,0:T(8,128)S(1)} %get-tuple-element.63), channel_id=1, source_target_pairs={{2,0},{3,1},{18,16},{19,17},{6,4},{7,5},{22,20},{23,21},{10,8},{11... | collective-permute-start | bytes 393224 | tf_op jit(solution)/shard_map/ppermute | solution.py:432
  55.7 11.4 %collective-permute-start.16 = (f32[2,64,256]{2,1,0:T(8,128)S(1)}, f32[2,64,256]{2,1,0:T(8,128)S(1)}, u32[]{:S(2)}, u32[]{:S(2)}) collective-permute-start(f32[2,64,256]{2,1,0:T(8,128)S(1)} %get-tuple-element.64), channel_id=1, source_target_pairs={{2,1},{3,0},{18,17},{19,16},{6,5},{7,4},{22,21},{23,20},{10,9},{11... | collective-permute-start | bytes 393224 | tf_op jit(solution)/shard_map/ppermute | solution.py:432

commit v6 on v5

--- a/solution.py
+++ b/solution.py
@@ -102,9 +102,13 @@
     def holds(self, device, row, home):
         return 0 <= self.window_of(device, row, home) < self.half
 
+    def crosses(self, s, home):
+        return not home and 0 < s < self.half
+
     def inward(self, s, home):
         n = self.n
-        return [(a * n + p, a * n + (p ^ s)) for a in range(2) for p in range(n) if self.holds(p ^ s, a, home)]
+        core = (lambda a: 1 - a) if self.crosses(s, home) else (lambda a: a)
+        return [(core(a) * n + p, a * n + (p ^ s)) for a in range(2) for p in range(n) if self.holds(p ^ s, a, home)]
 
     def outward(self, s):
         return [(d, o) for o, d in self.inward(s, False)]
@@ -121,13 +125,22 @@
     return lax.axis_index("ty"), lax.axis_index("tx"), lax.axis_index("pos")
 
 
-def masks(place_ref, k, a, p, lay):
+def step(lay):
+    return min(lay.h, 8)
+
+
+def by_rows(lay, body):
+    for start in range(0, lay.h, step(lay)):
+        body(start, slice(start, start + step(lay)))
+
+
+def masks(place_refs, a, k, p, lay, start):
     h, t, m = lay.h, lay.t, lay.m
     k = jnp.clip(k, 0, lay.slots - 1)
-    top = place_ref[0, 0, 0, k] - m
-    left = place_ref[0, 0, 1, k] - m
-    rows = iota((h, t), 0) + p * h
-    cols = iota((h, t), 1)
+    mine = a == lax.axis_index("ty")
+    top, left = (jnp.where(mine, place_refs[0][0, 0, i, k], place_refs[1][0, 0, i, k]) - m for i in range(2))
+    rows = iota((step(lay), t), 0) + (p * h + start)
+    cols = iota((step(lay), t), 1)
     above = rows >= top + t
     below = rows < top
     outside = above | below
@@ -136,19 +149,23 @@
     return outside, partner, halo
 
 
-def pack_blocks(place_ref, own, own_halo, prt, prt_halo, out_refs, lay, home):
+def pack_blocks(place_refs, own, own_halo, prt, prt_halo, out_refs, lay, home):
     a, _, p = where_am_i()
-    for s in range(lay.n):
-        k = lay.window_of(p ^ s, a, home)
-        outside, partner, halo = masks(place_ref, k, a, p, lay)
-        for c in range(4):
-            mine = jnp.where(halo, spread(own_halo[c], lay), own[c])
-            theirs = jnp.where(halo, spread(prt_halo[c], lay), prt[c])
-            value = jnp.where(partner, theirs, jnp.where(outside, 0.0, mine))
-            if home:
-                out_refs[c // 2 * lay.n + s][c % 2] = value
-            else:
-                out_refs[s][c] = value
+
+    def few(start, rows):
+        for s in range(lay.n):
+            row = 1 - a if lay.crosses(s, home) else a
+            k = lay.window_of(p ^ s, row, home)
+            outside, partner, halo = masks(place_refs, row, k, p, lay, start)
+            for c in range(4):
+                mine = jnp.where(halo, spread(own_halo[c, rows, :], lay), own[c, rows, :])
+                theirs = jnp.where(halo, spread(prt_halo[c, rows, :], lay), prt[c, rows, :])
+                if lay.crosses(s, home):
+                    mine, theirs = theirs, mine
+                value = jnp.where(partner, theirs, jnp.where(outside, 0.0, mine))
+                out_refs[c // 2 * lay.n + s][c % 2, rows, :] = value
+
+    by_rows(lay, few)
 
 
 def spread(halo, lay):
@@ -181,9 +198,9 @@
 def kernel_pack(lay):
     m = lay.m
 
-    def body(place_ref, own_ref, prt_ref, mine_ref, theirs_ref, *outs):
+    def body(place_ref, other_ref, own_ref, prt_ref, mine_ref, theirs_ref, *outs):
         a, b, _ = where_am_i()
-        blocks, own_halo_ref, prt_halo_ref = outs[: lay.n], outs[lay.n], outs[lay.n + 1]
+        blocks, own_halo_ref, prt_halo_ref = outs[: 2 * lay.n], *outs[2 * lay.n :]
         low = iota((lay.h, 2 * m), 1) < m
         keep = jnp.where(low, (b < lay.ntx - 1).astype(F32), (b > 0).astype(F32))
         for c in range(4):
@@ -193,7 +210,7 @@
             halo1 = jnp.where(low, roll_half(from_right, lay), roll_half(from_left, lay))
             own_halo_ref[c] = jnp.where(keep > 0, jnp.where(a == 0, halo0, halo1), 0.0)
             prt_halo_ref[c] = jnp.where(keep > 0, jnp.where(a == 0, halo1, halo0), 0.0)
-        pack_blocks(place_ref, own_ref, own_halo_ref, prt_ref, prt_halo_ref, blocks, lay, False)
+        pack_blocks((place_ref, other_ref), own_ref, own_halo_ref, prt_ref, prt_halo_ref, blocks, lay, False)
 
     return body
 
@@ -221,20 +238,29 @@
     )(*[pltpu.with_memory_space_constraint(x, pltpu.HBM if inward else pltpu.VMEM) for x in arrays])
 
 
+def series(z, first):
+    terms = [(-1) ** i / math.factorial(2 * i + first) for i in range(8)]
+    value = terms[-1]
+    for term in terms[-2::-1]:
+        value = value * z + term
+    return value
+
+
 def kernel_slab(phase_ref, slab_ref):
-    slab_ref[0] = jnp.cos(phase_ref[...])
-    slab_ref[1] = jnp.sin(phase_ref[...])
-
-
-def kernel_probe(lay):
+    y = 0.5 * phase_ref[...]
+    z = y * y
+    sine, cosine = series(z, 1) * y, series(z, 0)
+    slab_ref[0] = 1.0 - 2.0 * sine * sine
+    slab_ref[1] = 2.0 * sine * cosine
+
+
+def kernel_probe(lay, home):
     def body(place_ref, light_ref, out_ref):
         a, _, p = where_am_i()
-        for i, home in enumerate((False, True)):
-            k = jnp.clip(lay.window_of(p, a, home), 0, lay.slots - 1)
-            down = (place_ref[0, 0, 0, k] + (lay.t - lay.m)) % lay.t
-            along = (place_ref[0, 0, 1, k] + (lay.t - lay.m)) % lay.t
-            for c in range(2):
-                out_ref[i, c] = pltpu.roll(pltpu.roll(light_ref[c], down, 0), along, 1)
+        k = jnp.clip(lay.window_of(p, a, home), 0, lay.slots - 1)
+        down, along = ((place_ref[0, 0, i, k] + (lay.t - lay.m)) % lay.t for i in range(2))
+        for c in range(2):
+            out_ref[c] = pltpu.roll(pltpu.roll(light_ref[c], down, 0), along, 1)
 
     return body
 
@@ -247,44 +273,60 @@
             window_ref[c, pl.ds(start, lay.h), :] = blocks[s][c]
 
 
-def propagate(o1r, o1i, light_ref, which, slab_ref, tab):
-    er, ei = cmul(light_ref[which, 0], light_ref[which, 1], o1r, o1i)
+def propagate(o1r, o1i, light_ref, slab_ref, tab):
+    er, ei = cmul(light_ref[0], light_ref[1], o1r, o1i)
     sr, si = transform(er, ei, tab, False)
     sr, si = cmul(sr, si, slab_ref[0], slab_ref[1])
     return transform(sr, si, tab, True)
 
 
-def kernel_gradient(lay):
+def live(count_ref, lay, home):
+    a, _, p = where_am_i()
+    k = lay.window_of(p, a, home)
+    return (k >= 0) & (k < count_ref[0, 0])
+
+
+def scatter(value, c, outs, lay):
+    p = lax.axis_index("pos")
+    for s in range(lay.n):
+        outs[s][c] = value[pl.ds(pl.multiple_of((p ^ s) * lay.h, lay.h), lay.h), :]
+
+
+def kernel_backward(lay):
     def body(count_ref, *refs):
         n = lay.n
-        blocks, (light_ref, slab_ref, tab, meas_ref, moved_ref) = refs[:n], refs[n : n + 5]
-        outs, window_ref = refs[n + 5 : 2 * n + 5], refs[2 * n + 5]
-        a, _, p = where_am_i()
-        k = lay.window_of(p, a, False)
-
-        @pl.when((k >= 0) & (k < count_ref[0, 0]))
+        blocks, (between_ref, tab, meas_ref, moved_ref) = refs[:n], refs[n : n + 4]
+        toward_ref, outs, window_ref, grad_ref = refs[n + 4], refs[n + 5 : 2 * n + 5], *refs[2 * n + 5 :]
+
+        @pl.when(live(count_ref, lay, False))
         def _():
             assemble(blocks, window_ref, lay)
-            br, bi = propagate(window_ref[0], window_ref[1], light_ref, 0, slab_ref, tab)
-            lr, li = cmul(br, bi, window_ref[2], window_ref[3])
+            br, bi = between_ref[0], between_ref[1]
+            lr, li = cmul(br, bi, window_ref[0], window_ref[1])
             fr, fi = transform(lr, li, tab, False)
-            seen = jnp.where(a == 0, meas_ref[0, 0, 0], moved_ref[0, 0, 0])
+            seen = jnp.where(lax.axis_index("ty") == 0, meas_ref[0, 0, 0], moved_ref[0, 0, 0])
             keeping = 1.0 - seen / jnp.maximum(jnp.sqrt(fr * fr + fi * fi), magnitude_floor)
             kr, ki = transform(fr * keeping, fi * keeping, tab, True)
-            g2r, g2i = cmul(br, -bi, kr, ki)
-            tr, ti = cmul(window_ref[2], -window_ref[3], kr, ki)
-            window_ref[2] = g2r
-            window_ref[3] = g2i
-            sr, si = transform(tr, ti, tab, False)
+            toward_ref[0], toward_ref[1] = cmul(window_ref[0], -window_ref[1], kr, ki)
+            grad_ref[0], grad_ref[1] = cmul(br, -bi, kr, ki)
+            for c in range(2):
+                scatter(grad_ref.at[c], c, outs, lay)
+
+    return body
+
+
+def kernel_final(lay):
+    def body(count_ref, toward_ref, light_ref, slab_ref, tab, *refs):
+        outs, grad_ref = refs[: lay.n], refs[lay.n]
+
+        @pl.when(live(count_ref, lay, False))
+        def _():
+            sr, si = transform(toward_ref[0], toward_ref[1], tab, False)
             sr, si = cmul(sr, si, slab_ref[0], -slab_ref[1])
             ir, ii = transform(sr, si, tab, True)
-            g1r, g1i = cmul(light_ref[0, 0], -light_ref[0, 1], ir, ii)
-            window_ref[0] = g1r
-            window_ref[1] = g1i
-            for s in range(n):
-                start = pl.multiple_of((p ^ s) * lay.h, lay.h)
-                for c in range(4):
-                    outs[s][c] = window_ref[c, pl.ds(start, lay.h), :]
+            grad_ref[0], grad_ref[1] = cmul(light_ref[0], -light_ref[1], ir, ii)
+            for c in range(2):
+                scatter(grad_ref.at[c], c, outs, lay)
 
     return body
 
@@ -292,27 +334,35 @@
 def kernel_collect(lay):
     t, m = lay.t, lay.m
 
-    def body(place_ref, count_ref, *refs):
+    def body(place_ref, other_ref, count_ref, other_count_ref, *refs):
         n = lay.n
-        blocks, mom_ref = refs[:n], refs[n]
-        own_ref, halo_ref = refs[n + 1 :]
+        blocks, mom_ref = refs[: 2 * n], refs[2 * n]
+        own_ref, halo_ref = refs[2 * n + 1 :]
         a, _, p = where_am_i()
-        low = iota((lay.h, 2 * m), 1) < m
-        own_ref[0] = momentum_rate * mom_ref[...]
-        own_ref[1] = jnp.zeros(own_ref.shape[1:], F32)
-        halo_ref[...] = jnp.zeros(halo_ref.shape, F32)
-        for s in range(n):
-            k = lay.window_of(p ^ s, a, False)
-
-            @pl.when((k >= 0) & (k < count_ref[0, 0]))
-            def _(s=s, k=k):
-                outside, partner, halo = masks(place_ref, k, a, p, lay)
-                for c in range(4):
-                    g = blocks[s][c]
-                    for i, rows in enumerate((~outside, partner)):
-                        own_ref[i, c] += jnp.where(rows & ~halo, g, 0.0)
-                        x = jnp.where(rows & halo, g, 0.0)
-                        halo_ref[i, c] += jnp.where(low, x[:, : 2 * m], x[:, t - 2 * m :])
+        low = iota((step(lay), 2 * m), 1) < m
+
+        def few(start, few_rows):
+            totals = [[momentum_rate * mom_ref[c, few_rows, :], jnp.zeros((step(lay), t), F32)] for c in range(4)]
+            edges = [[jnp.zeros((step(lay), 2 * m), F32) for _ in range(2)] for _ in range(4)]
+            for s in range(n):
+                crosses = lay.crosses(s, False)
+                row = 1 - a if crosses else a
+                k = lay.window_of(p ^ s, row, False)
+                valid = (k >= 0) & (k < (other_count_ref if crosses else count_ref)[0, 0])
+                outside, partner, halo = masks((place_ref, other_ref), row, k, p, lay, start)
+                inside, partner = ~outside & valid, partner & valid
+                for i, rows in enumerate((partner, inside) if crosses else (inside, partner)):
+                    for c in range(4):
+                        g = jnp.where(rows, blocks[c // 2 * n + s][c % 2, few_rows, :], 0.0)
+                        x = jnp.where(halo, g, 0.0)
+                        totals[c][i] += jnp.where(halo, 0.0, g)
+                        edges[c][i] += jnp.where(low, x[:, : 2 * m], x[:, t - 2 * m :])
+            for c in range(4):
+                for i in range(2):
+                    own_ref[i, c, few_rows, :] = totals[c][i]
+                    halo_ref[i, c, few_rows, :] = edges[c][i]
+
+        by_rows(lay, few)
 
     return body
 
@@ -370,20 +420,20 @@
                     vel_ref[c] = v
                 new[c] = obj[c] - step_length * v
                 new_halo[c] = jnp.where(keep, halo[c] - step_length * hv, 0.0)
-        pack_blocks(place_ref, new_ref, own_halo, prt_new, prt_halo, blocks, lay, True)
-
-    return body
-
-
-def kernel_between(lay):
+        pack_blocks((place_ref, place_ref), new_ref, own_halo, prt_new, prt_halo, blocks, lay, True)
+
+    return body
+
+
+def kernel_between(lay, home):
     def body(count_ref, *refs):
         n = lay.n
         blocks, (light_ref, slab_ref, tab), out_ref, window_ref = refs[:n], refs[n : n + 3], refs[n + 3], refs[n + 4]
 
-        @pl.when(lax.axis_index("pos") < count_ref[0, 0])
+        @pl.when(live(count_ref, lay, home))
         def _():
             assemble(blocks, window_ref, lay)
-            out_ref[0], out_ref[1] = propagate(window_ref[0], window_ref[1], light_ref, 1, slab_ref, tab)
+            out_ref[0], out_ref[1] = propagate(window_ref[0], window_ref[1], light_ref, slab_ref, tab)
 
     return body
 
@@ -392,16 +442,16 @@
     def body(count_ref, *refs):
         n = lay.n
         blocks, (between_ref, tab), out_ref, window_ref = refs[:n], refs[n : n + 2], refs[n + 2], refs[n + 3]
-        live = lax.axis_index("pos") < count_ref[0, 0]
-
-        @pl.when(live)
+        used = live(count_ref, lay, True)
+
+        @pl.when(used)
         def _():
             assemble(blocks, window_ref, lay)
             lr, li = cmul(between_ref[0], between_ref[1], window_ref[0], window_ref[1])
             fr, fi = transform(lr, li, tab, False)
             out_ref[0, 0, 0] = jnp.sqrt(fr * fr + fi * fi)
 
-        @pl.when(jnp.logical_not(live))
+        @pl.when(jnp.logical_not(used))
         def _():
             out_ref[...] = jnp.zeros(out_ref.shape, F32)
 
@@ -414,13 +464,13 @@
     own = object_field.reshape(4, h, t)
     offsets = offsets.transpose(0, 1, 3, 2)
     velocity_old = momentum.reshape(4, h, t)
-    block, halo_shape = (4, h, t), (4, h, 2 * m)
+    block, half_block, halo_shape = (4, h, t), (2, h, t), (4, h, 2 * m)
     tab = jnp.asarray(dft_tables(t))
     cores = lambda x: lax.ppermute(x, "ty", [(0, 1), (1, 0)])
     partner = cores(own)
-    own, velocity_old, measured, illumination, slab_phase, tab = move(
-        pltpu.VMEM, own, velocity_old, measured, illumination, slab_phase, tab
-    )
+    other_offsets = cores(offsets)
+    other_counts = cores(entry_counts)
+    (own,) = move(pltpu.VMEM, own)
     ntx = lay.ntx
     shift = [(b, b + 1) for b in range(ntx - 1)] + [(ntx - 1, 2 * ntx - 1)]
     shift += [(ntx + b + 1, ntx + b) for b in range(ntx - 1)] + [(ntx, 0)]
@@ -432,29 +482,57 @@
             got.append(lax.ppermute(values[s], ("ty", "pos"), complete(pairs_of(s), n)))
         return got
 
-    moved = lax.ppermute(measured, "pos", [(p, p ^ lay.half) for p in range(n)])
+    low, high = range(lay.half), range(lay.half, n)
+    pairs = [(n + p, n + p + lay.half) for p in low] + [(p, p - lay.half) for p in high]
+    pairs += [(p, n + p) for p in low] + [(n + p, p) for p in high]
+    moved = lax.ppermute(measured, ("ty", "pos"), pairs)
+    velocity_old, measured, illumination, slab_phase, tab = move(
+        pltpu.VMEM, velocity_old, measured, illumination, slab_phase, tab
+    )
     (slab,) = call(kernel_slab, [(2, t, t)], [slab_phase])
-    (light,) = call(kernel_probe(lay), [(2, 2, t, t)], [offsets, illumination], 1)
-
+    lights = []
+    for home in range(2):
+        (light,) = call(kernel_probe(lay, bool(home)), [(2, t, t)], [offsets, illumination], 1)
+        lights.append(light)
+    light, light_home = lights
     (strips,) = call(kernel_strips(lay), [halo_shape], [own, partner])
     strips = columns(strips)
     strips_other = cores(strips)
     *blocks, own_halo, partner_halo = call(
-        kernel_pack(lay), [block] * n + [halo_shape] * 2, [offsets, own, partner, strips, strips_other], 1
-    )
-    received = exchange(blocks, lambda s: lay.inward(s, False))
-    window = pltpu.VMEM((4, t, t), F32)
-    terms = call(
-        kernel_gradient(lay),
-        [block] * n,
-        [entry_counts, *received, light, slab, tab, measured, moved],
+        kernel_pack(lay),
+        [half_block] * (2 * n) + [halo_shape] * 2,
+        [offsets, other_offsets, own, partner, strips, strips_other],
+        2,
+    )
+    first = exchange(blocks[:n], lambda s: lay.inward(s, False))
+    second = exchange(blocks[n:], lambda s: lay.inward(s, False))
+    half_window = pltpu.VMEM((2, t, t), F32)
+
+    def propagated(first, light, home):
+        (between,) = call(
+            kernel_between(lay, home), [(2, t, t)], [entry_counts, *first, light, slab, tab], 1, [half_window], limit=24
+        )
+        return between
+
+    between = propagated(first, light, False)
+    toward, *terms_second = call(
+        kernel_backward(lay),
+        [(2, t, t)] + [half_block] * n,
+        [entry_counts, *second, between, tab, measured, moved],
         1,
-        [window],
+        [half_window, half_window],
         limit=24,
     )
-    parts = exchange(terms, lay.outward)
+    parts_second = exchange(terms_second, lay.outward)
+    terms_first = call(
+        kernel_final(lay), [half_block] * n, [entry_counts, toward, light, slab, tab], 1, [half_window], limit=24
+    )
+    parts_first = exchange(terms_first, lay.outward)
     sums, halos = call(
-        kernel_collect(lay), [(2, *block), (2, *halo_shape)], [offsets, entry_counts, *parts, velocity_old], 2
+        kernel_collect(lay),
+        [(2, *block), (2, *halo_shape)],
+        [offsets, other_offsets, entry_counts, other_counts, *parts_first, *parts_second, velocity_old],
+        4,
     )
     sums, halos, strips = call(
         kernel_strips_back(lay),
@@ -464,7 +542,7 @@
     strips = columns(strips)
     updated, velocity, *rest = call(
         kernel_update(lay),
-        [block] * 2 + [(2, h, t)] * (2 * n),
+        [block] * 2 + [half_block] * (2 * n),
         [offsets, own, partner, own_halo, partner_halo, sums, halos, strips, cores(strips)],
         1,
         [pltpu.VMEM(block, F32), pltpu.VMEM(halo_shape, F32), pltpu.VMEM(halo_shape, F32)],
@@ -472,10 +550,7 @@
     first = exchange(rest[:n], lambda s: lay.inward(s, True))
     second = exchange(rest[n : 2 * n], lambda s: lay.inward(s, True))
     updated, velocity = move(pltpu.HBM, updated, velocity)
-    half_window = pltpu.VMEM((2, t, t), F32)
-    (between,) = call(
-        kernel_between(lay), [(2, t, t)], [entry_counts, *first, light, slab, tab], 1, [half_window], limit=24
-    )
+    between = propagated(first, light_home, True)
     (amplitudes,) = call(
         kernel_predict(lay),
         [measured.shape],

time: 70 us -> 67.3 us (0.961)
  waiting for transfers between devices: 31 us -> 27.7 us
  Pallas kernels: 11.6 us -> 12.8 us
    ppermute x12 -> x18, waiting for transfers between devices: 17.5 us -> 12.1 us  [exchange(): got.append(lax.ppermute(values[s], ('ty', 'pos'), complete(pairs_of(s), n)))]
    ppermute x5 -> x7, waiting for transfers between devices: 3 us -> 5.2 us  [iteration(): cores = lambda x: lax.ppermute(x, 'ty', [(0, 1), (1, 0)])]
    ppermute x1, starting transfers between devices: 1.24 us -> 0.01 us  [iteration(): moved = lax.ppermute(measured, ('ty', 'pos'), pairs)]
    pallas_call x2 -> x3, Pallas kernels: 2.47 us -> 3.34 us  [move(): pl.pallas_call(body, out_shape=tuple((target(x.shape, x.dtype) for x in a...]
    ppermute x12 -> x18, starting transfers between devices: 21.2 us -> 21.7 us  [exchange(): got.append(lax.ppermute(values[s], ('ty', 'pos'), complete(pairs_of(s), n)))]
    ppermute x5 -> x7, starting transfers between devices: 1.71 us -> 2.1 us  [iteration(): cores = lambda x: lax.ppermute(x, 'ty', [(0, 1), (1, 0)])]
    pallas_call x10 -> x13, Pallas kernels: 9.1 us -> 9.47 us  [call(): pl.pallas_call(body, out_shape=tuple(((jax.ShapeDtypeStruct if last else...]
  transfers between devices with their start and end apart: 20 -> 28, of which waited for: 10 -> 15; matrix products, arithmetic and copies ran while one was open for 0% -> 0% of each run, Pallas kernels for 11% -> 11%
where the time goes in v6:
time: 67.3 us; the launch traced here: 66.1 us
  waiting for transfers between devices  27.7 us (41%)
  starting transfers between devices  24.1 us (36%)
  Pallas kernels  12.8 us (19%)
  between operations  1.51 us (2%)
    ppermute x18, starting transfers between devices, exchange(): got.append(lax.ppermute(values[s], ('ty', 'pos'), complete(pairs_of(s), n)))  21.7 us
    ppermute x18, waiting for transfers between devices, exchange(): got.append(lax.ppermute(values[s], ('ty', 'pos'), complete(pairs_of(s), n)))  12.1 us
    ppermute x2, waiting for transfers between devices, iteration(): columns = lambda x: lax.ppermute(x, ('ty', 'tx'), shift)  10.4 us
    pallas_call x13, Pallas kernels, call(): pl.pallas_call(body, out_shape=tuple(((jax.ShapeDtypeStruct if last else...  9.47 us
    ppermute x7, waiting for transfers between devices, iteration(): cores = lambda x: lax.ppermute(x, 'ty', [(0, 1), (1, 0)])  5.2 us
    pallas_call x3, Pallas kernels, move(): pl.pallas_call(body, out_shape=tuple((target(x.shape, x.dtype) for x in a...  3.34 us
    ppermute x7, starting transfers between devices, iteration(): cores = lambda x: lax.ppermute(x, 'ty', [(0, 1), (1, 0)])  2.1 us
  transfers between devices with their start and end apart: 28, of which 15 were waited for; matrix products, arithmetic and copies ran while one was open for 0% of the time, Pallas kernels for 11%

profile of v6, /device:TPU:1, one launch (start us, length us, event | category | flops | bytes accessed | tf_op | source)
XLA Modules:
  0.0 66.1 jit_solution(16117019342397998906)
XLA Ops:
  0.7 1.0 %shard_map.103.own_ref.obj_ref = f32[4,64,256]{2,1,0:T(8,128)S(1)} custom-call(f32[4,64,256]{2,1,0:T(8,128)} %bitcast.12), custom_call_target="tpu_custom_call" | custom-call | tf_op jit(solution)/shard_map/pallas_call | solution.py:231
  2.9 4.6 %collective-permute-done.2.mine_ref = f32[4,64,128]{2,1,0:T(8,128)S(1)} collective-permute-done((f32[4,64,128]{2,1,0:T(8,128)S(1)}, f32[4,64,128]{2,1,0:T(8,128)S(1)}, u32[]{:S(2)}, u32[]{:S(2)}) %collective-permute-start.2) | collective-permute-done | bytes 131104 | tf_op jit(solution)/shard_map/ppermute | solution.py:477
  7.5 0.8 %collective-permute-start.3 = (f32[4,64,128]{2,1,0:T(8,128)S(1)}, f32[4,64,128]{2,1,0:T(8,128)S(1)}, u32[]{:S(2)}, u32[]{:S(2)}) collective-permute-start(f32[4,64,128]{2,1,0:T(8,128)S(1)} %collective-permute-done.2.mine_ref), channel_id=1, source_target_pairs={{0,16},{16,0},{1,17},{17,1},{2,18},{18,2},{3,19},{19,3},{4,20},{20... | collective-permute-start | bytes 393224 | tf_op jit(solution)/shard_map/ppermute | solution.py:469
  8.4 1.2 %collective-permute-done.1.other_ref = s32[1,1,2,4]{3,2,1,0:T(2,128)S(1)} collective-permute-done((s32[1,1,2,4]{3,2,1,0:T(2,128)S(1)}, s32[1,1,2,4]{3,2,1,0:T(2,128)S(1)}, u32[]{:S(2)}, u32[]{:S(2)}) %collective-permute-start.1) | collective-permute-done | bytes 64 | tf_op jit(solution)/shard_map/ppermute | solution.py:469
  9.5 1.0 %shard_map.105 = (f32[2,64,256]{2,1,0:T(8,128)S(1)}, f32[2,64,256]{2,1,0:T(8,128)S(1)}, f32[2,64,256]{2,1,0:T(8,128)S(1)}, f32[2,64,256]{2,1,0:T(8,128)S(1)}, f3...) custom-call(s32[1,1,2,4]{3,2,1,0:T(2,128)S(1)} %bitcast.6, ...), custom_call_target="tpu_custom_call" | custom-call | tf_op jit(solution)/shard_map/pallas_call | solution.py:30
  10.5 2.2 %collective-permute-start.10 = (f32[2,64,256]{2,1,0:T(8,128)S(1)}, f32[2,64,256]{2,1,0:T(8,128)S(1)}, u32[]{:S(2)}, u32[]{:S(2)}) collective-permute-start(f32[2,64,256]{2,1,0:T(8,128)S(1)} %get-tuple-element.53), channel_id=1, source_target_pairs={{2,1},{3,0},{16,19},{17,18},{0,16},{1,17},{18,2},{19,3},{6,5},{7,4... | collective-permute-start | bytes 393224 | tf_op jit(solution)/shard_map/ppermute | solution.py:482
  13.5 1.6 %collective-permute-start.5 = (f32[2,64,256]{2,1,0:T(8,128)S(1)}, f32[2,64,256]{2,1,0:T(8,128)S(1)}, u32[]{:S(2)}, u32[]{:S(2)}) collective-permute-start(f32[2,64,256]{2,1,0:T(8,128)S(1)} %get-tuple-element.47), channel_id=1, source_target_pairs={{16,1},{17,0},{2,19},{3,18},{0,16},{1,17},{18,2},{19,3},{20,5},{21... | collective-permute-start | bytes 393224 | tf_op jit(solution)/shard_map/ppermute | solution.py:482
  15.0 1.6 %collective-permute-start.6 = (f32[2,64,256]{2,1,0:T(8,128)S(1)}, f32[2,64,256]{2,1,0:T(8,128)S(1)}, u32[]{:S(2)}, u32[]{:S(2)}) collective-permute-start(f32[2,64,256]{2,1,0:T(8,128)S(1)} %get-tuple-element.48), channel_id=1, source_target_pairs={{2,0},{3,1},{16,18},{17,19},{0,16},{1,17},{18,2},{19,3},{6,4},{7,5... | collective-permute-start | bytes 393224 | tf_op jit(solution)/shard_map/ppermute | solution.py:482
  16.7 2.0 %collective-permute-start.7 = (f32[2,64,256]{2,1,0:T(8,128)S(1)}, f32[2,64,256]{2,1,0:T(8,128)S(1)}, u32[]{:S(2)}, u32[]{:S(2)}) collective-permute-start(f32[2,64,256]{2,1,0:T(8,128)S(1)} %get-tuple-element.49), channel_id=1, source_target_pairs={{2,1},{3,0},{16,19},{17,18},{0,16},{1,17},{18,2},{19,3},{6,5},{7,4... | collective-permute-start | bytes 393224 | tf_op jit(solution)/shard_map/ppermute | solution.py:482
  18.6 1.6 %shard_map.106 = (f32[4,64,256]{2,1,0:T(8,128)S(1)}, f32[1,1,1,256,256]{4,3,2,1,0:T(8,128)S(1)}, f32[2,256,256]{2,1,0:T(8,128)S(1)}, f32[256,256]{1,0:T(8,128)S(1)}, bf16[6,256,256]{2,1,0:T(8,128)(2,1)S(1)}) custom-call(f32[4,64,256]{2,1,0:T(8,128)} %bitcast.13, f32[1,1,1,256,256]{4,3,2,1,0:T(8,128)} %refs_1_.1, f32[2,256,256]{2,1,0:T(8,128)} %refs_2_.1, ...), custom_call_target="tpu_custom_call" | custom-call | tf_op jit(solution)/shard_map/pallas_call | solution.py:231
  20.2 0.8 %shard_map.107.refs_4_.light_ref = f32[2,256,256]{2,1,0:T(8,128)S(1)} custom-call(s32[1,1,2,4]{3,2,1,0:T(2,128)S(1)} %bitcast.7, f32[2,256,256]{2,1,0:T(8,128)S(1)} %get-tuple-element.54.light_ref), custom_call_target="tpu_custom_call" | custom-call | tf_op jit(solution)/shard_map/pallas_call | solution.py:30
  22.1 5.4 %collective-permute-start.12 = (f32[2,64,256]{2,1,0:T(8,128)S(1)}, f32[2,64,256]{2,1,0:T(8,128)S(1)}, u32[]{:S(2)}, u32[]{:S(2)}) collective-permute-start(f32[2,64,256]{2,1,0:T(8,128)S(1)} %get-tuple-element.60), channel_id=1, source_target_pairs={{1,16},{0,17},{19,2},{18,3},{2,18},{3,19},{16,0},{17,1},{5,20},{4,... | collective-permute-start | bytes 393224 | tf_op jit(solution)/shard_map/ppermute | solution.py:482
  29.4 1.6 %collective-permute-done.12.refs_1_ = f32[2,64,256]{2,1,0:T(8,128)S(1)} collective-permute-done((f32[2,64,256]{2,1,0:T(8,128)S(1)}, f32[2,64,256]{2,1,0:T(8,128)S(1)}, u32[]{:S(2)}, u32[]{:S(2)}) %collective-permute-start.12) | collective-permute-done | bytes 131104 | tf_op jit(solution)/shard_map/ppermute | solution.py:482
  31.5 1.4 %collective-permute-done.14.refs_3_ = f32[2,64,256]{2,1,0:T(8,128)S(1)} collective-permute-done((f32[2,64,256]{2,1,0:T(8,128)S(1)}, f32[2,64,256]{2,1,0:T(8,128)S(1)}, u32[]{:S(2)}, u32[]{:S(2)}) %collective-permute-start.14) | collective-permute-done | bytes 131104 | tf_op jit(solution)/shard_map/ppermute | solution.py:482
  32.9 1.2 %collective-permute-done.15.refs_5_ = f32[2,64,256]{2,1,0:T(8,128)S(1)} collective-permute-done((f32[2,64,256]{2,1,0:T(8,128)S(1)}, f32[2,64,256]{2,1,0:T(8,128)S(1)}, u32[]{:S(2)}, u32[]{:S(2)}) %collective-permute-start.15) | collective-permute-done | bytes 131104 | tf_op jit(solution)/shard_map/ppermute | solution.py:482
  34.3 1.5 %collective-permute-done.17.refs_7_ = f32[2,64,256]{2,1,0:T(8,128)S(1)} collective-permute-done((f32[2,64,256]{2,1,0:T(8,128)S(1)}, f32[2,64,256]{2,1,0:T(8,128)S(1)}, u32[]{:S(2)}, u32[]{:S(2)}) %collective-permute-start.17) | collective-permute-done | bytes 131104 | tf_op jit(solution)/shard_map/ppermute | solution.py:482
  35.8 1.7 %shard_map.112 = (f32[2,4,64,256]{3,2,1,0:T(8,128)S(1)}, f32[2,4,64,128]{3,2,1,0:T(8,128)S(1)}) custom-call(s32[1,1,2,4]{3,2,1,0:T(2,128)S(1)} %bitcast.8, s32[1,1,2,4]{3,2,1,0:T(2,128)S(1)} %collective-permute-done.1.other_ref, s32[1,1]{1,0:T(1,128)S(6)} %copy.11.count_ref, s32[1,1]{1,0:T(1,128)} %collective-permute-done.4.other_count_ref, ...), custom_call_target="tpu_custom_call" | custom-call | tf_op jit(solution)/shard_map/pallas_call | solution.py:30
  38.0 1.8 %collective-permute-done.19.their_halo_ref = f32[2,4,64,128]{3,2,1,0:T(8,128)S(1)} collective-permute-done((f32[2,4,64,128]{3,2,1,0:T(8,128)S(1)}, f32[2,4,64,128]{3,2,1,0:T(8,128)S(1)}, u32[]{:S(2)}, u32[]{:S(2)}) %collective-permute-start.19) | collective-permute-done | bytes 262176 | tf_op jit(solution)/shard_map/ppermute | solution.py:469
  40.1 5.7 %collective-permute-done.20.mine_ref = f32[2,4,64,128]{3,2,1,0:T(8,128)S(1)} collective-permute-done((f32[2,4,64,128]{3,2,1,0:T(8,128)S(1)}, f32[2,4,64,128]{3,2,1,0:T(8,128)S(1)}, u32[]{:S(2)}, u32[]{:S(2)}) %collective-permute-start.20) | collective-permute-done | bytes 262176 | tf_op jit(solution)/shard_map/ppermute | solution.py:477
  46.4 1.2 %collective-permute-done.21.theirs_ref = f32[2,4,64,128]{3,2,1,0:T(8,128)S(1)} collective-permute-done((f32[2,4,64,128]{3,2,1,0:T(8,128)S(1)}, f32[2,4,64,128]{3,2,1,0:T(8,128)S(1)}, u32[]{:S(2)}, u32[]{:S(2)}) %collective-permute-start.21) | collective-permute-done | bytes 262176 | tf_op jit(solution)/shard_map/ppermute | solution.py:469
  47.5 0.9 %shard_map.114 = (f32[4,64,256]{2,1,0:T(8,128)S(1)}, f32[4,64,256]{2,1,0:T(8,128)S(1)}, f32[2,64,256]{2,1,0:T(8,128)S(1)}, f32[2,64,256]{2,1,0:T(8,128)S(1)}, f3...) custom-call(s32[1,1,2,4]{3,2,1,0:T(2,128)S(1)} %bitcast.9, ...), custom_call_target="tpu_custom_call" | custom-call | tf_op jit(solution)/shard_map/pallas_call | solution.py:30
  49.1 1.3 %collective-permute-start.26 = (f32[2,64,256]{2,1,0:T(8,128)S(1)}, f32[2,64,256]{2,1,0:T(8,128)S(1)}, u32[]{:S(2)}, u32[]{:S(2)}) collective-permute-start(f32[2,64,256]{2,1,0:T(8,128)S(1)} %get-tuple-element.83), channel_id=1, source_target_pairs={{2,0},{3,1},{18,16},{19,17},{6,4},{7,5},{22,20},{23,21},{10,8},{11... | collective-permute-start | bytes 393224 | tf_op jit(solution)/shard_map/ppermute | solution.py:482
  50.4 1.3 %collective-permute-start.27 = (f32[2,64,256]{2,1,0:T(8,128)S(1)}, f32[2,64,256]{2,1,0:T(8,128)S(1)}, u32[]{:S(2)}, u32[]{:S(2)}) collective-permute-start(f32[2,64,256]{2,1,0:T(8,128)S(1)} %get-tuple-element.84), channel_id=1, source_target_pairs={{2,1},{3,0},{18,17},{19,16},{6,5},{7,4},{22,21},{23,20},{10,9},{11... | collective-permute-start | bytes 393224 | tf_op jit(solution)/shard_map/ppermute | solution.py:482
  51.7 0.9 %collective-permute-start.22 = (f32[2,64,256]{2,1,0:T(8,128)S(1)}, f32[2,64,256]{2,1,0:T(8,128)S(1)}, u32[]{:S(2)}, u32[]{:S(2)}) collective-permute-start(f32[2,64,256]{2,1,0:T(8,128)S(1)} %get-tuple-element.78), channel_id=1, source_target_pairs={{0,1},{1,0},{16,17},{17,16},{2,18},{3,19},{18,2},{19,3},{4,5},{5,4... | collective-permute-start | bytes 393224 | tf_op jit(solution)/shard_map/ppermute | solution.py:482
  52.6 1.3 %collective-permute-start.23 = (f32[2,64,256]{2,1,0:T(8,128)S(1)}, f32[2,64,256]{2,1,0:T(8,128)S(1)}, u32[]{:S(2)}, u32[]{:S(2)}) collective-permute-start(f32[2,64,256]{2,1,0:T(8,128)S(1)} %get-tuple-element.79), channel_id=1, source_target_pairs={{2,0},{3,1},{18,16},{19,17},{6,4},{7,5},{22,20},{23,21},{10,8},{11... | collective-permute-start | bytes 393224 | tf_op jit(solution)/shard_map/ppermute | solution.py:482
  53.9 1.3 %collective-permute-start.24 = (f32[2,64,256]{2,1,0:T(8,128)S(1)}, f32[2,64,256]{2,1,0:T(8,128)S(1)}, u32[]{:S(2)}, u32[]{:S(2)}) collective-permute-start(f32[2,64,256]{2,1,0:T(8,128)S(1)} %get-tuple-element.80), channel_id=1, source_target_pairs={{2,1},{3,0},{18,17},{19,16},{6,5},{7,4},{22,21},{23,20},{10,9},{11... | collective-permute-start | bytes 393224 | tf_op jit(solution)/shard_map/ppermute | solution.py:482
  55.2 0.8 %shard_map.116.refs_4_ = f32[2,256,256]{2,1,0:T(8,128)S(1)} custom-call(s32[1,1,2,4]{3,2,1,0:T(2,128)S(1)} %bitcast.10, f32[2,256,256]{2,1,0:T(8,128)S(1)} %get-tuple-element.54.light_ref), custom_call_target="tpu_custom_call" | custom-call | tf_op jit(solution)/shard_map/pallas_call | solution.py:30
  56.0 0.8 %shard_map.115 = (f32[4,64,256]{2,1,0:T(8,128)}, f32[4,64,256]{2,1,0:T(8,128)}) custom-call(f32[4,64,256]{2,1,0:T(8,128)S(1)} %get-tuple-element.73.refs_0_, f32[4,64,256]{2,1,0:T(8,128)S(1)} %get-tuple-element.74.refs_1_), custom_call_target="tpu_custom_call" | custom-call | tf_op jit(solution)/shard_map/pallas_call | solution.py:231
  56.9 0.8 %collective-permute-done.27.refs_3_ = f32[2,64,256]{2,1,0:T(8,128)S(1)} collective-permute-done((f32[2,64,256]{2,1,0:T(8,128)S(1)}, f32[2,64,256]{2,1,0:T(8,128)S(1)}, u32[]{:S(2)}, u32[]{:S(2)}) %collective-permute-start.27) | collective-permute-done | bytes 131104 | tf_op jit(solution)/shard_map/ppermute | solution.py:482
  57.7 1.8 %shard_map.117.refs_4_ = f32[2,256,256]{2,1,0:T(8,128)S(1)} custom-call(s32[1,1]{1,0:T(1,128)S(6)} %copy.11.count_ref, f32[2,64,256]{2,1,0:T(8,128)S(1)} %get-tuple-element.81.refs_0_, f32[2,64,256]{2,1,0:T(8,128)S(1)} %collective-permute-done.25.refs_1_, f32[2,64,256]{2,1,0:T(8,128)S(1)} %collective-permute-done.26.refs_2_, ...), custom_call_target="tpu_custom_call" | custom-call | tf_op jit(solution)/shard_map/pallas_call | solution.py:30
  59.5 4.9 %collective-permute-done.23.refs_2_ = f32[2,64,256]{2,1,0:T(8,128)S(1)} collective-permute-done((f32[2,64,256]{2,1,0:T(8,128)S(1)}, f32[2,64,256]{2,1,0:T(8,128)S(1)}, u32[]{:S(2)}, u32[]{:S(2)}) %collective-permute-start.23) | collective-permute-done | bytes 131104 | tf_op jit(solution)/shard_map/ppermute | solution.py:482
  64.4 1.7 %shard_map.118 = f32[1,1,1,256,256]{4,3,2,1,0:T(8,128)} custom-call(s32[1,1]{1,0:T(1,128)S(6)} %copy.11.count_ref, f32[2,64,256]{2,1,0:T(8,128)S(1)} %get-tuple-element.77.refs_0_, f32[2,64,256]{2,1,0:T(8,128)S(1)} %collective-permute-done.22.refs_1_, f32[2,64,256]{2,1,0:T(8,128)S(1)} %collective-permute-done.23.refs_2_, ...), custom_call_target="tpu_custom_call" | custom-call | tf_op jit(solution)/shard_map/pallas_call | solution.py:30
  (44 shorter events, 7.0 us)
Async XLA Ops:
  0.6 1.8 %collective-permute-start = (f32[4,64,256]{2,1,0:T(8,128)}, f32[4,64,256]{2,1,0:T(8,128)S(1)}, u32[]{:S(2)}, u32[]{:S(2)}) collective-permute-start(f32[4,64,256]{2,1,0:T(8,128)} %bitcast.11), channel_id=1, source_target_pairs={{0,16},{16,0},{1,17},{17,1},{2,18},{18,2},{3,19},{19,3},{4,20},{20... | collective-permute-start | bytes 786440 | tf_op jit(solution)/shard_map/ppermute | solution.py:469
  2.7 5.6 %copy-start = (s32[1,1,4,2]{2,3,1,0:T(2,128)S(1)}, s32[1,1,4,2]{2,3,1,0:T(2,128)}, u32[]{:S(2)}) copy-start(s32[1,1,4,2]{2,3,1,0:T(2,128)} %param.13) | copy-start | bytes 100
  2.8 4.8 %collective-permute-start.2 = (f32[4,64,128]{2,1,0:T(8,128)S(1)}, f32[4,64,128]{2,1,0:T(8,128)S(1)}, u32[]{:S(2)}, u32[]{:S(2)}) collective-permute-start(f32[4,64,128]{2,1,0:T(8,128)S(1)} %shard_map.104), channel_id=1, source_target_pairs={{0,4},{4,8},{8,12},{12,28},{20,16},{24,20},{28,24},{16,0},{1,5},{5... | collective-permute-start | bytes 393224 | tf_op jit(solution)/shard_map/ppermute | solution.py:477
  7.5 2.0 %collective-permute-start.3 = (f32[4,64,128]{2,1,0:T(8,128)S(1)}, f32[4,64,128]{2,1,0:T(8,128)S(1)}, u32[]{:S(2)}, u32[]{:S(2)}) collective-permute-start(f32[4,64,128]{2,1,0:T(8,128)S(1)} %collective-permute-done.2.mine_ref), channel_id=1, source_target_pairs={{0,16},{16,0},{1,17},{17,1},{2,18},{18,2},{3,19},{19,3},{4,20},{20... | collective-permute-start | bytes 393224 | tf_op jit(solution)/shard_map/ppermute | solution.py:469
  8.4 4.4 %copy-start.1 = (f32[1,1,1,256,256]{4,3,2,1,0:T(8,128)S(1)}, f32[1,1,1,256,256]{4,3,2,1,0:T(8,128)}, u32[]{:S(2)}) copy-start(f32[1,1,1,256,256]{4,3,2,1,0:T(8,128)} %refs_1_.1) | copy-start | bytes 786436
  8.4 1.2 %collective-permute-start.1 = (s32[1,1,2,4]{3,2,1,0:T(2,128)S(1)}, s32[1,1,2,4]{3,2,1,0:T(2,128)S(1)}, u32[]{:S(2)}, u32[]{:S(2)}) collective-permute-start(s32[1,1,2,4]{3,2,1,0:T(2,128)S(1)} %bitcast.5), channel_id=1, source_target_pairs={{0,16},{16,0},{1,17},{17,1},{2,18},{18,2},{3,19},{19,3},{4,20},{20... | collective-permute-start | bytes 104 | tf_op jit(solution)/shard_map/ppermute | solution.py:469
  10.5 4.5 %collective-permute-start.10 = (f32[2,64,256]{2,1,0:T(8,128)S(1)}, f32[2,64,256]{2,1,0:T(8,128)S(1)}, u32[]{:S(2)}, u32[]{:S(2)}) collective-permute-start(f32[2,64,256]{2,1,0:T(8,128)S(1)} %get-tuple-element.53), channel_id=1, source_target_pairs={{2,1},{3,0},{16,19},{17,18},{0,16},{1,17},{18,2},{19,3},{6,5},{7,4... | collective-permute-start | bytes 393224 | tf_op jit(solution)/shard_map/ppermute | solution.py:482
  12.8 9.3 %collective-permute-start.11 = (f32[1,1,1,256,256]{4,3,2,1,0:T(8,128)S(1)}, f32[1,1,1,256,256]{4,3,2,1,0:T(8,128)S(1)}, u32[]{:S(2)}, u32[]{:S(2)}) collective-permute-start(f32[1,1,1,256,256]{4,3,2,1,0:T(8,128)S(1)} %copy-done.1), channel_id=1, source_target_pairs={{16,18},{17,19},{2,0},{3,1},{0,16},{1,17},{18,2},{19,3},{20,22},{2... | collective-permute-start | bytes 786440 | tf_op jit(solution)/shard_map/ppermute | solution.py:488
  12.8 3.9 %collective-permute-start.8 = (f32[2,64,256]{2,1,0:T(8,128)S(1)}, f32[2,64,256]{2,1,0:T(8,128)S(1)}, u32[]{:S(2)}, u32[]{:S(2)}) collective-permute-start(f32[2,64,256]{2,1,0:T(8,128)S(1)} %get-tuple-element.51), channel_id=1, source_target_pairs={{16,1},{17,0},{2,19},{3,18},{0,16},{1,17},{18,2},{19,3},{20,5},{21... | collective-permute-start | bytes 393224 | tf_op jit(solution)/shard_map/ppermute | solution.py:482
  13.4 8.6 %collective-permute-start.9 = (f32[2,64,256]{2,1,0:T(8,128)S(1)}, f32[2,64,256]{2,1,0:T(8,128)S(1)}, u32[]{:S(2)}, u32[]{:S(2)}) collective-permute-start(f32[2,64,256]{2,1,0:T(8,128)S(1)} %get-tuple-element.52), channel_id=1, source_target_pairs={{2,0},{3,1},{16,18},{17,19},{0,16},{1,17},{18,2},{19,3},{6,4},{7,5... | collective-permute-start | bytes 393224 | tf_op jit(solution)/shard_map/ppermute | solution.py:482
  13.5 8.6 %collective-permute-start.5 = (f32[2,64,256]{2,1,0:T(8,128)S(1)}, f32[2,64,256]{2,1,0:T(8,128)S(1)}, u32[]{:S(2)}, u32[]{:S(2)}) collective-permute-start(f32[2,64,256]{2,1,0:T(8,128)S(1)} %get-tuple-element.47), channel_id=1, source_target_pairs={{16,1},{17,0},{2,19},{3,18},{0,16},{1,17},{18,2},{19,3},{20,5},{21... | collective-permute-start | bytes 393224 | tf_op jit(solution)/shard_map/ppermute | solution.py:482
  15.0 7.0 %collective-permute-start.6 = (f32[2,64,256]{2,1,0:T(8,128)S(1)}, f32[2,64,256]{2,1,0:T(8,128)S(1)}, u32[]{:S(2)}, u32[]{:S(2)}) collective-permute-start(f32[2,64,256]{2,1,0:T(8,128)S(1)} %get-tuple-element.48), channel_id=1, source_target_pairs={{2,0},{3,1},{16,18},{17,19},{0,16},{1,17},{18,2},{19,3},{6,4},{7,5... | collective-permute-start | bytes 393224 | tf_op jit(solution)/shard_map/ppermute | solution.py:482
  16.7 5.4 %collective-permute-start.7 = (f32[2,64,256]{2,1,0:T(8,128)S(1)}, f32[2,64,256]{2,1,0:T(8,128)S(1)}, u32[]{:S(2)}, u32[]{:S(2)}) collective-permute-start(f32[2,64,256]{2,1,0:T(8,128)S(1)} %get-tuple-element.49), channel_id=1, source_target_pairs={{2,1},{3,0},{16,19},{17,18},{0,16},{1,17},{18,2},{19,3},{6,5},{7,4... | collective-permute-start | bytes 393224 | tf_op jit(solution)/shard_map/ppermute | solution.py:482
  22.1 8.9 %collective-permute-start.12 = (f32[2,64,256]{2,1,0:T(8,128)S(1)}, f32[2,64,256]{2,1,0:T(8,128)S(1)}, u32[]{:S(2)}, u32[]{:S(2)}) collective-permute-start(f32[2,64,256]{2,1,0:T(8,128)S(1)} %get-tuple-element.60), channel_id=1, source_target_pairs={{1,16},{0,17},{19,2},{18,3},{2,18},{3,19},{16,0},{17,1},{5,20},{4,... | collective-permute-start | bytes 393224 | tf_op jit(solution)/shard_map/ppermute | solution.py:482
  27.6 1.3 %collective-permute-start.4 = (s32[1,1]{1,0:T(1,128)}, s32[1,1]{1,0:T(1,128)}, u32[]{:S(2)}, u32[]{:S(2)}) collective-permute-start(s32[1,1]{1,0:T(1,128)} %param.14), channel_id=1, source_target_pairs={{0,16},{16,0},{1,17},{17,1},{2,18},{18,2},{3,19},{19,3},{4,20},{20... | collective-permute-start | bytes 20 | tf_op jit(solution)/shard_map/ppermute | solution.py:469
  27.6 3.8 %collective-permute-start.13 = (f32[2,64,256]{2,1,0:T(8,128)S(1)}, f32[2,64,256]{2,1,0:T(8,128)S(1)}, u32[]{:S(2)}, u32[]{:S(2)}) collective-permute-start(f32[2,64,256]{2,1,0:T(8,128)S(1)} %get-tuple-element.61), channel_id=1, source_target_pairs={{0,2},{1,3},{18,16},{19,17},{2,18},{3,19},{16,0},{17,1},{4,6},{5,7... | collective-permute-start | bytes 393224 | tf_op jit(solution)/shard_map/ppermute | solution.py:482
  28.1 4.8 %collective-permute-start.14 = (f32[2,64,256]{2,1,0:T(8,128)S(1)}, f32[2,64,256]{2,1,0:T(8,128)S(1)}, u32[]{:S(2)}, u32[]{:S(2)}) collective-permute-start(f32[2,64,256]{2,1,0:T(8,128)S(1)} %get-tuple-element.62), channel_id=1, source_target_pairs={{1,2},{0,3},{19,16},{18,17},{2,18},{3,19},{16,0},{17,1},{5,6},{4,7... | collective-permute-start | bytes 393224 | tf_op jit(solution)/shard_map/ppermute | solution.py:482
  28.5 5.6 %collective-permute-start.15 = (f32[2,64,256]{2,1,0:T(8,128)S(1)}, f32[2,64,256]{2,1,0:T(8,128)S(1)}, u32[]{:S(2)}, u32[]{:S(2)}) collective-permute-start(f32[2,64,256]{2,1,0:T(8,128)S(1)} %get-tuple-element.64), channel_id=1, source_target_pairs={{1,16},{0,17},{19,2},{18,3},{2,18},{3,19},{16,0},{17,1},{5,20},{4,... | collective-permute-start | bytes 393224 | tf_op jit(solution)/shard_map/ppermute | solution.py:482
  28.8 5.4 %collective-permute-start.16 = (f32[2,64,256]{2,1,0:T(8,128)S(1)}, f32[2,64,256]{2,1,0:T(8,128)S(1)}, u32[]{:S(2)}, u32[]{:S(2)}) collective-permute-start(f32[2,64,256]{2,1,0:T(8,128)S(1)} %get-tuple-element.65), channel_id=1, source_target_pairs={{0,2},{1,3},{18,16},{19,17},{2,18},{3,19},{16,0},{17,1},{4,6},{5,7... | collective-permute-start | bytes 393224 | tf_op jit(solution)/shard_map/ppermute | solution.py:482
  31.0 4.7 %collective-permute-start.17 = (f32[2,64,256]{2,1,0:T(8,128)S(1)}, f32[2,64,256]{2,1,0:T(8,128)S(1)}, u32[]{:S(2)}, u32[]{:S(2)}) collective-permute-start(f32[2,64,256]{2,1,0:T(8,128)S(1)} %get-tuple-element.66), channel_id=1, source_target_pairs={{1,2},{0,3},{19,16},{18,17},{2,18},{3,19},{16,0},{17,1},{5,6},{4,7... | collective-permute-start | bytes 393224 | tf_op jit(solution)/shard_map/ppermute | solution.py:482
  37.5 2.4 %collective-permute-start.18 = (f32[2,4,64,256]{3,2,1,0:T(8,128)S(1)}, f32[2,4,64,256]{3,2,1,0:T(8,128)S(1)}, u32[]{:S(2)}, u32[]{:S(2)}) collective-permute-start(f32[2,4,64,256]{3,2,1,0:T(8,128)S(1)} %get-tuple-element.68.own_ref), channel_id=1, source_target_pairs={{0,16},{16,0},{1,17},{17,1},{2,18},{18,2},{3,19},{19,3},{4,20},{20... | collective-permute-start | bytes 1572872 | tf_op jit(solution)/shard_map/ppermute | solution.py:469
  37.5 2.3 %collective-permute-start.19 = (f32[2,4,64,128]{3,2,1,0:T(8,128)S(1)}, f32[2,4,64,128]{3,2,1,0:T(8,128)S(1)}, u32[]{:S(2)}, u32[]{:S(2)}) collective-permute-start(f32[2,4,64,128]{3,2,1,0:T(8,128)S(1)} %get-tuple-element.69.halo_ref), channel_id=1, source_target_pairs={{0,16},{16,0},{1,17},{17,1},{2,18},{18,2},{3,19},{19,3},{4,20},{20... | collective-permute-start | bytes 786440 | tf_op jit(solution)/shard_map/ppermute | solution.py:469
  39.9 5.9 %collective-permute-start.20 = (f32[2,4,64,128]{3,2,1,0:T(8,128)S(1)}, f32[2,4,64,128]{3,2,1,0:T(8,128)S(1)}, u32[]{:S(2)}, u32[]{:S(2)}) collective-permute-start(f32[2,4,64,128]{3,2,1,0:T(8,128)S(1)} %get-tuple-element.72), channel_id=1, source_target_pairs={{0,4},{4,8},{8,12},{12,28},{20,16},{24,20},{28,24},{16,0},{1,5},{5... | collective-permute-start | bytes 786440 | tf_op jit(solution)/shard_map/ppermute | solution.py:477
  45.8 1.7 %collective-permute-start.21 = (f32[2,4,64,128]{3,2,1,0:T(8,128)S(1)}, f32[2,4,64,128]{3,2,1,0:T(8,128)S(1)}, u32[]{:S(2)}, u32[]{:S(2)}) collective-permute-start(f32[2,4,64,128]{3,2,1,0:T(8,128)S(1)} %collective-permute-done.20.mine_ref), channel_id=1, source_target_pairs={{0,16},{16,0},{1,17},{17,1},{2,18},{18,2},{3,19},{19,3},{4,20},{20... | collective-permute-start | bytes 786440 | tf_op jit(solution)/shard_map/ppermute | solution.py:469
  48.4 5.5 %collective-permute-start.25 = (f32[2,64,256]{2,1,0:T(8,128)S(1)}, f32[2,64,256]{2,1,0:T(8,128)S(1)}, u32[]{:S(2)}, u32[]{:S(2)}) collective-permute-start(f32[2,64,256]{2,1,0:T(8,128)S(1)} %get-tuple-element.82), channel_id=1, source_target_pairs={{0,1},{1,0},{16,17},{17,16},{2,18},{3,19},{18,2},{19,3},{4,5},{5,4... | collective-permute-start | bytes 393224 | tf_op jit(solution)/shard_map/ppermute | solution.py:482
  49.1 7.7 %collective-permute-start.26 = (f32[2,64,256]{2,1,0:T(8,128)S(1)}, f32[2,64,256]{2,1,0:T(8,128)S(1)}, u32[]{:S(2)}, u32[]{:S(2)}) collective-permute-start(f32[2,64,256]{2,1,0:T(8,128)S(1)} %get-tuple-element.83), channel_id=1, source_target_pairs={{2,0},{3,1},{18,16},{19,17},{6,4},{7,5},{22,20},{23,21},{10,8},{11... | collective-permute-start | bytes 393224 | tf_op jit(solution)/shard_map/ppermute | solution.py:482
  50.4 7.3 %collective-permute-start.27 = (f32[2,64,256]{2,1,0:T(8,128)S(1)}, f32[2,64,256]{2,1,0:T(8,128)S(1)}, u32[]{:S(2)}, u32[]{:S(2)}) collective-permute-start(f32[2,64,256]{2,1,0:T(8,128)S(1)} %get-tuple-element.84), channel_id=1, source_target_pairs={{2,1},{3,0},{18,17},{19,16},{6,5},{7,4},{22,21},{23,20},{10,9},{11... | collective-permute-start | bytes 393224 | tf_op jit(solution)/shard_map/ppermute | solution.py:482
  51.7 7.8 %collective-permute-start.22 = (f32[2,64,256]{2,1,0:T(8,128)S(1)}, f32[2,64,256]{2,1,0:T(8,128)S(1)}, u32[]{:S(2)}, u32[]{:S(2)}) collective-permute-start(f32[2,64,256]{2,1,0:T(8,128)S(1)} %get-tuple-element.78), channel_id=1, source_target_pairs={{0,1},{1,0},{16,17},{17,16},{2,18},{3,19},{18,2},{19,3},{4,5},{5,4... | collective-permute-start | bytes 393224 | tf_op jit(solution)/shard_map/ppermute | solution.py:482
  52.6 11.8 %collective-permute-start.23 = (f32[2,64,256]{2,1,0:T(8,128)S(1)}, f32[2,64,256]{2,1,0:T(8,128)S(1)}, u32[]{:S(2)}, u32[]{:S(2)}) collective-permute-start(f32[2,64,256]{2,1,0:T(8,128)S(1)} %get-tuple-element.79), channel_id=1, source_target_pairs={{2,0},{3,1},{18,16},{19,17},{6,4},{7,5},{22,20},{23,21},{10,8},{11... | collective-permute-start | bytes 393224 | tf_op jit(solution)/shard_map/ppermute | solution.py:482
  53.9 10.5 %collective-permute-start.24 = (f32[2,64,256]{2,1,0:T(8,128)S(1)}, f32[2,64,256]{2,1,0:T(8,128)S(1)}, u32[]{:S(2)}, u32[]{:S(2)}) collective-permute-start(f32[2,64,256]{2,1,0:T(8,128)S(1)} %get-tuple-element.80), channel_id=1, source_target_pairs={{2,1},{3,0},{18,17},{19,16},{6,5},{7,4},{22,21},{23,20},{10,9},{11... | collective-permute-start | bytes 393224 | tf_op jit(solution)/shard_map/ppermute | solution.py:482

commit v7 on v6

--- a/solution.py
+++ b/solution.py
@@ -125,38 +125,36 @@
     return lax.axis_index("ty"), lax.axis_index("tx"), lax.axis_index("pos")
 
 
-def step(lay):
-    return min(lay.h, 8)
-
-
-def by_rows(lay, body):
-    for start in range(0, lay.h, step(lay)):
-        body(start, slice(start, start + step(lay)))
-
-
-def masks(place_refs, a, k, p, lay, start):
+def by_rows(lay, body, size):
+    size = min(size, lay.h)
+    for start in range(0, lay.h, size):
+        body(start, slice(start, start + size))
+
+
+def masks(place_refs, a, k, p, lay, few):
     h, t, m = lay.h, lay.t, lay.m
     k = jnp.clip(k, 0, lay.slots - 1)
     mine = a == lax.axis_index("ty")
     top, left = (jnp.where(mine, place_refs[0][0, 0, i, k], place_refs[1][0, 0, i, k]) - m for i in range(2))
-    rows = iota((step(lay), t), 0) + (p * h + start)
-    cols = iota((step(lay), t), 1)
+    rows = iota((few.stop - few.start, t), 0) + (p * h + few.start)
+    cols = iota((few.stop - few.start, t), 1)
+    reaches = ((p * h + h > top + t) & (a == 1)) | ((p * h < top) & (a == 0))
     above = rows >= top + t
     below = rows < top
     outside = above | below
     partner = (above & (a == 1)) | (below & (a == 0))
     halo = (cols >= left + t) | (cols < left)
-    return outside, partner, halo
+    return outside, partner, halo, reaches
 
 
 def pack_blocks(place_refs, own, own_halo, prt, prt_halo, out_refs, lay, home):
     a, _, p = where_am_i()
 
-    def few(start, rows):
+    def few(_, rows):
         for s in range(lay.n):
             row = 1 - a if lay.crosses(s, home) else a
             k = lay.window_of(p ^ s, row, home)
-            outside, partner, halo = masks(place_refs, row, k, p, lay, start)
+            outside, partner, halo, _ = masks(place_refs, row, k, p, lay, rows)
             for c in range(4):
                 mine = jnp.where(halo, spread(own_halo[c, rows, :], lay), own[c, rows, :])
                 theirs = jnp.where(halo, spread(prt_halo[c, rows, :], lay), prt[c, rows, :])
@@ -165,7 +163,7 @@
                 value = jnp.where(partner, theirs, jnp.where(outside, 0.0, mine))
                 out_refs[c // 2 * lay.n + s][c % 2, rows, :] = value
 
-    by_rows(lay, few)
+    by_rows(lay, few, 8 if home else lay.h)
 
 
 def spread(halo, lay):
@@ -298,7 +296,9 @@
         blocks, (between_ref, tab, meas_ref, moved_ref) = refs[:n], refs[n : n + 4]
         toward_ref, outs, window_ref, grad_ref = refs[n + 4], refs[n + 5 : 2 * n + 5], *refs[2 * n + 5 :]
 
-        @pl.when(live(count_ref, lay, False))
+        used = live(count_ref, lay, False)
+
+        @pl.when(used)
         def _():
             assemble(blocks, window_ref, lay)
             br, bi = between_ref[0], between_ref[1]
@@ -312,14 +312,20 @@
             for c in range(2):
                 scatter(grad_ref.at[c], c, outs, lay)
 
+        @pl.when(jnp.logical_not(used))
+        def _():
+            for out in outs:
+                out[...] = jnp.zeros(out.shape, F32)
+
     return body
 
 
 def kernel_final(lay):
     def body(count_ref, toward_ref, light_ref, slab_ref, tab, *refs):
         outs, grad_ref = refs[: lay.n], refs[lay.n]
-
-        @pl.when(live(count_ref, lay, False))
+        used = live(count_ref, lay, False)
+
+        @pl.when(used)
         def _():
             sr, si = transform(toward_ref[0], toward_ref[1], tab, False)
             sr, si = cmul(sr, si, slab_ref[0], -slab_ref[1])
@@ -328,41 +334,50 @@
             for c in range(2):
                 scatter(grad_ref.at[c], c, outs, lay)
 
+        @pl.when(jnp.logical_not(used))
+        def _():
+            for out in outs:
+                out[...] = jnp.zeros(out.shape, F32)
+
     return body
 
 
 def kernel_collect(lay):
     t, m = lay.t, lay.m
 
-    def body(place_ref, other_ref, count_ref, other_count_ref, *refs):
+    def body(place_ref, other_ref, *refs):
         n = lay.n
         blocks, mom_ref = refs[: 2 * n], refs[2 * n]
         own_ref, halo_ref = refs[2 * n + 1 :]
         a, _, p = where_am_i()
-        low = iota((step(lay), 2 * m), 1) < m
-
-        def few(start, few_rows):
-            totals = [[momentum_rate * mom_ref[c, few_rows, :], jnp.zeros((step(lay), t), F32)] for c in range(4)]
-            edges = [[jnp.zeros((step(lay), 2 * m), F32) for _ in range(2)] for _ in range(4)]
-            for s in range(n):
-                crosses = lay.crosses(s, False)
-                row = 1 - a if crosses else a
-                k = lay.window_of(p ^ s, row, False)
-                valid = (k >= 0) & (k < (other_count_ref if crosses else count_ref)[0, 0])
-                outside, partner, halo = masks((place_ref, other_ref), row, k, p, lay, start)
-                inside, partner = ~outside & valid, partner & valid
-                for i, rows in enumerate((partner, inside) if crosses else (inside, partner)):
-                    for c in range(4):
-                        g = jnp.where(rows, blocks[c // 2 * n + s][c % 2, few_rows, :], 0.0)
-                        x = jnp.where(halo, g, 0.0)
-                        totals[c][i] += jnp.where(halo, 0.0, g)
-                        edges[c][i] += jnp.where(low, x[:, : 2 * m], x[:, t - 2 * m :])
-            for c in range(4):
-                for i in range(2):
-                    own_ref[i, c, few_rows, :] = totals[c][i]
-                    halo_ref[i, c, few_rows, :] = edges[c][i]
-
-        by_rows(lay, few)
+        low = iota((lay.h, 2 * m), 1) < m
+        own_ref[0] = momentum_rate * mom_ref[...]
+        own_ref[1] = jnp.zeros(own_ref.shape[1:], F32)
+        halo_ref[...] = jnp.zeros(halo_ref.shape, F32)
+        for s in range(n):
+            crosses = lay.crosses(s, False)
+            row = 1 - a if crosses else a
+            k = lay.window_of(p ^ s, row, False)
+            valid = (k >= 0) & (k < lay.half)
+            cells = lambda row=row, k=k: masks((place_ref, other_ref), row, k, p, lay, slice(0, lay.h))
+            reaches = cells()[3]
+
+            def add(i, rows, halo, s=s):
+                inner, left, right = rows & ~halo, (rows & halo)[:, : 2 * m] & low, (rows & halo)[:, t - 2 * m :] & ~low
+                for c in range(4):
+                    g = blocks[c // 2 * n + s][c % 2]
+                    own_ref[i, c] += jnp.where(inner, g, 0.0)
+                    halo_ref[i, c] += jnp.where(left, g[:, : 2 * m], jnp.where(right, g[:, t - 2 * m :], 0.0))
+
+            @pl.when(valid)
+            def _(i=int(crosses), cells=cells, add=add):
+                outside, _, halo, _ = cells()
+                add(i, ~outside, halo)
+
+            @pl.when(valid & reaches)
+            def _(i=1 - int(crosses), cells=cells, add=add):
+                _, partner, halo, _ = cells()
+                add(i, partner, halo)
 
     return body
 
@@ -469,7 +484,6 @@
     cores = lambda x: lax.ppermute(x, "ty", [(0, 1), (1, 0)])
     partner = cores(own)
     other_offsets = cores(offsets)
-    other_counts = cores(entry_counts)
     (own,) = move(pltpu.VMEM, own)
     ntx = lay.ntx
     shift = [(b, b + 1) for b in range(ntx - 1)] + [(ntx - 1, 2 * ntx - 1)]
@@ -531,8 +545,8 @@
     sums, halos = call(
         kernel_collect(lay),
         [(2, *block), (2, *halo_shape)],
-        [offsets, other_offsets, entry_counts, other_counts, *parts_first, *parts_second, velocity_old],
-        4,
+        [offsets, other_offsets, *parts_first, *parts_second, velocity_old],
+        2,
     )
     sums, halos, strips = call(
         kernel_strips_back(lay),

time: 67.3 us -> 70.2 us (1.043)
  waiting for transfers between devices: 27.7 us -> 30.9 us
  Pallas kernels: 12.8 us -> 11.9 us
    ppermute x18, waiting for transfers between devices: 12.1 us -> 15.5 us  [exchange(): got.append(lax.ppermute(values[s], ('ty', 'pos'), complete(pairs_of(s), n)))]
    pallas_call x13, Pallas kernels: 9.47 us -> 8.57 us  [call(): pl.pallas_call(body, out_shape=tuple(((jax.ShapeDtypeStruct if last else...]
    ppermute x7 -> x6, waiting for transfers between devices: 5.2 us -> 4.86 us  [iteration(): cores = lambda x: lax.ppermute(x, 'ty', [(0, 1), (1, 0)])]
    ppermute x7 -> x6, starting transfers between devices: 2.1 us -> 2.02 us  [iteration(): cores = lambda x: lax.ppermute(x, 'ty', [(0, 1), (1, 0)])]
  transfers between devices with their start and end apart: 28 -> 27, of which waited for: 15 -> 13; matrix products, arithmetic and copies ran while one was open for 0% -> 0% of each run, Pallas kernels for 11% -> 10%
where the time goes in v7:
time: 70.2 us; the launch traced here: 69.1 us
  waiting for transfers between devices  30.9 us (44%)
  starting transfers between devices  24.7 us (35%)
  Pallas kernels  11.9 us (17%)
  between operations  1.52 us (2%)
    ppermute x18, starting transfers between devices, exchange(): got.append(lax.ppermute(values[s], ('ty', 'pos'), complete(pairs_of(s), n)))  22.3 us
    ppermute x18, waiting for transfers between devices, exchange(): got.append(lax.ppermute(values[s], ('ty', 'pos'), complete(pairs_of(s), n)))  15.5 us
    ppermute x2, waiting for transfers between devices, iteration(): columns = lambda x: lax.ppermute(x, ('ty', 'tx'), shift)  10.5 us
    pallas_call x13, Pallas kernels, call(): pl.pallas_call(body, out_shape=tuple(((jax.ShapeDtypeStruct if last else...  8.57 us
    ppermute x6, waiting for transfers between devices, iteration(): cores = lambda x: lax.ppermute(x, 'ty', [(0, 1), (1, 0)])  4.86 us
    pallas_call x3, Pallas kernels, move(): pl.pallas_call(body, out_shape=tuple((target(x.shape, x.dtype) for x in a...  3.35 us
    ppermute x6, starting transfers between devices, iteration(): cores = lambda x: lax.ppermute(x, 'ty', [(0, 1), (1, 0)])  2.02 us
  transfers between devices with their start and end apart: 27, of which 13 were waited for; matrix products, arithmetic and copies ran while one was open for 0% of the time, Pallas kernels for 10%

profile of v7, /device:TPU:1, one launch (start us, length us, event | category | flops | bytes accessed | tf_op | source)
XLA Modules:
  0.0 69.1 jit_solution(15436935024491790800)
XLA Ops:
  0.7 1.0 %shard_map.103.own_ref.obj_ref = f32[4,64,256]{2,1,0:T(8,128)S(1)} custom-call(f32[4,64,256]{2,1,0:T(8,128)} %bitcast.12), custom_call_target="tpu_custom_call" | custom-call | tf_op jit(solution)/shard_map/pallas_call | solution.py:229
  2.9 4.6 %collective-permute-done.2.mine_ref = f32[4,64,128]{2,1,0:T(8,128)S(1)} collective-permute-done((f32[4,64,128]{2,1,0:T(8,128)S(1)}, f32[4,64,128]{2,1,0:T(8,128)S(1)}, u32[]{:S(2)}, u32[]{:S(2)}) %collective-permute-start.2) | collective-permute-done | bytes 131104 | tf_op jit(solution)/shard_map/ppermute | solution.py:491
  7.5 0.8 %collective-permute-start.3 = (f32[4,64,128]{2,1,0:T(8,128)S(1)}, f32[4,64,128]{2,1,0:T(8,128)S(1)}, u32[]{:S(2)}, u32[]{:S(2)}) collective-permute-start(f32[4,64,128]{2,1,0:T(8,128)S(1)} %collective-permute-done.2.mine_ref), channel_id=1, source_target_pairs={{0,16},{16,0},{1,17},{17,1},{2,18},{18,2},{3,19},{19,3},{4,20},{20... | collective-permute-start | bytes 393224 | tf_op jit(solution)/shard_map/ppermute | solution.py:484
  8.4 1.2 %collective-permute-done.1.other_ref = s32[1,1,2,4]{3,2,1,0:T(2,128)S(1)} collective-permute-done((s32[1,1,2,4]{3,2,1,0:T(2,128)S(1)}, s32[1,1,2,4]{3,2,1,0:T(2,128)S(1)}, u32[]{:S(2)}, u32[]{:S(2)}) %collective-permute-start.1) | collective-permute-done | bytes 64 | tf_op jit(solution)/shard_map/ppermute | solution.py:484
  9.5 0.9 %shard_map.105 = (f32[2,64,256]{2,1,0:T(8,128)S(1)}, f32[2,64,256]{2,1,0:T(8,128)S(1)}, f32[2,64,256]{2,1,0:T(8,128)S(1)}, f32[2,64,256]{2,1,0:T(8,128)S(1)}, f3...) custom-call(s32[1,1,2,4]{3,2,1,0:T(2,128)S(1)} %bitcast.6, ...), custom_call_target="tpu_custom_call" | custom-call | tf_op jit(solution)/shard_map/pallas_call | solution.py:30
  10.4 1.3 %collective-permute-start.7 = (f32[2,64,256]{2,1,0:T(8,128)S(1)}, f32[2,64,256]{2,1,0:T(8,128)S(1)}, u32[]{:S(2)}, u32[]{:S(2)}) collective-permute-start(f32[2,64,256]{2,1,0:T(8,128)S(1)} %get-tuple-element.51), channel_id=1, source_target_pairs={{16,1},{17,0},{2,19},{3,18},{0,16},{1,17},{18,2},{19,3},{20,5},{21... | collective-permute-start | bytes 393224 | tf_op jit(solution)/shard_map/ppermute | solution.py:496
  11.9 1.4 %collective-permute-start.8 = (f32[2,64,256]{2,1,0:T(8,128)S(1)}, f32[2,64,256]{2,1,0:T(8,128)S(1)}, u32[]{:S(2)}, u32[]{:S(2)}) collective-permute-start(f32[2,64,256]{2,1,0:T(8,128)S(1)} %get-tuple-element.52), channel_id=1, source_target_pairs={{2,0},{3,1},{16,18},{17,19},{0,16},{1,17},{18,2},{19,3},{6,4},{7,5... | collective-permute-start | bytes 393224 | tf_op jit(solution)/shard_map/ppermute | solution.py:496
  14.0 2.1 %collective-permute-start.5 = (f32[2,64,256]{2,1,0:T(8,128)S(1)}, f32[2,64,256]{2,1,0:T(8,128)S(1)}, u32[]{:S(2)}, u32[]{:S(2)}) collective-permute-start(f32[2,64,256]{2,1,0:T(8,128)S(1)} %get-tuple-element.48), channel_id=1, source_target_pairs={{2,0},{3,1},{16,18},{17,19},{0,16},{1,17},{18,2},{19,3},{6,4},{7,5... | collective-permute-start | bytes 393224 | tf_op jit(solution)/shard_map/ppermute | solution.py:496
  16.1 1.9 %collective-permute-done.8.refs_2_ = f32[2,64,256]{2,1,0:T(8,128)S(1)} collective-permute-done((f32[2,64,256]{2,1,0:T(8,128)S(1)}, f32[2,64,256]{2,1,0:T(8,128)S(1)}, u32[]{:S(2)}, u32[]{:S(2)}) %collective-permute-start.8) | collective-permute-done | bytes 131104 | tf_op jit(solution)/shard_map/ppermute | solution.py:496
  18.0 2.8 %collective-permute-start.6 = (f32[2,64,256]{2,1,0:T(8,128)S(1)}, f32[2,64,256]{2,1,0:T(8,128)S(1)}, u32[]{:S(2)}, u32[]{:S(2)}) collective-permute-start(f32[2,64,256]{2,1,0:T(8,128)S(1)} %get-tuple-element.49), channel_id=1, source_target_pairs={{2,1},{3,0},{16,19},{17,18},{0,16},{1,17},{18,2},{19,3},{6,5},{7,4... | collective-permute-start | bytes 393224 | tf_op jit(solution)/shard_map/ppermute | solution.py:496
  21.5 1.6 %shard_map.106 = (f32[4,64,256]{2,1,0:T(8,128)S(1)}, f32[1,1,1,256,256]{4,3,2,1,0:T(8,128)S(1)}, f32[2,256,256]{2,1,0:T(8,128)S(1)}, f32[256,256]{1,0:T(8,128)S(1)}, bf16[6,256,256]{2,1,0:T(8,128)(2,1)S(1)}) custom-call(f32[4,64,256]{2,1,0:T(8,128)} %bitcast.13, f32[1,1,1,256,256]{4,3,2,1,0:T(8,128)} %refs_1_.1, f32[2,256,256]{2,1,0:T(8,128)} %refs_2_.1, ...), custom_call_target="tpu_custom_call" | custom-call | tf_op jit(solution)/shard_map/pallas_call | solution.py:229
  23.4 0.8 %shard_map.107.refs_4_.light_ref = f32[2,256,256]{2,1,0:T(8,128)S(1)} custom-call(s32[1,1,2,4]{3,2,1,0:T(2,128)S(1)} %bitcast.7, f32[2,256,256]{2,1,0:T(8,128)S(1)} %get-tuple-element.54.light_ref), custom_call_target="tpu_custom_call" | custom-call | tf_op jit(solution)/shard_map/pallas_call | solution.py:30
  24.4 6.1 %collective-permute-start.11 = (f32[2,64,256]{2,1,0:T(8,128)S(1)}, f32[2,64,256]{2,1,0:T(8,128)S(1)}, u32[]{:S(2)}, u32[]{:S(2)}) collective-permute-start(f32[2,64,256]{2,1,0:T(8,128)S(1)} %get-tuple-element.60), channel_id=1, source_target_pairs={{1,16},{0,17},{19,2},{18,3},{2,18},{3,19},{16,0},{17,1},{5,20},{4,... | collective-permute-start | bytes 393224 | tf_op jit(solution)/shard_map/ppermute | solution.py:496
  30.7 0.9 %collective-permute-start.15 = (f32[2,64,256]{2,1,0:T(8,128)S(1)}, f32[2,64,256]{2,1,0:T(8,128)S(1)}, u32[]{:S(2)}, u32[]{:S(2)}) collective-permute-start(f32[2,64,256]{2,1,0:T(8,128)S(1)} %get-tuple-element.65), channel_id=1, source_target_pairs={{0,2},{1,3},{18,16},{19,17},{2,18},{3,19},{16,0},{17,1},{4,6},{5,7... | collective-permute-start | bytes 393224 | tf_op jit(solution)/shard_map/ppermute | solution.py:496
  31.6 2.0 %collective-permute-done.11.refs_1_ = f32[2,64,256]{2,1,0:T(8,128)S(1)} collective-permute-done((f32[2,64,256]{2,1,0:T(8,128)S(1)}, f32[2,64,256]{2,1,0:T(8,128)S(1)}, u32[]{:S(2)}, u32[]{:S(2)}) %collective-permute-start.11) | collective-permute-done | bytes 131104 | tf_op jit(solution)/shard_map/ppermute | solution.py:496
  33.7 2.1 %collective-permute-done.12.refs_2_ = f32[2,64,256]{2,1,0:T(8,128)S(1)} collective-permute-done((f32[2,64,256]{2,1,0:T(8,128)S(1)}, f32[2,64,256]{2,1,0:T(8,128)S(1)}, u32[]{:S(2)}, u32[]{:S(2)}) %collective-permute-start.12) | collective-permute-done | bytes 131104 | tf_op jit(solution)/shard_map/ppermute | solution.py:496
  36.5 2.1 %collective-permute-done.15.refs_6_ = f32[2,64,256]{2,1,0:T(8,128)S(1)} collective-permute-done((f32[2,64,256]{2,1,0:T(8,128)S(1)}, f32[2,64,256]{2,1,0:T(8,128)S(1)}, u32[]{:S(2)}, u32[]{:S(2)}) %collective-permute-start.15) | collective-permute-done | bytes 131104 | tf_op jit(solution)/shard_map/ppermute | solution.py:496
  38.6 0.9 %shard_map.112 = (f32[2,4,64,256]{3,2,1,0:T(8,128)S(1)}, f32[2,4,64,128]{3,2,1,0:T(8,128)S(1)}) custom-call(s32[1,1,2,4]{3,2,1,0:T(2,128)S(1)} %bitcast.8, s32[1,1,2,4]{3,2,1,0:T(2,128)S(1)} %collective-permute-done.1.other_ref, f32[2,64,256]{2,1,0:T(8,128)S(1)} %get-tuple-element.59.refs_0_, f32[2,64,256]{2,1,0:T(8,128)S(1)} %collective-permute-done.11.refs_1_, ...), custom_call_target="tpu_custom_call" | custom-call | tf_op jit(solution)/shard_map/pallas_call | solution.py:30
  40.0 1.8 %collective-permute-done.18.their_halo_ref = f32[2,4,64,128]{3,2,1,0:T(8,128)S(1)} collective-permute-done((f32[2,4,64,128]{3,2,1,0:T(8,128)S(1)}, f32[2,4,64,128]{3,2,1,0:T(8,128)S(1)}, u32[]{:S(2)}, u32[]{:S(2)}) %collective-permute-start.18) | collective-permute-done | bytes 262176 | tf_op jit(solution)/shard_map/ppermute | solution.py:484
  42.1 5.8 %collective-permute-done.19.mine_ref = f32[2,4,64,128]{3,2,1,0:T(8,128)S(1)} collective-permute-done((f32[2,4,64,128]{3,2,1,0:T(8,128)S(1)}, f32[2,4,64,128]{3,2,1,0:T(8,128)S(1)}, u32[]{:S(2)}, u32[]{:S(2)}) %collective-permute-start.19) | collective-permute-done | bytes 262176 | tf_op jit(solution)/shard_map/ppermute | solution.py:491
  48.5 1.2 %collective-permute-done.20.theirs_ref = f32[2,4,64,128]{3,2,1,0:T(8,128)S(1)} collective-permute-done((f32[2,4,64,128]{3,2,1,0:T(8,128)S(1)}, f32[2,4,64,128]{3,2,1,0:T(8,128)S(1)}, u32[]{:S(2)}, u32[]{:S(2)}) %collective-permute-start.20) | collective-permute-done | bytes 262176 | tf_op jit(solution)/shard_map/ppermute | solution.py:484
  49.6 0.9 %shard_map.114 = (f32[4,64,256]{2,1,0:T(8,128)S(1)}, f32[4,64,256]{2,1,0:T(8,128)S(1)}, f32[2,64,256]{2,1,0:T(8,128)S(1)}, f32[2,64,256]{2,1,0:T(8,128)S(1)}, f3...) custom-call(s32[1,1,2,4]{3,2,1,0:T(2,128)S(1)} %bitcast.9, ...), custom_call_target="tpu_custom_call" | custom-call | tf_op jit(solution)/shard_map/pallas_call | solution.py:30
  51.2 0.8 %collective-permute-start.21 = (f32[2,64,256]{2,1,0:T(8,128)S(1)}, f32[2,64,256]{2,1,0:T(8,128)S(1)}, u32[]{:S(2)}, u32[]{:S(2)}) collective-permute-start(f32[2,64,256]{2,1,0:T(8,128)S(1)} %get-tuple-element.78), channel_id=1, source_target_pairs={{0,1},{1,0},{16,17},{17,16},{2,18},{3,19},{18,2},{19,3},{4,5},{5,4... | collective-permute-start | bytes 393224 | tf_op jit(solution)/shard_map/ppermute | solution.py:496
  52.1 1.3 %collective-permute-start.25 = (f32[2,64,256]{2,1,0:T(8,128)S(1)}, f32[2,64,256]{2,1,0:T(8,128)S(1)}, u32[]{:S(2)}, u32[]{:S(2)}) collective-permute-start(f32[2,64,256]{2,1,0:T(8,128)S(1)} %get-tuple-element.83), channel_id=1, source_target_pairs={{2,0},{3,1},{18,16},{19,17},{6,4},{7,5},{22,20},{23,21},{10,8},{11... | collective-permute-start | bytes 393224 | tf_op jit(solution)/shard_map/ppermute | solution.py:496
  53.4 1.3 %collective-permute-start.26 = (f32[2,64,256]{2,1,0:T(8,128)S(1)}, f32[2,64,256]{2,1,0:T(8,128)S(1)}, u32[]{:S(2)}, u32[]{:S(2)}) collective-permute-start(f32[2,64,256]{2,1,0:T(8,128)S(1)} %get-tuple-element.84), channel_id=1, source_target_pairs={{2,1},{3,0},{18,17},{19,16},{6,5},{7,4},{22,21},{23,20},{10,9},{11... | collective-permute-start | bytes 393224 | tf_op jit(solution)/shard_map/ppermute | solution.py:496
  54.7 1.3 %collective-permute-start.22 = (f32[2,64,256]{2,1,0:T(8,128)S(1)}, f32[2,64,256]{2,1,0:T(8,128)S(1)}, u32[]{:S(2)}, u32[]{:S(2)}) collective-permute-start(f32[2,64,256]{2,1,0:T(8,128)S(1)} %get-tuple-element.79), channel_id=1, source_target_pairs={{2,0},{3,1},{18,16},{19,17},{6,4},{7,5},{22,20},{23,21},{10,8},{11... | collective-permute-start | bytes 393224 | tf_op jit(solution)/shard_map/ppermute | solution.py:496
  56.0 1.3 %collective-permute-start.23 = (f32[2,64,256]{2,1,0:T(8,128)S(1)}, f32[2,64,256]{2,1,0:T(8,128)S(1)}, u32[]{:S(2)}, u32[]{:S(2)}) collective-permute-start(f32[2,64,256]{2,1,0:T(8,128)S(1)} %get-tuple-element.80), channel_id=1, source_target_pairs={{2,1},{3,0},{18,17},{19,16},{6,5},{7,4},{22,21},{23,20},{10,9},{11... | collective-permute-start | bytes 393224 | tf_op jit(solution)/shard_map/ppermute | solution.py:496
  58.1 0.8 %shard_map.115 = (f32[4,64,256]{2,1,0:T(8,128)}, f32[4,64,256]{2,1,0:T(8,128)}) custom-call(f32[4,64,256]{2,1,0:T(8,128)S(1)} %get-tuple-element.73.refs_0_, f32[4,64,256]{2,1,0:T(8,128)S(1)} %get-tuple-element.74.refs_1_), custom_call_target="tpu_custom_call" | custom-call | tf_op jit(solution)/shard_map/pallas_call | solution.py:229
  58.9 1.5 %collective-permute-done.26.refs_3_ = f32[2,64,256]{2,1,0:T(8,128)S(1)} collective-permute-done((f32[2,64,256]{2,1,0:T(8,128)S(1)}, f32[2,64,256]{2,1,0:T(8,128)S(1)}, u32[]{:S(2)}, u32[]{:S(2)}) %collective-permute-start.26) | collective-permute-done | bytes 131104 | tf_op jit(solution)/shard_map/ppermute | solution.py:496
  60.4 1.8 %shard_map.117.refs_4_ = f32[2,256,256]{2,1,0:T(8,128)S(1)} custom-call(s32[1,1]{1,0:T(1,128)S(6)} %copy.11.count_ref, f32[2,64,256]{2,1,0:T(8,128)S(1)} %get-tuple-element.81.refs_0_, f32[2,64,256]{2,1,0:T(8,128)S(1)} %collective-permute-done.24.refs_1_, f32[2,64,256]{2,1,0:T(8,128)S(1)} %collective-permute-done.25.refs_2_, ...), custom_call_target="tpu_custom_call" | custom-call | tf_op jit(solution)/shard_map/pallas_call | solution.py:30
  62.2 5.2 %collective-permute-done.22.refs_2_ = f32[2,64,256]{2,1,0:T(8,128)S(1)} collective-permute-done((f32[2,64,256]{2,1,0:T(8,128)S(1)}, f32[2,64,256]{2,1,0:T(8,128)S(1)}, u32[]{:S(2)}, u32[]{:S(2)}) %collective-permute-start.22) | collective-permute-done | bytes 131104 | tf_op jit(solution)/shard_map/ppermute | solution.py:496
  67.4 1.7 %shard_map.118 = f32[1,1,1,256,256]{4,3,2,1,0:T(8,128)} custom-call(s32[1,1]{1,0:T(1,128)S(6)} %copy.11.count_ref, f32[2,64,256]{2,1,0:T(8,128)S(1)} %get-tuple-element.77.refs_0_, f32[2,64,256]{2,1,0:T(8,128)S(1)} %collective-permute-done.21.refs_1_, f32[2,64,256]{2,1,0:T(8,128)S(1)} %collective-permute-done.22.refs_2_, ...), custom_call_target="tpu_custom_call" | custom-call | tf_op jit(solution)/shard_map/pallas_call | solution.py:30
  (42 shorter events, 6.4 us)
Async XLA Ops:
  0.6 1.8 %collective-permute-start = (f32[4,64,256]{2,1,0:T(8,128)}, f32[4,64,256]{2,1,0:T(8,128)S(1)}, u32[]{:S(2)}, u32[]{:S(2)}) collective-permute-start(f32[4,64,256]{2,1,0:T(8,128)} %bitcast.11), channel_id=1, source_target_pairs={{0,16},{16,0},{1,17},{17,1},{2,18},{18,2},{3,19},{19,3},{4,20},{20... | collective-permute-start | bytes 786440 | tf_op jit(solution)/shard_map/ppermute | solution.py:484
  2.7 5.6 %copy-start = (s32[1,1,4,2]{2,3,1,0:T(2,128)S(1)}, s32[1,1,4,2]{2,3,1,0:T(2,128)}, u32[]{:S(2)}) copy-start(s32[1,1,4,2]{2,3,1,0:T(2,128)} %param.13) | copy-start | bytes 100
  2.8 4.8 %collective-permute-start.2 = (f32[4,64,128]{2,1,0:T(8,128)S(1)}, f32[4,64,128]{2,1,0:T(8,128)S(1)}, u32[]{:S(2)}, u32[]{:S(2)}) collective-permute-start(f32[4,64,128]{2,1,0:T(8,128)S(1)} %shard_map.104), channel_id=1, source_target_pairs={{0,4},{4,8},{8,12},{12,28},{20,16},{24,20},{28,24},{16,0},{1,5},{5... | collective-permute-start | bytes 393224 | tf_op jit(solution)/shard_map/ppermute | solution.py:491
  7.5 2.0 %collective-permute-start.3 = (f32[4,64,128]{2,1,0:T(8,128)S(1)}, f32[4,64,128]{2,1,0:T(8,128)S(1)}, u32[]{:S(2)}, u32[]{:S(2)}) collective-permute-start(f32[4,64,128]{2,1,0:T(8,128)S(1)} %collective-permute-done.2.mine_ref), channel_id=1, source_target_pairs={{0,16},{16,0},{1,17},{17,1},{2,18},{18,2},{3,19},{19,3},{4,20},{20... | collective-permute-start | bytes 393224 | tf_op jit(solution)/shard_map/ppermute | solution.py:484
  8.4 3.4 %copy-start.1 = (f32[1,1,1,256,256]{4,3,2,1,0:T(8,128)S(1)}, f32[1,1,1,256,256]{4,3,2,1,0:T(8,128)}, u32[]{:S(2)}) copy-start(f32[1,1,1,256,256]{4,3,2,1,0:T(8,128)} %refs_1_.1) | copy-start | bytes 786436
  8.4 1.2 %collective-permute-start.1 = (s32[1,1,2,4]{3,2,1,0:T(2,128)S(1)}, s32[1,1,2,4]{3,2,1,0:T(2,128)S(1)}, u32[]{:S(2)}, u32[]{:S(2)}) collective-permute-start(s32[1,1,2,4]{3,2,1,0:T(2,128)S(1)} %bitcast.5), channel_id=1, source_target_pairs={{0,16},{16,0},{1,17},{17,1},{2,18},{18,2},{3,19},{19,3},{4,20},{20... | collective-permute-start | bytes 104 | tf_op jit(solution)/shard_map/ppermute | solution.py:484
  10.4 3.6 %collective-permute-start.7 = (f32[2,64,256]{2,1,0:T(8,128)S(1)}, f32[2,64,256]{2,1,0:T(8,128)S(1)}, u32[]{:S(2)}, u32[]{:S(2)}) collective-permute-start(f32[2,64,256]{2,1,0:T(8,128)S(1)} %get-tuple-element.51), channel_id=1, source_target_pairs={{16,1},{17,0},{2,19},{3,18},{0,16},{1,17},{18,2},{19,3},{20,5},{21... | collective-permute-start | bytes 393224 | tf_op jit(solution)/shard_map/ppermute | solution.py:496
  11.8 12.5 %collective-permute-start.10 = (f32[1,1,1,256,256]{4,3,2,1,0:T(8,128)S(1)}, f32[1,1,1,256,256]{4,3,2,1,0:T(8,128)S(1)}, u32[]{:S(2)}, u32[]{:S(2)}) collective-permute-start(f32[1,1,1,256,256]{4,3,2,1,0:T(8,128)S(1)} %copy-done.1), channel_id=1, source_target_pairs={{16,18},{17,19},{2,0},{3,1},{0,16},{1,17},{18,2},{19,3},{20,22},{2... | collective-permute-start | bytes 786440 | tf_op jit(solution)/shard_map/ppermute | solution.py:502
  11.9 6.1 %collective-permute-start.8 = (f32[2,64,256]{2,1,0:T(8,128)S(1)}, f32[2,64,256]{2,1,0:T(8,128)S(1)}, u32[]{:S(2)}, u32[]{:S(2)}) collective-permute-start(f32[2,64,256]{2,1,0:T(8,128)S(1)} %get-tuple-element.52), channel_id=1, source_target_pairs={{2,0},{3,1},{16,18},{17,19},{0,16},{1,17},{18,2},{19,3},{6,4},{7,5... | collective-permute-start | bytes 393224 | tf_op jit(solution)/shard_map/ppermute | solution.py:496
  13.3 10.9 %collective-permute-start.9 = (f32[2,64,256]{2,1,0:T(8,128)S(1)}, f32[2,64,256]{2,1,0:T(8,128)S(1)}, u32[]{:S(2)}, u32[]{:S(2)}) collective-permute-start(f32[2,64,256]{2,1,0:T(8,128)S(1)} %get-tuple-element.53), channel_id=1, source_target_pairs={{2,1},{3,0},{16,19},{17,18},{0,16},{1,17},{18,2},{19,3},{6,5},{7,4... | collective-permute-start | bytes 393224 | tf_op jit(solution)/shard_map/ppermute | solution.py:496
  13.7 10.6 %collective-permute-start.4 = (f32[2,64,256]{2,1,0:T(8,128)S(1)}, f32[2,64,256]{2,1,0:T(8,128)S(1)}, u32[]{:S(2)}, u32[]{:S(2)}) collective-permute-start(f32[2,64,256]{2,1,0:T(8,128)S(1)} %get-tuple-element.47), channel_id=1, source_target_pairs={{16,1},{17,0},{2,19},{3,18},{0,16},{1,17},{18,2},{19,3},{20,5},{21... | collective-permute-start | bytes 393224 | tf_op jit(solution)/shard_map/ppermute | solution.py:496
  14.0 10.3 %collective-permute-start.5 = (f32[2,64,256]{2,1,0:T(8,128)S(1)}, f32[2,64,256]{2,1,0:T(8,128)S(1)}, u32[]{:S(2)}, u32[]{:S(2)}) collective-permute-start(f32[2,64,256]{2,1,0:T(8,128)S(1)} %get-tuple-element.48), channel_id=1, source_target_pairs={{2,0},{3,1},{16,18},{17,19},{0,16},{1,17},{18,2},{19,3},{6,4},{7,5... | collective-permute-start | bytes 393224 | tf_op jit(solution)/shard_map/ppermute | solution.py:496
  18.0 6.3 %collective-permute-start.6 = (f32[2,64,256]{2,1,0:T(8,128)S(1)}, f32[2,64,256]{2,1,0:T(8,128)S(1)}, u32[]{:S(2)}, u32[]{:S(2)}) collective-permute-start(f32[2,64,256]{2,1,0:T(8,128)S(1)} %get-tuple-element.49), channel_id=1, source_target_pairs={{2,1},{3,0},{16,19},{17,18},{0,16},{1,17},{18,2},{19,3},{6,5},{7,4... | collective-permute-start | bytes 393224 | tf_op jit(solution)/shard_map/ppermute | solution.py:496
  24.4 9.2 %collective-permute-start.11 = (f32[2,64,256]{2,1,0:T(8,128)S(1)}, f32[2,64,256]{2,1,0:T(8,128)S(1)}, u32[]{:S(2)}, u32[]{:S(2)}) collective-permute-start(f32[2,64,256]{2,1,0:T(8,128)S(1)} %get-tuple-element.60), channel_id=1, source_target_pairs={{1,16},{0,17},{19,2},{18,3},{2,18},{3,19},{16,0},{17,1},{5,20},{4,... | collective-permute-start | bytes 393224 | tf_op jit(solution)/shard_map/ppermute | solution.py:496
  30.5 5.2 %collective-permute-start.12 = (f32[2,64,256]{2,1,0:T(8,128)S(1)}, f32[2,64,256]{2,1,0:T(8,128)S(1)}, u32[]{:S(2)}, u32[]{:S(2)}) collective-permute-start(f32[2,64,256]{2,1,0:T(8,128)S(1)} %get-tuple-element.61), channel_id=1, source_target_pairs={{0,2},{1,3},{18,16},{19,17},{2,18},{3,19},{16,0},{17,1},{4,6},{5,7... | collective-permute-start | bytes 393224 | tf_op jit(solution)/shard_map/ppermute | solution.py:496
  30.6 5.2 %collective-permute-start.13 = (f32[2,64,256]{2,1,0:T(8,128)S(1)}, f32[2,64,256]{2,1,0:T(8,128)S(1)}, u32[]{:S(2)}, u32[]{:S(2)}) collective-permute-start(f32[2,64,256]{2,1,0:T(8,128)S(1)} %get-tuple-element.62), channel_id=1, source_target_pairs={{1,2},{0,3},{19,16},{18,17},{2,18},{3,19},{16,0},{17,1},{5,6},{4,7... | collective-permute-start | bytes 393224 | tf_op jit(solution)/shard_map/ppermute | solution.py:496
  30.6 5.9 %collective-permute-start.14 = (f32[2,64,256]{2,1,0:T(8,128)S(1)}, f32[2,64,256]{2,1,0:T(8,128)S(1)}, u32[]{:S(2)}, u32[]{:S(2)}) collective-permute-start(f32[2,64,256]{2,1,0:T(8,128)S(1)} %get-tuple-element.64), channel_id=1, source_target_pairs={{1,16},{0,17},{19,2},{18,3},{2,18},{3,19},{16,0},{17,1},{5,20},{4,... | collective-permute-start | bytes 393224 | tf_op jit(solution)/shard_map/ppermute | solution.py:496
  30.7 7.9 %collective-permute-start.15 = (f32[2,64,256]{2,1,0:T(8,128)S(1)}, f32[2,64,256]{2,1,0:T(8,128)S(1)}, u32[]{:S(2)}, u32[]{:S(2)}) collective-permute-start(f32[2,64,256]{2,1,0:T(8,128)S(1)} %get-tuple-element.65), channel_id=1, source_target_pairs={{0,2},{1,3},{18,16},{19,17},{2,18},{3,19},{16,0},{17,1},{4,6},{5,7... | collective-permute-start | bytes 393224 | tf_op jit(solution)/shard_map/ppermute | solution.py:496
  33.7 4.9 %collective-permute-start.16 = (f32[2,64,256]{2,1,0:T(8,128)S(1)}, f32[2,64,256]{2,1,0:T(8,128)S(1)}, u32[]{:S(2)}, u32[]{:S(2)}) collective-permute-start(f32[2,64,256]{2,1,0:T(8,128)S(1)} %get-tuple-element.66), channel_id=1, source_target_pairs={{1,2},{0,3},{19,16},{18,17},{2,18},{3,19},{16,0},{17,1},{5,6},{4,7... | collective-permute-start | bytes 393224 | tf_op jit(solution)/shard_map/ppermute | solution.py:496
  39.4 2.4 %collective-permute-start.17 = (f32[2,4,64,256]{3,2,1,0:T(8,128)S(1)}, f32[2,4,64,256]{3,2,1,0:T(8,128)S(1)}, u32[]{:S(2)}, u32[]{:S(2)}) collective-permute-start(f32[2,4,64,256]{3,2,1,0:T(8,128)S(1)} %get-tuple-element.68.own_ref), channel_id=1, source_target_pairs={{0,16},{16,0},{1,17},{17,1},{2,18},{18,2},{3,19},{19,3},{4,20},{20... | collective-permute-start | bytes 1572872 | tf_op jit(solution)/shard_map/ppermute | solution.py:484
  39.5 2.3 %collective-permute-start.18 = (f32[2,4,64,128]{3,2,1,0:T(8,128)S(1)}, f32[2,4,64,128]{3,2,1,0:T(8,128)S(1)}, u32[]{:S(2)}, u32[]{:S(2)}) collective-permute-start(f32[2,4,64,128]{3,2,1,0:T(8,128)S(1)} %get-tuple-element.69.halo_ref), channel_id=1, source_target_pairs={{0,16},{16,0},{1,17},{17,1},{2,18},{18,2},{3,19},{19,3},{4,20},{20... | collective-permute-start | bytes 786440 | tf_op jit(solution)/shard_map/ppermute | solution.py:484
  41.9 6.0 %collective-permute-start.19 = (f32[2,4,64,128]{3,2,1,0:T(8,128)S(1)}, f32[2,4,64,128]{3,2,1,0:T(8,128)S(1)}, u32[]{:S(2)}, u32[]{:S(2)}) collective-permute-start(f32[2,4,64,128]{3,2,1,0:T(8,128)S(1)} %get-tuple-element.72), channel_id=1, source_target_pairs={{0,4},{4,8},{8,12},{12,28},{20,16},{24,20},{28,24},{16,0},{1,5},{5... | collective-permute-start | bytes 786440 | tf_op jit(solution)/shard_map/ppermute | solution.py:491
  47.9 1.7 %collective-permute-start.20 = (f32[2,4,64,128]{3,2,1,0:T(8,128)S(1)}, f32[2,4,64,128]{3,2,1,0:T(8,128)S(1)}, u32[]{:S(2)}, u32[]{:S(2)}) collective-permute-start(f32[2,4,64,128]{3,2,1,0:T(8,128)S(1)} %collective-permute-done.19.mine_ref), channel_id=1, source_target_pairs={{0,16},{16,0},{1,17},{17,1},{2,18},{18,2},{3,19},{19,3},{4,20},{20... | collective-permute-start | bytes 786440 | tf_op jit(solution)/shard_map/ppermute | solution.py:484
  50.6 5.4 %collective-permute-start.24 = (f32[2,64,256]{2,1,0:T(8,128)S(1)}, f32[2,64,256]{2,1,0:T(8,128)S(1)}, u32[]{:S(2)}, u32[]{:S(2)}) collective-permute-start(f32[2,64,256]{2,1,0:T(8,128)S(1)} %get-tuple-element.82), channel_id=1, source_target_pairs={{0,1},{1,0},{16,17},{17,16},{2,18},{3,19},{18,2},{19,3},{4,5},{5,4... | collective-permute-start | bytes 393224 | tf_op jit(solution)/shard_map/ppermute | solution.py:496
  51.2 10.9 %collective-permute-start.21 = (f32[2,64,256]{2,1,0:T(8,128)S(1)}, f32[2,64,256]{2,1,0:T(8,128)S(1)}, u32[]{:S(2)}, u32[]{:S(2)}) collective-permute-start(f32[2,64,256]{2,1,0:T(8,128)S(1)} %get-tuple-element.78), channel_id=1, source_target_pairs={{0,1},{1,0},{16,17},{17,16},{2,18},{3,19},{18,2},{19,3},{4,5},{5,4... | collective-permute-start | bytes 393224 | tf_op jit(solution)/shard_map/ppermute | solution.py:496
  52.1 6.8 %collective-permute-start.25 = (f32[2,64,256]{2,1,0:T(8,128)S(1)}, f32[2,64,256]{2,1,0:T(8,128)S(1)}, u32[]{:S(2)}, u32[]{:S(2)}) collective-permute-start(f32[2,64,256]{2,1,0:T(8,128)S(1)} %get-tuple-element.83), channel_id=1, source_target_pairs={{2,0},{3,1},{18,16},{19,17},{6,4},{7,5},{22,20},{23,21},{10,8},{11... | collective-permute-start | bytes 393224 | tf_op jit(solution)/shard_map/ppermute | solution.py:496
  53.4 7.0 %collective-permute-start.26 = (f32[2,64,256]{2,1,0:T(8,128)S(1)}, f32[2,64,256]{2,1,0:T(8,128)S(1)}, u32[]{:S(2)}, u32[]{:S(2)}) collective-permute-start(f32[2,64,256]{2,1,0:T(8,128)S(1)} %get-tuple-element.84), channel_id=1, source_target_pairs={{2,1},{3,0},{18,17},{19,16},{6,5},{7,4},{22,21},{23,20},{10,9},{11... | collective-permute-start | bytes 393224 | tf_op jit(solution)/shard_map/ppermute | solution.py:496
  54.7 12.7 %collective-permute-start.22 = (f32[2,64,256]{2,1,0:T(8,128)S(1)}, f32[2,64,256]{2,1,0:T(8,128)S(1)}, u32[]{:S(2)}, u32[]{:S(2)}) collective-permute-start(f32[2,64,256]{2,1,0:T(8,128)S(1)} %get-tuple-element.79), channel_id=1, source_target_pairs={{2,0},{3,1},{18,16},{19,17},{6,4},{7,5},{22,20},{23,21},{10,8},{11... | collective-permute-start | bytes 393224 | tf_op jit(solution)/shard_map/ppermute | solution.py:496
  56.0 11.4 %collective-permute-start.23 = (f32[2,64,256]{2,1,0:T(8,128)S(1)}, f32[2,64,256]{2,1,0:T(8,128)S(1)}, u32[]{:S(2)}, u32[]{:S(2)}) collective-permute-start(f32[2,64,256]{2,1,0:T(8,128)S(1)} %get-tuple-element.80), channel_id=1, source_target_pairs={{2,1},{3,0},{18,17},{19,16},{6,5},{7,4},{22,21},{23,20},{10,9},{11... | collective-permute-start | bytes 393224 | tf_op jit(solution)/shard_map/ppermute | solution.py:496

commit v8 on v7

--- a/solution.py
+++ b/solution.py
@@ -147,7 +147,7 @@
     return outside, partner, halo, reaches
 
 
-def pack_blocks(place_refs, own, own_halo, prt, prt_halo, out_refs, lay, home):
+def pack_blocks(place_refs, own, own_halo, prt, prt_halo, out_refs, lay, home, parts):
     a, _, p = where_am_i()
 
     def few(_, rows):
@@ -155,13 +155,13 @@
             row = 1 - a if lay.crosses(s, home) else a
             k = lay.window_of(p ^ s, row, home)
             outside, partner, halo, _ = masks(place_refs, row, k, p, lay, rows)
-            for c in range(4):
+            for c in parts:
                 mine = jnp.where(halo, spread(own_halo[c, rows, :], lay), own[c, rows, :])
                 theirs = jnp.where(halo, spread(prt_halo[c, rows, :], lay), prt[c, rows, :])
                 if lay.crosses(s, home):
                     mine, theirs = theirs, mine
                 value = jnp.where(partner, theirs, jnp.where(outside, 0.0, mine))
-                out_refs[c // 2 * lay.n + s][c % 2, rows, :] = value
+                out_refs[(c - parts[0]) // 2 * lay.n + s][c % 2, rows, :] = value
 
     by_rows(lay, few, 8 if home else lay.h)
 
@@ -198,7 +198,7 @@
 
     def body(place_ref, other_ref, own_ref, prt_ref, mine_ref, theirs_ref, *outs):
         a, b, _ = where_am_i()
-        blocks, own_halo_ref, prt_halo_ref = outs[: 2 * lay.n], *outs[2 * lay.n :]
+        blocks, own_halo_ref, prt_halo_ref = outs[: lay.n], *outs[lay.n :]
         low = iota((lay.h, 2 * m), 1) < m
         keep = jnp.where(low, (b < lay.ntx - 1).astype(F32), (b > 0).astype(F32))
         for c in range(4):
@@ -208,7 +208,15 @@
             halo1 = jnp.where(low, roll_half(from_right, lay), roll_half(from_left, lay))
             own_halo_ref[c] = jnp.where(keep > 0, jnp.where(a == 0, halo0, halo1), 0.0)
             prt_halo_ref[c] = jnp.where(keep > 0, jnp.where(a == 0, halo1, halo0), 0.0)
-        pack_blocks((place_ref, other_ref), own_ref, own_halo_ref, prt_ref, prt_halo_ref, blocks, lay, False)
+        pack_blocks((place_ref, other_ref), own_ref, own_halo_ref, prt_ref, prt_halo_ref, blocks, lay, False, range(2))
+
+    return body
+
+
+def kernel_pack_second(lay):
+    def body(place_ref, other_ref, own_ref, prt_ref, own_halo_ref, prt_halo_ref, *outs):
+        places = (place_ref, other_ref)
+        pack_blocks(places, own_ref, own_halo_ref, prt_ref, prt_halo_ref, outs, lay, False, range(2, 4))
 
     return body
 
@@ -435,7 +443,7 @@
                     vel_ref[c] = v
                 new[c] = obj[c] - step_length * v
                 new_halo[c] = jnp.where(keep, halo[c] - step_length * hv, 0.0)
-        pack_blocks((place_ref, place_ref), new_ref, own_halo, prt_new, prt_halo, blocks, lay, True)
+        pack_blocks((place_ref, place_ref), new_ref, own_halo, prt_new, prt_halo, blocks, lay, True, range(4))
 
     return body
 
@@ -514,12 +522,15 @@
     strips_other = cores(strips)
     *blocks, own_halo, partner_halo = call(
         kernel_pack(lay),
-        [half_block] * (2 * n) + [halo_shape] * 2,
+        [half_block] * n + [halo_shape] * 2,
         [offsets, other_offsets, own, partner, strips, strips_other],
         2,
     )
-    first = exchange(blocks[:n], lambda s: lay.inward(s, False))
-    second = exchange(blocks[n:], lambda s: lay.inward(s, False))
+    more = call(
+        kernel_pack_second(lay), [half_block] * n, [offsets, other_offsets, own, partner, own_halo, partner_halo], 2
+    )
+    first = exchange(blocks, lambda s: lay.inward(s, False))
+    second = exchange(more, lambda s: lay.inward(s, False))
     half_window = pltpu.VMEM((2, t, t), F32)
 
     def propagated(first, light, home):

time: 70.2 us -> 70.2 us (level)
    ppermute x18, starting transfers between devices: 22.3 us -> 21.6 us  [exchange(): got.append(lax.ppermute(values[s], ('ty', 'pos'), complete(pairs_of(s), n)))]
    pallas_call x13 -> x14, Pallas kernels: 8.57 us -> 9.18 us  [call(): pl.pallas_call(body, out_shape=tuple(((jax.ShapeDtypeStruct if last else...]
  transfers between devices with their start and end apart: 27 -> 27, of which waited for: 13 -> 13; matrix products, arithmetic and copies ran while one was open for 0% -> 0% of each run, Pallas kernels for 10% -> 11%
where the time goes in v8:
time: 70.2 us; the launch traced here: 69 us
  waiting for transfers between devices  30.9 us (44%)
  starting transfers between devices  24 us (34%)
  Pallas kernels  12.5 us (18%)
  between operations  1.52 us (2%)
    ppermute x18, starting transfers between devices, exchange(): got.append(lax.ppermute(values[s], ('ty', 'pos'), complete(pairs_of(s), n)))  21.6 us
    ppermute x18, waiting for transfers between devices, exchange(): got.append(lax.ppermute(values[s], ('ty', 'pos'), complete(pairs_of(s), n)))  15.6 us
    ppermute x2, waiting for transfers between devices, iteration(): columns = lambda x: lax.ppermute(x, ('ty', 'tx'), shift)  10.5 us
    pallas_call x14, Pallas kernels, call(): pl.pallas_call(body, out_shape=tuple(((jax.ShapeDtypeStruct if last else...  9.18 us
    ppermute x6, waiting for transfers between devices, iteration(): cores = lambda x: lax.ppermute(x, 'ty', [(0, 1), (1, 0)])  4.86 us
    pallas_call x3, Pallas kernels, move(): pl.pallas_call(body, out_shape=tuple((target(x.shape, x.dtype) for x in a...  3.35 us
    ppermute x6, starting transfers between devices, iteration(): cores = lambda x: lax.ppermute(x, 'ty', [(0, 1), (1, 0)])  2.02 us
  transfers between devices with their start and end apart: 27, of which 13 were waited for; matrix products, arithmetic and copies ran while one was open for 0% of the time, Pallas kernels for 11%

profile of v8, /device:TPU:1, one launch (start us, length us, event | category | flops | bytes accessed | tf_op | source)
XLA Modules:
  0.0 69.0 jit_solution(6351428910878015297)
XLA Ops:
  0.7 1.0 %shard_map.103.own_ref.obj_ref = f32[4,64,256]{2,1,0:T(8,128)S(1)} custom-call(f32[4,64,256]{2,1,0:T(8,128)} %bitcast.13), custom_call_target="tpu_custom_call" | custom-call | tf_op jit(solution)/shard_map/pallas_call | solution.py:237
  2.9 4.6 %collective-permute-done.2.mine_ref = f32[4,64,128]{2,1,0:T(8,128)S(1)} collective-permute-done((f32[4,64,128]{2,1,0:T(8,128)S(1)}, f32[4,64,128]{2,1,0:T(8,128)S(1)}, u32[]{:S(2)}, u32[]{:S(2)}) %collective-permute-start.2) | collective-permute-done | bytes 131104 | tf_op jit(solution)/shard_map/ppermute | solution.py:499
  7.5 0.8 %collective-permute-start.3 = (f32[4,64,128]{2,1,0:T(8,128)S(1)}, f32[4,64,128]{2,1,0:T(8,128)S(1)}, u32[]{:S(2)}, u32[]{:S(2)}) collective-permute-start(f32[4,64,128]{2,1,0:T(8,128)S(1)} %collective-permute-done.2.mine_ref), channel_id=1, source_target_pairs={{0,16},{16,0},{1,17},{17,1},{2,18},{18,2},{3,19},{19,3},{4,20},{20... | collective-permute-start | bytes 393224 | tf_op jit(solution)/shard_map/ppermute | solution.py:492
  8.4 1.2 %collective-permute-done.1.other_ref = s32[1,1,2,4]{3,2,1,0:T(2,128)S(1)} collective-permute-done((s32[1,1,2,4]{3,2,1,0:T(2,128)S(1)}, s32[1,1,2,4]{3,2,1,0:T(2,128)S(1)}, u32[]{:S(2)}, u32[]{:S(2)}) %collective-permute-start.1) | collective-permute-done | bytes 64 | tf_op jit(solution)/shard_map/ppermute | solution.py:492
  9.5 0.8 %shard_map.105 = (f32[2,64,256]{2,1,0:T(8,128)S(1)}, f32[2,64,256]{2,1,0:T(8,128)S(1)}, f32[2,64,256]{2,1,0:T(8,128)S(1)}, f32[2,64,256]{2,1,0:T(8,128)S(1)}, f3...) custom-call(s32[1,1,2,4]{3,2,1,0:T(2,128)S(1)} %bitcast.6, s32[1,1,2,4]{3,2,1,0:T(2,128)S(1)} %collective-permute-done.1.other_ref, ...), custom_call_target="tpu_custom_call" | custom-call | tf_op jit(solution)/shard_map/pallas_call | solution.py:30
  10.3 1.3 %collective-permute-start.7 = (f32[2,64,256]{2,1,0:T(8,128)S(1)}, f32[2,64,256]{2,1,0:T(8,128)S(1)}, u32[]{:S(2)}, u32[]{:S(2)}) collective-permute-start(f32[2,64,256]{2,1,0:T(8,128)S(1)} %get-tuple-element.51), channel_id=1, source_target_pairs={{16,1},{17,0},{2,19},{3,18},{0,16},{1,17},{18,2},{19,3},{20,5},{21... | collective-permute-start | bytes 393224 | tf_op jit(solution)/shard_map/ppermute | solution.py:504
  11.8 1.4 %collective-permute-start.8 = (f32[2,64,256]{2,1,0:T(8,128)S(1)}, f32[2,64,256]{2,1,0:T(8,128)S(1)}, u32[]{:S(2)}, u32[]{:S(2)}) collective-permute-start(f32[2,64,256]{2,1,0:T(8,128)S(1)} %get-tuple-element.52), channel_id=1, source_target_pairs={{2,0},{3,1},{16,18},{17,19},{0,16},{1,17},{18,2},{19,3},{6,4},{7,5... | collective-permute-start | bytes 393224 | tf_op jit(solution)/shard_map/ppermute | solution.py:504
  14.7 1.4 %collective-permute-start.5 = (f32[2,64,256]{2,1,0:T(8,128)S(1)}, f32[2,64,256]{2,1,0:T(8,128)S(1)}, u32[]{:S(2)}, u32[]{:S(2)}) collective-permute-start(f32[2,64,256]{2,1,0:T(8,128)S(1)} %get-tuple-element.48), channel_id=1, source_target_pairs={{2,0},{3,1},{16,18},{17,19},{0,16},{1,17},{18,2},{19,3},{6,4},{7,5... | collective-permute-start | bytes 393224 | tf_op jit(solution)/shard_map/ppermute | solution.py:504
  16.0 1.9 %collective-permute-done.8.refs_2_ = f32[2,64,256]{2,1,0:T(8,128)S(1)} collective-permute-done((f32[2,64,256]{2,1,0:T(8,128)S(1)}, f32[2,64,256]{2,1,0:T(8,128)S(1)}, u32[]{:S(2)}, u32[]{:S(2)}) %collective-permute-start.8) | collective-permute-done | bytes 131104 | tf_op jit(solution)/shard_map/ppermute | solution.py:504
  17.9 2.8 %collective-permute-start.6 = (f32[2,64,256]{2,1,0:T(8,128)S(1)}, f32[2,64,256]{2,1,0:T(8,128)S(1)}, u32[]{:S(2)}, u32[]{:S(2)}) collective-permute-start(f32[2,64,256]{2,1,0:T(8,128)S(1)} %get-tuple-element.49), channel_id=1, source_target_pairs={{2,1},{3,0},{16,19},{17,18},{0,16},{1,17},{18,2},{19,3},{6,5},{7,4... | collective-permute-start | bytes 393224 | tf_op jit(solution)/shard_map/ppermute | solution.py:504
  21.4 1.6 %shard_map.107 = (f32[4,64,256]{2,1,0:T(8,128)S(1)}, f32[1,1,1,256,256]{4,3,2,1,0:T(8,128)S(1)}, f32[2,256,256]{2,1,0:T(8,128)S(1)}, f32[256,256]{1,0:T(8,128)S(1)}, bf16[6,256,256]{2,1,0:T(8,128)(2,1)S(1)}) custom-call(f32[4,64,256]{2,1,0:T(8,128)} %bitcast.14, f32[1,1,1,256,256]{4,3,2,1,0:T(8,128)} %refs_1_.1, f32[2,256,256]{2,1,0:T(8,128)} %refs_2_.1, ...), custom_call_target="tpu_custom_call" | custom-call | tf_op jit(solution)/shard_map/pallas_call | solution.py:237
  23.4 0.8 %shard_map.108.refs_4_.light_ref = f32[2,256,256]{2,1,0:T(8,128)S(1)} custom-call(s32[1,1,2,4]{3,2,1,0:T(2,128)S(1)} %bitcast.8, f32[2,256,256]{2,1,0:T(8,128)S(1)} %get-tuple-element.54.light_ref), custom_call_target="tpu_custom_call" | custom-call | tf_op jit(solution)/shard_map/pallas_call | solution.py:30
  24.4 6.1 %collective-permute-start.11 = (f32[2,64,256]{2,1,0:T(8,128)S(1)}, f32[2,64,256]{2,1,0:T(8,128)S(1)}, u32[]{:S(2)}, u32[]{:S(2)}) collective-permute-start(f32[2,64,256]{2,1,0:T(8,128)S(1)} %get-tuple-element.60), channel_id=1, source_target_pairs={{1,16},{0,17},{19,2},{18,3},{2,18},{3,19},{16,0},{17,1},{5,20},{4,... | collective-permute-start | bytes 393224 | tf_op jit(solution)/shard_map/ppermute | solution.py:504
  30.6 0.9 %collective-permute-start.15 = (f32[2,64,256]{2,1,0:T(8,128)S(1)}, f32[2,64,256]{2,1,0:T(8,128)S(1)}, u32[]{:S(2)}, u32[]{:S(2)}) collective-permute-start(f32[2,64,256]{2,1,0:T(8,128)S(1)} %get-tuple-element.65), channel_id=1, source_target_pairs={{0,2},{1,3},{18,16},{19,17},{2,18},{3,19},{16,0},{17,1},{4,6},{5,7... | collective-permute-start | bytes 393224 | tf_op jit(solution)/shard_map/ppermute | solution.py:504
  31.6 2.0 %collective-permute-done.11.refs_1_ = f32[2,64,256]{2,1,0:T(8,128)S(1)} collective-permute-done((f32[2,64,256]{2,1,0:T(8,128)S(1)}, f32[2,64,256]{2,1,0:T(8,128)S(1)}, u32[]{:S(2)}, u32[]{:S(2)}) %collective-permute-start.11) | collective-permute-done | bytes 131104 | tf_op jit(solution)/shard_map/ppermute | solution.py:504
  33.6 2.1 %collective-permute-done.12.refs_2_ = f32[2,64,256]{2,1,0:T(8,128)S(1)} collective-permute-done((f32[2,64,256]{2,1,0:T(8,128)S(1)}, f32[2,64,256]{2,1,0:T(8,128)S(1)}, u32[]{:S(2)}, u32[]{:S(2)}) %collective-permute-start.12) | collective-permute-done | bytes 131104 | tf_op jit(solution)/shard_map/ppermute | solution.py:504
  36.4 2.1 %collective-permute-done.15.refs_6_ = f32[2,64,256]{2,1,0:T(8,128)S(1)} collective-permute-done((f32[2,64,256]{2,1,0:T(8,128)S(1)}, f32[2,64,256]{2,1,0:T(8,128)S(1)}, u32[]{:S(2)}, u32[]{:S(2)}) %collective-permute-start.15) | collective-permute-done | bytes 131104 | tf_op jit(solution)/shard_map/ppermute | solution.py:504
  38.5 0.9 %shard_map.113 = (f32[2,4,64,256]{3,2,1,0:T(8,128)S(1)}, f32[2,4,64,128]{3,2,1,0:T(8,128)S(1)}) custom-call(s32[1,1,2,4]{3,2,1,0:T(2,128)S(1)} %bitcast.9, s32[1,1,2,4]{3,2,1,0:T(2,128)S(1)} %collective-permute-done.1.other_ref, f32[2,64,256]{2,1,0:T(8,128)S(1)} %get-tuple-element.59.refs_0_, f32[2,64,256]{2,1,0:T(8,128)S(1)} %collective-permute-done.11.refs_1_, ...), custom_call_target="tpu_custom_call" | custom-call | tf_op jit(solution)/shard_map/pallas_call | solution.py:30
  39.9 1.8 %collective-permute-done.18.their_halo_ref = f32[2,4,64,128]{3,2,1,0:T(8,128)S(1)} collective-permute-done((f32[2,4,64,128]{3,2,1,0:T(8,128)S(1)}, f32[2,4,64,128]{3,2,1,0:T(8,128)S(1)}, u32[]{:S(2)}, u32[]{:S(2)}) %collective-permute-start.18) | collective-permute-done | bytes 262176 | tf_op jit(solution)/shard_map/ppermute | solution.py:492
  42.0 5.8 %collective-permute-done.19.mine_ref = f32[2,4,64,128]{3,2,1,0:T(8,128)S(1)} collective-permute-done((f32[2,4,64,128]{3,2,1,0:T(8,128)S(1)}, f32[2,4,64,128]{3,2,1,0:T(8,128)S(1)}, u32[]{:S(2)}, u32[]{:S(2)}) %collective-permute-start.19) | collective-permute-done | bytes 262176 | tf_op jit(solution)/shard_map/ppermute | solution.py:499
  48.4 1.2 %collective-permute-done.20.theirs_ref = f32[2,4,64,128]{3,2,1,0:T(8,128)S(1)} collective-permute-done((f32[2,4,64,128]{3,2,1,0:T(8,128)S(1)}, f32[2,4,64,128]{3,2,1,0:T(8,128)S(1)}, u32[]{:S(2)}, u32[]{:S(2)}) %collective-permute-start.20) | collective-permute-done | bytes 262176 | tf_op jit(solution)/shard_map/ppermute | solution.py:492
  49.6 0.9 %shard_map.115 = (f32[4,64,256]{2,1,0:T(8,128)S(1)}, f32[4,64,256]{2,1,0:T(8,128)S(1)}, f32[2,64,256]{2,1,0:T(8,128)S(1)}, f32[2,64,256]{2,1,0:T(8,128)S(1)}, f3...) custom-call(s32[1,1,2,4]{3,2,1,0:T(2,128)S(1)} %bitcast.10, ...), custom_call_target="tpu_custom_call" | custom-call | tf_op jit(solution)/shard_map/pallas_call | solution.py:30
  51.2 0.8 %collective-permute-start.21 = (f32[2,64,256]{2,1,0:T(8,128)S(1)}, f32[2,64,256]{2,1,0:T(8,128)S(1)}, u32[]{:S(2)}, u32[]{:S(2)}) collective-permute-start(f32[2,64,256]{2,1,0:T(8,128)S(1)} %get-tuple-element.78), channel_id=1, source_target_pairs={{0,1},{1,0},{16,17},{17,16},{2,18},{3,19},{18,2},{19,3},{4,5},{5,4... | collective-permute-start | bytes 393224 | tf_op jit(solution)/shard_map/ppermute | solution.py:504
  52.0 1.3 %collective-permute-start.25 = (f32[2,64,256]{2,1,0:T(8,128)S(1)}, f32[2,64,256]{2,1,0:T(8,128)S(1)}, u32[]{:S(2)}, u32[]{:S(2)}) collective-permute-start(f32[2,64,256]{2,1,0:T(8,128)S(1)} %get-tuple-element.83), channel_id=1, source_target_pairs={{2,0},{3,1},{18,16},{19,17},{6,4},{7,5},{22,20},{23,21},{10,8},{11... | collective-permute-start | bytes 393224 | tf_op jit(solution)/shard_map/ppermute | solution.py:504
  53.3 1.3 %collective-permute-start.26 = (f32[2,64,256]{2,1,0:T(8,128)S(1)}, f32[2,64,256]{2,1,0:T(8,128)S(1)}, u32[]{:S(2)}, u32[]{:S(2)}) collective-permute-start(f32[2,64,256]{2,1,0:T(8,128)S(1)} %get-tuple-element.84), channel_id=1, source_target_pairs={{2,1},{3,0},{18,17},{19,16},{6,5},{7,4},{22,21},{23,20},{10,9},{11... | collective-permute-start | bytes 393224 | tf_op jit(solution)/shard_map/ppermute | solution.py:504
  54.6 1.3 %collective-permute-start.22 = (f32[2,64,256]{2,1,0:T(8,128)S(1)}, f32[2,64,256]{2,1,0:T(8,128)S(1)}, u32[]{:S(2)}, u32[]{:S(2)}) collective-permute-start(f32[2,64,256]{2,1,0:T(8,128)S(1)} %get-tuple-element.79), channel_id=1, source_target_pairs={{2,0},{3,1},{18,16},{19,17},{6,4},{7,5},{22,20},{23,21},{10,8},{11... | collective-permute-start | bytes 393224 | tf_op jit(solution)/shard_map/ppermute | solution.py:504
  55.9 1.3 %collective-permute-start.23 = (f32[2,64,256]{2,1,0:T(8,128)S(1)}, f32[2,64,256]{2,1,0:T(8,128)S(1)}, u32[]{:S(2)}, u32[]{:S(2)}) collective-permute-start(f32[2,64,256]{2,1,0:T(8,128)S(1)} %get-tuple-element.80), channel_id=1, source_target_pairs={{2,1},{3,0},{18,17},{19,16},{6,5},{7,4},{22,21},{23,20},{10,9},{11... | collective-permute-start | bytes 393224 | tf_op jit(solution)/shard_map/ppermute | solution.py:504
  58.0 0.8 %shard_map.116 = (f32[4,64,256]{2,1,0:T(8,128)}, f32[4,64,256]{2,1,0:T(8,128)}) custom-call(f32[4,64,256]{2,1,0:T(8,128)S(1)} %get-tuple-element.73.refs_0_, f32[4,64,256]{2,1,0:T(8,128)S(1)} %get-tuple-element.74.refs_1_), custom_call_target="tpu_custom_call" | custom-call | tf_op jit(solution)/shard_map/pallas_call | solution.py:237
  58.8 1.5 %collective-permute-done.26.refs_3_ = f32[2,64,256]{2,1,0:T(8,128)S(1)} collective-permute-done((f32[2,64,256]{2,1,0:T(8,128)S(1)}, f32[2,64,256]{2,1,0:T(8,128)S(1)}, u32[]{:S(2)}, u32[]{:S(2)}) %collective-permute-start.26) | collective-permute-done | bytes 131104 | tf_op jit(solution)/shard_map/ppermute | solution.py:504
  60.3 1.8 %shard_map.118.refs_4_ = f32[2,256,256]{2,1,0:T(8,128)S(1)} custom-call(s32[1,1]{1,0:T(1,128)S(6)} %copy.11.count_ref, f32[2,64,256]{2,1,0:T(8,128)S(1)} %get-tuple-element.81.refs_0_, f32[2,64,256]{2,1,0:T(8,128)S(1)} %collective-permute-done.24.refs_1_, f32[2,64,256]{2,1,0:T(8,128)S(1)} %collective-permute-done.25.refs_2_, ...), custom_call_target="tpu_custom_call" | custom-call | tf_op jit(solution)/shard_map/pallas_call | solution.py:30
  62.1 5.2 %collective-permute-done.22.refs_2_ = f32[2,64,256]{2,1,0:T(8,128)S(1)} collective-permute-done((f32[2,64,256]{2,1,0:T(8,128)S(1)}, f32[2,64,256]{2,1,0:T(8,128)S(1)}, u32[]{:S(2)}, u32[]{:S(2)}) %collective-permute-start.22) | collective-permute-done | bytes 131104 | tf_op jit(solution)/shard_map/ppermute | solution.py:504
  67.3 1.7 %shard_map.119 = f32[1,1,1,256,256]{4,3,2,1,0:T(8,128)} custom-call(s32[1,1]{1,0:T(1,128)S(6)} %copy.11.count_ref, f32[2,64,256]{2,1,0:T(8,128)S(1)} %get-tuple-element.77.refs_0_, f32[2,64,256]{2,1,0:T(8,128)S(1)} %collective-permute-done.21.refs_1_, f32[2,64,256]{2,1,0:T(8,128)S(1)} %collective-permute-done.22.refs_2_, ...), custom_call_target="tpu_custom_call" | custom-call | tf_op jit(solution)/shard_map/pallas_call | solution.py:30
  (43 shorter events, 7.1 us)
Async XLA Ops:
  0.6 1.8 %collective-permute-start = (f32[4,64,256]{2,1,0:T(8,128)}, f32[4,64,256]{2,1,0:T(8,128)S(1)}, u32[]{:S(2)}, u32[]{:S(2)}) collective-permute-start(f32[4,64,256]{2,1,0:T(8,128)} %bitcast.12), channel_id=1, source_target_pairs={{0,16},{16,0},{1,17},{17,1},{2,18},{18,2},{3,19},{19,3},{4,20},{20... | collective-permute-start | bytes 786440 | tf_op jit(solution)/shard_map/ppermute | solution.py:492
  2.7 5.6 %copy-start = (s32[1,1,4,2]{2,3,1,0:T(2,128)S(1)}, s32[1,1,4,2]{2,3,1,0:T(2,128)}, u32[]{:S(2)}) copy-start(s32[1,1,4,2]{2,3,1,0:T(2,128)} %param.13) | copy-start | bytes 100
  2.8 4.8 %collective-permute-start.2 = (f32[4,64,128]{2,1,0:T(8,128)S(1)}, f32[4,64,128]{2,1,0:T(8,128)S(1)}, u32[]{:S(2)}, u32[]{:S(2)}) collective-permute-start(f32[4,64,128]{2,1,0:T(8,128)S(1)} %shard_map.104), channel_id=1, source_target_pairs={{0,4},{4,8},{8,12},{12,28},{20,16},{24,20},{28,24},{16,0},{1,5},{5... | collective-permute-start | bytes 393224 | tf_op jit(solution)/shard_map/ppermute | solution.py:499
  7.5 2.0 %collective-permute-start.3 = (f32[4,64,128]{2,1,0:T(8,128)S(1)}, f32[4,64,128]{2,1,0:T(8,128)S(1)}, u32[]{:S(2)}, u32[]{:S(2)}) collective-permute-start(f32[4,64,128]{2,1,0:T(8,128)S(1)} %collective-permute-done.2.mine_ref), channel_id=1, source_target_pairs={{0,16},{16,0},{1,17},{17,1},{2,18},{18,2},{3,19},{19,3},{4,20},{20... | collective-permute-start | bytes 393224 | tf_op jit(solution)/shard_map/ppermute | solution.py:492
  8.4 3.3 %copy-start.1 = (f32[1,1,1,256,256]{4,3,2,1,0:T(8,128)S(1)}, f32[1,1,1,256,256]{4,3,2,1,0:T(8,128)}, u32[]{:S(2)}) copy-start(f32[1,1,1,256,256]{4,3,2,1,0:T(8,128)} %refs_1_.1) | copy-start | bytes 786436
  8.4 1.2 %collective-permute-start.1 = (s32[1,1,2,4]{3,2,1,0:T(2,128)S(1)}, s32[1,1,2,4]{3,2,1,0:T(2,128)S(1)}, u32[]{:S(2)}, u32[]{:S(2)}) collective-permute-start(s32[1,1,2,4]{3,2,1,0:T(2,128)S(1)} %bitcast.5), channel_id=1, source_target_pairs={{0,16},{16,0},{1,17},{17,1},{2,18},{18,2},{3,19},{19,3},{4,20},{20... | collective-permute-start | bytes 104 | tf_op jit(solution)/shard_map/ppermute | solution.py:492
  10.3 4.3 %collective-permute-start.7 = (f32[2,64,256]{2,1,0:T(8,128)S(1)}, f32[2,64,256]{2,1,0:T(8,128)S(1)}, u32[]{:S(2)}, u32[]{:S(2)}) collective-permute-start(f32[2,64,256]{2,1,0:T(8,128)S(1)} %get-tuple-element.51), channel_id=1, source_target_pairs={{16,1},{17,0},{2,19},{3,18},{0,16},{1,17},{18,2},{19,3},{20,5},{21... | collective-permute-start | bytes 393224 | tf_op jit(solution)/shard_map/ppermute | solution.py:504
  11.7 12.5 %collective-permute-start.10 = (f32[1,1,1,256,256]{4,3,2,1,0:T(8,128)S(1)}, f32[1,1,1,256,256]{4,3,2,1,0:T(8,128)S(1)}, u32[]{:S(2)}, u32[]{:S(2)}) collective-permute-start(f32[1,1,1,256,256]{4,3,2,1,0:T(8,128)S(1)} %copy-done.1), channel_id=1, source_target_pairs={{16,18},{17,19},{2,0},{3,1},{0,16},{1,17},{18,2},{19,3},{20,22},{2... | collective-permute-start | bytes 786440 | tf_op jit(solution)/shard_map/ppermute | solution.py:510
  11.8 6.1 %collective-permute-start.8 = (f32[2,64,256]{2,1,0:T(8,128)S(1)}, f32[2,64,256]{2,1,0:T(8,128)S(1)}, u32[]{:S(2)}, u32[]{:S(2)}) collective-permute-start(f32[2,64,256]{2,1,0:T(8,128)S(1)} %get-tuple-element.52), channel_id=1, source_target_pairs={{2,0},{3,1},{16,18},{17,19},{0,16},{1,17},{18,2},{19,3},{6,4},{7,5... | collective-permute-start | bytes 393224 | tf_op jit(solution)/shard_map/ppermute | solution.py:504
  13.2 10.9 %collective-permute-start.9 = (f32[2,64,256]{2,1,0:T(8,128)S(1)}, f32[2,64,256]{2,1,0:T(8,128)S(1)}, u32[]{:S(2)}, u32[]{:S(2)}) collective-permute-start(f32[2,64,256]{2,1,0:T(8,128)S(1)} %get-tuple-element.53), channel_id=1, source_target_pairs={{2,1},{3,0},{16,19},{17,18},{0,16},{1,17},{18,2},{19,3},{6,5},{7,4... | collective-permute-start | bytes 393224 | tf_op jit(solution)/shard_map/ppermute | solution.py:504
  14.3 9.9 %collective-permute-start.4 = (f32[2,64,256]{2,1,0:T(8,128)S(1)}, f32[2,64,256]{2,1,0:T(8,128)S(1)}, u32[]{:S(2)}, u32[]{:S(2)}) collective-permute-start(f32[2,64,256]{2,1,0:T(8,128)S(1)} %get-tuple-element.47), channel_id=1, source_target_pairs={{16,1},{17,0},{2,19},{3,18},{0,16},{1,17},{18,2},{19,3},{20,5},{21... | collective-permute-start | bytes 393224 | tf_op jit(solution)/shard_map/ppermute | solution.py:504
  14.7 9.6 %collective-permute-start.5 = (f32[2,64,256]{2,1,0:T(8,128)S(1)}, f32[2,64,256]{2,1,0:T(8,128)S(1)}, u32[]{:S(2)}, u32[]{:S(2)}) collective-permute-start(f32[2,64,256]{2,1,0:T(8,128)S(1)} %get-tuple-element.48), channel_id=1, source_target_pairs={{2,0},{3,1},{16,18},{17,19},{0,16},{1,17},{18,2},{19,3},{6,4},{7,5... | collective-permute-start | bytes 393224 | tf_op jit(solution)/shard_map/ppermute | solution.py:504
  17.9 6.3 %collective-permute-start.6 = (f32[2,64,256]{2,1,0:T(8,128)S(1)}, f32[2,64,256]{2,1,0:T(8,128)S(1)}, u32[]{:S(2)}, u32[]{:S(2)}) collective-permute-start(f32[2,64,256]{2,1,0:T(8,128)S(1)} %get-tuple-element.49), channel_id=1, source_target_pairs={{2,1},{3,0},{16,19},{17,18},{0,16},{1,17},{18,2},{19,3},{6,5},{7,4... | collective-permute-start | bytes 393224 | tf_op jit(solution)/shard_map/ppermute | solution.py:504
  24.4 9.2 %collective-permute-start.11 = (f32[2,64,256]{2,1,0:T(8,128)S(1)}, f32[2,64,256]{2,1,0:T(8,128)S(1)}, u32[]{:S(2)}, u32[]{:S(2)}) collective-permute-start(f32[2,64,256]{2,1,0:T(8,128)S(1)} %get-tuple-element.60), channel_id=1, source_target_pairs={{1,16},{0,17},{19,2},{18,3},{2,18},{3,19},{16,0},{17,1},{5,20},{4,... | collective-permute-start | bytes 393224 | tf_op jit(solution)/shard_map/ppermute | solution.py:504
  30.5 5.2 %collective-permute-start.12 = (f32[2,64,256]{2,1,0:T(8,128)S(1)}, f32[2,64,256]{2,1,0:T(8,128)S(1)}, u32[]{:S(2)}, u32[]{:S(2)}) collective-permute-start(f32[2,64,256]{2,1,0:T(8,128)S(1)} %get-tuple-element.61), channel_id=1, source_target_pairs={{0,2},{1,3},{18,16},{19,17},{2,18},{3,19},{16,0},{17,1},{4,6},{5,7... | collective-permute-start | bytes 393224 | tf_op jit(solution)/shard_map/ppermute | solution.py:504
  30.5 5.2 %collective-permute-start.13 = (f32[2,64,256]{2,1,0:T(8,128)S(1)}, f32[2,64,256]{2,1,0:T(8,128)S(1)}, u32[]{:S(2)}, u32[]{:S(2)}) collective-permute-start(f32[2,64,256]{2,1,0:T(8,128)S(1)} %get-tuple-element.62), channel_id=1, source_target_pairs={{1,2},{0,3},{19,16},{18,17},{2,18},{3,19},{16,0},{17,1},{5,6},{4,7... | collective-permute-start | bytes 393224 | tf_op jit(solution)/shard_map/ppermute | solution.py:504
  30.6 5.9 %collective-permute-start.14 = (f32[2,64,256]{2,1,0:T(8,128)S(1)}, f32[2,64,256]{2,1,0:T(8,128)S(1)}, u32[]{:S(2)}, u32[]{:S(2)}) collective-permute-start(f32[2,64,256]{2,1,0:T(8,128)S(1)} %get-tuple-element.64), channel_id=1, source_target_pairs={{1,16},{0,17},{19,2},{18,3},{2,18},{3,19},{16,0},{17,1},{5,20},{4,... | collective-permute-start | bytes 393224 | tf_op jit(solution)/shard_map/ppermute | solution.py:504
  30.6 7.9 %collective-permute-start.15 = (f32[2,64,256]{2,1,0:T(8,128)S(1)}, f32[2,64,256]{2,1,0:T(8,128)S(1)}, u32[]{:S(2)}, u32[]{:S(2)}) collective-permute-start(f32[2,64,256]{2,1,0:T(8,128)S(1)} %get-tuple-element.65), channel_id=1, source_target_pairs={{0,2},{1,3},{18,16},{19,17},{2,18},{3,19},{16,0},{17,1},{4,6},{5,7... | collective-permute-start | bytes 393224 | tf_op jit(solution)/shard_map/ppermute | solution.py:504
  33.6 4.9 %collective-permute-start.16 = (f32[2,64,256]{2,1,0:T(8,128)S(1)}, f32[2,64,256]{2,1,0:T(8,128)S(1)}, u32[]{:S(2)}, u32[]{:S(2)}) collective-permute-start(f32[2,64,256]{2,1,0:T(8,128)S(1)} %get-tuple-element.66), channel_id=1, source_target_pairs={{1,2},{0,3},{19,16},{18,17},{2,18},{3,19},{16,0},{17,1},{5,6},{4,7... | collective-permute-start | bytes 393224 | tf_op jit(solution)/shard_map/ppermute | solution.py:504
  39.4 2.4 %collective-permute-start.17 = (f32[2,4,64,256]{3,2,1,0:T(8,128)S(1)}, f32[2,4,64,256]{3,2,1,0:T(8,128)S(1)}, u32[]{:S(2)}, u32[]{:S(2)}) collective-permute-start(f32[2,4,64,256]{3,2,1,0:T(8,128)S(1)} %get-tuple-element.68.own_ref), channel_id=1, source_target_pairs={{0,16},{16,0},{1,17},{17,1},{2,18},{18,2},{3,19},{19,3},{4,20},{20... | collective-permute-start | bytes 1572872 | tf_op jit(solution)/shard_map/ppermute | solution.py:492
  39.4 2.3 %collective-permute-start.18 = (f32[2,4,64,128]{3,2,1,0:T(8,128)S(1)}, f32[2,4,64,128]{3,2,1,0:T(8,128)S(1)}, u32[]{:S(2)}, u32[]{:S(2)}) collective-permute-start(f32[2,4,64,128]{3,2,1,0:T(8,128)S(1)} %get-tuple-element.69.halo_ref), channel_id=1, source_target_pairs={{0,16},{16,0},{1,17},{17,1},{2,18},{18,2},{3,19},{19,3},{4,20},{20... | collective-permute-start | bytes 786440 | tf_op jit(solution)/shard_map/ppermute | solution.py:492
  41.8 6.0 %collective-permute-start.19 = (f32[2,4,64,128]{3,2,1,0:T(8,128)S(1)}, f32[2,4,64,128]{3,2,1,0:T(8,128)S(1)}, u32[]{:S(2)}, u32[]{:S(2)}) collective-permute-start(f32[2,4,64,128]{3,2,1,0:T(8,128)S(1)} %get-tuple-element.72), channel_id=1, source_target_pairs={{0,4},{4,8},{8,12},{12,28},{20,16},{24,20},{28,24},{16,0},{1,5},{5... | collective-permute-start | bytes 786440 | tf_op jit(solution)/shard_map/ppermute | solution.py:499
  47.8 1.7 %collective-permute-start.20 = (f32[2,4,64,128]{3,2,1,0:T(8,128)S(1)}, f32[2,4,64,128]{3,2,1,0:T(8,128)S(1)}, u32[]{:S(2)}, u32[]{:S(2)}) collective-permute-start(f32[2,4,64,128]{3,2,1,0:T(8,128)S(1)} %collective-permute-done.19.mine_ref), channel_id=1, source_target_pairs={{0,16},{16,0},{1,17},{17,1},{2,18},{18,2},{3,19},{19,3},{4,20},{20... | collective-permute-start | bytes 786440 | tf_op jit(solution)/shard_map/ppermute | solution.py:492
  50.5 5.4 %collective-permute-start.24 = (f32[2,64,256]{2,1,0:T(8,128)S(1)}, f32[2,64,256]{2,1,0:T(8,128)S(1)}, u32[]{:S(2)}, u32[]{:S(2)}) collective-permute-start(f32[2,64,256]{2,1,0:T(8,128)S(1)} %get-tuple-element.82), channel_id=1, source_target_pairs={{0,1},{1,0},{16,17},{17,16},{2,18},{3,19},{18,2},{19,3},{4,5},{5,4... | collective-permute-start | bytes 393224 | tf_op jit(solution)/shard_map/ppermute | solution.py:504
  51.2 10.9 %collective-permute-start.21 = (f32[2,64,256]{2,1,0:T(8,128)S(1)}, f32[2,64,256]{2,1,0:T(8,128)S(1)}, u32[]{:S(2)}, u32[]{:S(2)}) collective-permute-start(f32[2,64,256]{2,1,0:T(8,128)S(1)} %get-tuple-element.78), channel_id=1, source_target_pairs={{0,1},{1,0},{16,17},{17,16},{2,18},{3,19},{18,2},{19,3},{4,5},{5,4... | collective-permute-start | bytes 393224 | tf_op jit(solution)/shard_map/ppermute | solution.py:504
  52.0 6.8 %collective-permute-start.25 = (f32[2,64,256]{2,1,0:T(8,128)S(1)}, f32[2,64,256]{2,1,0:T(8,128)S(1)}, u32[]{:S(2)}, u32[]{:S(2)}) collective-permute-start(f32[2,64,256]{2,1,0:T(8,128)S(1)} %get-tuple-element.83), channel_id=1, source_target_pairs={{2,0},{3,1},{18,16},{19,17},{6,4},{7,5},{22,20},{23,21},{10,8},{11... | collective-permute-start | bytes 393224 | tf_op jit(solution)/shard_map/ppermute | solution.py:504
  53.3 7.0 %collective-permute-start.26 = (f32[2,64,256]{2,1,0:T(8,128)S(1)}, f32[2,64,256]{2,1,0:T(8,128)S(1)}, u32[]{:S(2)}, u32[]{:S(2)}) collective-permute-start(f32[2,64,256]{2,1,0:T(8,128)S(1)} %get-tuple-element.84), channel_id=1, source_target_pairs={{2,1},{3,0},{18,17},{19,16},{6,5},{7,4},{22,21},{23,20},{10,9},{11... | collective-permute-start | bytes 393224 | tf_op jit(solution)/shard_map/ppermute | solution.py:504
  54.6 12.7 %collective-permute-start.22 = (f32[2,64,256]{2,1,0:T(8,128)S(1)}, f32[2,64,256]{2,1,0:T(8,128)S(1)}, u32[]{:S(2)}, u32[]{:S(2)}) collective-permute-start(f32[2,64,256]{2,1,0:T(8,128)S(1)} %get-tuple-element.79), channel_id=1, source_target_pairs={{2,0},{3,1},{18,16},{19,17},{6,4},{7,5},{22,20},{23,21},{10,8},{11... | collective-permute-start | bytes 393224 | tf_op jit(solution)/shard_map/ppermute | solution.py:504
  55.9 11.4 %collective-permute-start.23 = (f32[2,64,256]{2,1,0:T(8,128)S(1)}, f32[2,64,256]{2,1,0:T(8,128)S(1)}, u32[]{:S(2)}, u32[]{:S(2)}) collective-permute-start(f32[2,64,256]{2,1,0:T(8,128)S(1)} %get-tuple-element.80), channel_id=1, source_target_pairs={{2,1},{3,0},{18,17},{19,16},{6,5},{7,4},{22,21},{23,20},{10,9},{11... | collective-permute-start | bytes 393224 | tf_op jit(solution)/shard_map/ppermute | solution.py:504
